TPU v7x, 32 devices: a whole 2x2x4 slice. The times are simulated.
32 devices in a mesh: batch: 4 (over z), ulysses: 2 (over x), blk: 4 (over y, core).
Axes of the slice: x: 2, y: 2, z: 4, core: 2. Of those that a mesh axis runs over, the one named last changes fastest.
Arguments:
- residual_in: bfloat16 [512, 8, 1024], P(('ulysses', 'blk'), 'batch'), may hold values from -6 to 6
- qkv_weight: bfloat16 [1024, 3072], P(('batch', 'ulysses', 'blk')), may hold values from -3 to 3
- qkv_bias: bfloat16 [3072], P(('batch', 'ulysses', 'blk')), may hold values from -0.4375 to 0.4375
- dense_weight: bfloat16 [1024, 1024], P(('batch', 'ulysses', 'blk')), may hold values from -0.5 to 0.5
- dense_bias: bfloat16 [1024], P(('batch', 'ulysses', 'blk')), may hold values from -4 to 4
- norm1_gain: bfloat16 [1024], P(('batch', 'ulysses', 'blk')), may hold values from 0.5 to 1.5
- norm1_bias: bfloat16 [1024], P(('batch', 'ulysses', 'blk')), may hold values from -3 to 3
- norm2_gain: bfloat16 [1024], P(('batch', 'ulysses', 'blk')), may hold values from 0.5 to 1.5
- norm2_bias: bfloat16 [1024], P(('batch', 'ulysses', 'blk')), may hold values from -3 to 3
- up_weight: bfloat16 [1024, 4096], P(('batch', 'ulysses', 'blk')), may hold values from -0.1875 to 0.1875
- up_bias: bfloat16 [4096], P(('batch', 'ulysses', 'blk')), may hold values from -6 to 6
- down_weight: bfloat16 [4096, 1024], P(('batch', 'ulysses', 'blk')), may hold values from -0.09375 to 0.09375
- down_bias: bfloat16 [1024], P(('batch', 'ulysses', 'blk')), may hold values from -4 to 4
- cotangent: bfloat16 [512, 8, 1024], P(('ulysses', 'blk'), 'batch'), may hold values from -6 to 6
Outputs:
- output: bfloat16 [512, 8, 1024], P(('ulysses', 'blk'), 'batch')
- input_grad: float32 [512, 8, 1024], P(('ulysses', 'blk'), 'batch')
- qkv_weight_grad: float32 [1024, 3072], P(('batch', 'ulysses', 'blk'))
- qkv_bias_grad: float32 [3072], P(('batch', 'ulysses', 'blk'))
- dense_weight_grad: float32 [1024, 1024], P(('batch', 'ulysses', 'blk'))
- dense_bias_grad: float32 [1024], P(('batch', 'ulysses', 'blk'))
- norm1_gain_grad: float32 [1024], P(('batch', 'ulysses', 'blk'))
- norm1_bias_grad: float32 [1024], P(('batch', 'ulysses', 'blk'))
- norm2_gain_grad: float32 [1024], P(('batch', 'ulysses', 'blk'))
- norm2_bias_grad: float32 [1024], P(('batch', 'ulysses', 'blk'))
- up_weight_grad: float32 [1024, 4096], P(('batch', 'ulysses', 'blk'))
- up_bias_grad: float32 [4096], P(('batch', 'ulysses', 'blk'))
- down_weight_grad: float32 [4096, 1024], P(('batch', 'ulysses', 'blk'))
- down_bias_grad: float32 [1024], P(('batch', 'ulysses', 'blk'))
All inputs are finite; a program needn't handle non-finite values.
Results may differ from a plain program's by a relative error of at most 0.0091.
Values may be sent and summed in bfloat16 or wider, within the bound.
A program may use at most 192 MiB of HBM per device.

v0:
```python
import functools
import math

import jax
import jax.numpy as jnp
from jax import lax
from jax.experimental import pallas as pl
from jax.experimental.pallas import tpu as pltpu
from jax.sharding import PartitionSpec as P

HD = 64
BATCH, ULY, BLK = "batch", "ulysses", "blk"
AXES = (BATCH, ULY, BLK)
TOKENS = (ULY, BLK)


EPSILON = 1e-05
INV_ROOT_TWO = 0.7071067811865476
INV_ROOT_TWO_PI = 0.3989422804014327


def layer_norm(values):
    center = jnp.mean(values, axis=-1, keepdims=True)
    shifted = values - center
    inverse = lax.rsqrt(jnp.mean(shifted * shifted, axis=-1, keepdims=True) + EPSILON)
    return (shifted * inverse, inverse)


def norm_back(gradient, normed, inverse, gain_vec):
    scaled = gradient * gain_vec
    return inverse * (
        scaled
        - jnp.mean(scaled, axis=-1, keepdims=True)
        - normed * jnp.mean(scaled * normed, axis=-1, keepdims=True)
    )


def gelu_value(pre_values):
    return 0.5 * pre_values * (1.0 + jax.scipy.special.erf(pre_values * INV_ROOT_TWO))


def gelu_slope(pre_values):
    normal_cdf = 0.5 * (1.0 + jax.scipy.special.erf(pre_values * INV_ROOT_TWO))
    return normal_cdf + pre_values * jnp.exp(-0.5 * pre_values * pre_values) * INV_ROOT_TWO_PI


def rotary_tables(positions, rotary):
    half_rot = rotary // 2
    frequency = 1.0 / 10000.0 ** (jnp.arange(half_rot, dtype=jnp.float32) * (2.0 / rotary))
    angles = positions.astype(jnp.float32)[:, None] * frequency[None, :]
    cosine = jnp.concatenate([jnp.cos(angles), jnp.cos(angles)], axis=-1)
    sine_table = jnp.concatenate([jnp.sin(angles), jnp.sin(angles)], axis=-1)
    return (cosine, sine_table)


def expand_table(table, tensor):
    extra_dims = (1,) * (tensor.ndim - 2)
    return table.reshape((table.shape[0],) + extra_dims + (table.shape[1],))


def rotate_fwd(tensor, cosine, sine_table, rotary):
    half_rot = rotary // 2
    cos_full = expand_table(cosine, tensor)
    sin_full = expand_table(sine_table, tensor)
    rot_part = tensor[..., :rotary]
    turned = jnp.concatenate([-rot_part[..., half_rot:], rot_part[..., :half_rot]], axis=-1)
    return jnp.concatenate([rot_part * cos_full + turned * sin_full, tensor[..., rotary:]], axis=-1)


def rotate_back(tensor, cosine, sine_table, rotary):
    half_rot = rotary // 2
    cos_full = expand_table(cosine, tensor)
    sin_full = expand_table(sine_table, tensor)
    rot_part = tensor[..., :rotary]
    weighted = rot_part * sin_full
    turned = jnp.concatenate([weighted[..., half_rot:], -weighted[..., :half_rot]], axis=-1)
    return jnp.concatenate([rot_part * cos_full + turned, tensor[..., rotary:]], axis=-1)


def general_body(
    residual_in,
    qkv_weight,
    qkv_bias,
    dense_weight,
    dense_bias,
    norm1_gain,
    norm1_bias,
    norm2_gain,
    norm2_bias,
    up_weight,
    up_bias,
    down_weight,
    down_bias,
    cotangent,
):
    single = jnp.float32
    half_type = jnp.bfloat16
    gathered = (
        lax.all_gather(qkv_weight, AXES, axis=0, tiled=True),
        lax.all_gather(qkv_bias, AXES, axis=0, tiled=True),
        lax.all_gather(dense_weight, AXES, axis=0, tiled=True),
        lax.all_gather(dense_bias, AXES, axis=0, tiled=True),
        lax.all_gather(norm1_gain, AXES, axis=0, tiled=True),
        lax.all_gather(norm1_bias, AXES, axis=0, tiled=True),
        lax.all_gather(norm2_gain, AXES, axis=0, tiled=True),
        lax.all_gather(norm2_bias, AXES, axis=0, tiled=True),
        lax.all_gather(up_weight, AXES, axis=0, tiled=True),
        lax.all_gather(up_bias, AXES, axis=0, tiled=True),
        lax.all_gather(down_weight, AXES, axis=0, tiled=True),
        lax.all_gather(down_bias, AXES, axis=0, tiled=True),
    )
    (
        w_qkv,
        b_qkv,
        w_dense,
        b_dense,
        gain_one,
        shift_one,
        gain_two,
        shift_two,
        w_up,
        b_up,
        w_down,
        b_down,
    ) = gathered
    tok_rows = residual_in.shape[0]
    seq_count = residual_in.shape[1]
    model_width = residual_in.shape[2]
    head_count = model_width // HD
    rotary = HD // 4
    scale_factor = 1.0 / math.sqrt(HD)
    blk_size = lax.axis_size(BLK)
    uly_size = lax.axis_size(ULY)
    blk_index = lax.axis_index(BLK)
    block_id = lax.axis_index(ULY) * blk_size + blk_index
    seq_pos = block_id * tok_rows + jnp.arange(tok_rows, dtype=jnp.int32)
    inputs_f = residual_in.astype(single)
    normed, inverse = layer_norm(inputs_f)
    act_one = (normed * gain_one.astype(single) + shift_one.astype(single)).astype(half_type)
    act_two = (normed * gain_two.astype(single) + shift_two.astype(single)).astype(half_type)
    qkv_full = jnp.einsum(
        "tsd,df->tsf", act_one, w_qkv, preferred_element_type=single
    ) + b_qkv.astype(single)
    cos_seq, sin_seq = rotary_tables(seq_pos, rotary)
    head_shape = (tok_rows, seq_count, head_count, HD)
    query_seq = (
        rotate_fwd(qkv_full[..., :model_width].reshape(head_shape), cos_seq, sin_seq, rotary)
        .reshape(tok_rows, seq_count, model_width)
        .astype(half_type)
    )
    key_seq = (
        rotate_fwd(
            qkv_full[..., model_width : 2 * model_width].reshape(head_shape),
            cos_seq,
            sin_seq,
            rotary,
        )
        .reshape(tok_rows, seq_count, model_width)
        .astype(half_type)
    )
    value_seq = qkv_full[..., 2 * model_width :].astype(half_type)
    query_loc, key_loc, value_loc = (
        lax.all_to_all(query_seq, ULY, split_axis=2, concat_axis=0, tiled=True),
        lax.all_to_all(key_seq, ULY, split_axis=2, concat_axis=0, tiled=True),
        lax.all_to_all(value_seq, ULY, split_axis=2, concat_axis=0, tiled=True),
    )
    local_rows = query_loc.shape[0]
    features = query_loc.shape[2]
    local_heads = features // HD
    key_all, value_all = (
        lax.all_gather(key_loc, BLK, axis=0, tiled=True),
        lax.all_gather(value_loc, BLK, axis=0, tiled=True),
    )
    total_rows = key_all.shape[0]
    row_ids = jnp.arange(local_rows, dtype=jnp.int32)
    query_pos = (row_ids // tok_rows * blk_size + blk_index) * tok_rows + row_ids % tok_rows
    block_rows = math.gcd(512, local_rows)
    n_blocks = local_rows // block_rows
    query_h = query_loc.reshape(local_rows, seq_count, local_heads, HD)
    key_h = jnp.transpose(
        key_all.reshape(blk_size, uly_size, tok_rows, seq_count, features), (1, 0, 2, 3, 4)
    ).reshape(total_rows, seq_count, local_heads, HD)
    value_h = jnp.transpose(
        value_all.reshape(blk_size, uly_size, tok_rows, seq_count, features), (1, 0, 2, 3, 4)
    ).reshape(total_rows, seq_count, local_heads, HD)
    zero_idx = jnp.zeros((), jnp.int32)
    step_ids = jnp.arange(n_blocks * seq_count, dtype=jnp.int32)
    row_shape = (block_rows, 1, local_heads, HD)

    def select(step_index):
        row_start = step_index // seq_count * block_rows
        seq_index = step_index % seq_count
        query_rows = lax.dynamic_slice(
            query_h, (row_start, seq_index, zero_idx, zero_idx), row_shape
        )
        limit = jnp.max(query_pos) // block_rows + 1
        return (row_start, seq_index, query_rows, query_pos, limit)

    def block_scores(query_rows, row_pos, key_index, seq_index):
        key_start = key_index * block_rows
        slot = (key_start, seq_index, zero_idx, zero_idx)
        key_rows = lax.dynamic_slice(key_h, slot, (block_rows, 1, local_heads, HD))
        value_rows = lax.dynamic_slice(value_h, slot, (block_rows, 1, local_heads, HD))
        scores = (
            jnp.einsum("qshd,kshd->shqk", query_rows, key_rows, preferred_element_type=single)
            * scale_factor
        )
        key_ids = key_start + jnp.arange(block_rows, dtype=jnp.int32)
        allowed = (key_ids[None, :] <= row_pos[:, None])[None, None]
        return (jnp.where(allowed, scores, -jnp.inf), key_rows, value_rows, slot)

    def forward_block(step_index):
        row_start, seq_index, query_rows, row_pos, limit = select(step_index)

        def total_step(key_index, carry):
            running_max, running_sum = carry
            masked, key_rows, value_rows, slot = block_scores(
                query_rows, row_pos, key_index, seq_index
            )
            new_max = jnp.maximum(running_max, jnp.max(masked, axis=-1))
            new_sum = running_sum * jnp.exp(running_max - new_max) + jnp.sum(
                jnp.exp(masked - new_max[..., None]), axis=-1
            )
            return (new_max, new_sum)

        start_max = jnp.full((1, local_heads, block_rows), -jnp.inf, single)
        start_sum = jnp.zeros((1, local_heads, block_rows), single)
        final_max, final_sum = lax.fori_loop(zero_idx, limit, total_step, (start_max, start_sum))
        log_total = final_max + jnp.log(final_sum)

        def value_step(key_index, acc):
            masked, key_rows, value_rows, slot = block_scores(
                query_rows, row_pos, key_index, seq_index
            )
            weights_b = jnp.exp(masked - log_total[..., None]).astype(half_type)
            return acc + jnp.einsum(
                "shqk,kshd->qshd", weights_b, value_rows, preferred_element_type=single
            )

        result = lax.fori_loop(zero_idx, limit, value_step, jnp.zeros(row_shape, single)).astype(
            half_type
        )
        return (result[:, 0], log_total)

    results, log_totals = lax.map(forward_block, step_ids)
    attn_h = jnp.transpose(
        results.reshape(n_blocks, seq_count, block_rows, local_heads, HD), (0, 2, 1, 3, 4)
    ).reshape(local_rows, seq_count, local_heads, HD)
    attn_seq = lax.all_to_all(
        attn_h.reshape(local_rows, seq_count, features),
        ULY,
        split_axis=0,
        concat_axis=2,
        tiled=True,
    )
    proj_out = jnp.einsum(
        "tsd,de->tse", attn_seq, w_dense, preferred_element_type=single
    ) + b_dense.astype(single)
    pre_act = jnp.einsum("tsd,df->tsf", act_two, w_up, preferred_element_type=single) + b_up.astype(
        single
    )
    gelu_out = gelu_value(pre_act).astype(half_type)
    mlp_out = jnp.einsum(
        "tsf,fd->tsd", gelu_out, w_down, preferred_element_type=single
    ) + b_down.astype(single)
    output = (inputs_f + proj_out + mlp_out).astype(half_type)
    back_params = (
        lax.all_gather(qkv_weight, AXES, axis=0, tiled=True),
        lax.all_gather(qkv_bias, AXES, axis=0, tiled=True),
        lax.all_gather(dense_weight, AXES, axis=0, tiled=True),
        lax.all_gather(dense_bias, AXES, axis=0, tiled=True),
        lax.all_gather(norm1_gain, AXES, axis=0, tiled=True),
        lax.all_gather(norm1_bias, AXES, axis=0, tiled=True),
        lax.all_gather(norm2_gain, AXES, axis=0, tiled=True),
        lax.all_gather(norm2_bias, AXES, axis=0, tiled=True),
        lax.all_gather(up_weight, AXES, axis=0, tiled=True),
        lax.all_gather(up_bias, AXES, axis=0, tiled=True),
        lax.all_gather(down_weight, AXES, axis=0, tiled=True),
        lax.all_gather(down_bias, AXES, axis=0, tiled=True),
    )
    back_qkv = back_params[0]
    back_dense = back_params[2]
    back_gain_one = back_params[4].astype(single)
    back_gain_two = back_params[6].astype(single)
    back_up = back_params[8]
    back_down = back_params[10]
    grad_f = cotangent.astype(single)
    bias_sum = jnp.sum(grad_f, axis=(0, 1))
    down_w_grad = jnp.einsum("tsf,tsd->fd", gelu_out, cotangent, preferred_element_type=single)
    gelu_grad = jnp.einsum("tsd,fd->tsf", cotangent, back_down, preferred_element_type=single)
    pre_grad = (gelu_grad * gelu_slope(pre_act)).astype(half_type)
    up_w_grad = jnp.einsum("tsd,tsf->df", act_two, pre_grad, preferred_element_type=single)
    up_b_grad = jnp.sum(pre_grad.astype(single), axis=(0, 1))
    act_two_grad = jnp.einsum("tsf,df->tsd", pre_grad, back_up, preferred_element_type=single)
    gain_two_grad = jnp.sum(act_two_grad * normed, axis=(0, 1))
    shift_two_grad = jnp.sum(act_two_grad, axis=(0, 1))
    dense_w_grad = jnp.einsum("tsd,tse->de", attn_seq, cotangent, preferred_element_type=single)
    attn_grad = jnp.einsum(
        "tse,de->tsd", cotangent, back_dense, preferred_element_type=single
    ).astype(half_type)
    grad_loc = lax.all_to_all(attn_grad, ULY, split_axis=2, concat_axis=0, tiled=True)
    grad_h = grad_loc.reshape(local_rows, seq_count, local_heads, HD)

    def backward_block(acc_pair, step_index):
        row_start, seq_index, query_rows, row_pos, limit = select(step_index)
        own_slot = (row_start, seq_index, zero_idx, zero_idx)
        out_rows = lax.dynamic_slice(attn_h, own_slot, row_shape)
        grad_rows = lax.dynamic_slice(grad_h, own_slot, row_shape)
        log_total = log_totals[step_index]
        delta_row = jnp.transpose(
            jnp.sum(grad_rows.astype(single) * out_rows.astype(single), axis=-1), (1, 2, 0)
        )

        def grad_step(key_index, carry):
            key_acc, value_acc, query_acc = carry
            masked, key_rows, value_rows, slot = block_scores(
                query_rows, row_pos, key_index, seq_index
            )
            probs_f = jnp.exp(masked - log_total[..., None])
            value_part = jnp.einsum(
                "shqk,qshd->kshd",
                probs_f.astype(half_type),
                grad_rows,
                preferred_element_type=single,
            )
            grad_prob = jnp.einsum(
                "qshd,kshd->shqk", grad_rows, value_rows, preferred_element_type=single
            )
            grad_score = (probs_f * (grad_prob - delta_row[..., None]) * scale_factor).astype(
                half_type
            )
            query_acc = query_acc + jnp.einsum(
                "shqk,kshd->qshd", grad_score, key_rows, preferred_element_type=single
            )
            key_part = jnp.einsum(
                "shqk,qshd->kshd", grad_score, query_rows, preferred_element_type=single
            )
            key_acc = lax.dynamic_update_slice(
                key_acc, lax.dynamic_slice(key_acc, slot, key_part.shape) + key_part, slot
            )
            value_acc = lax.dynamic_update_slice(
                value_acc, lax.dynamic_slice(value_acc, slot, value_part.shape) + value_part, slot
            )
            return (key_acc, value_acc, query_acc)

        key_acc, value_acc, query_acc = lax.fori_loop(
            zero_idx, limit, grad_step, (acc_pair[0], acc_pair[1], jnp.zeros(row_shape, single))
        )
        return ((key_acc, value_acc), query_acc[:, 0])

    acc_zero = jnp.zeros((total_rows, seq_count, local_heads, HD), single)
    acc_final, query_parts = lax.scan(backward_block, (acc_zero, acc_zero), step_ids)
    query_grad = jnp.transpose(
        query_parts.reshape(n_blocks, seq_count, block_rows, local_heads, HD), (0, 2, 1, 3, 4)
    ).reshape(local_rows, seq_count, local_heads, HD)
    key_terms = jnp.transpose(
        acc_final[0].reshape(uly_size, blk_size, tok_rows, seq_count, features), (1, 0, 2, 3, 4)
    ).reshape(total_rows, seq_count, features)
    value_terms = jnp.transpose(
        acc_final[1].reshape(uly_size, blk_size, tok_rows, seq_count, features), (1, 0, 2, 3, 4)
    ).reshape(total_rows, seq_count, features)
    key_back, value_back = (
        lax.psum_scatter(key_terms, BLK, scatter_dimension=0, tiled=True),
        lax.psum_scatter(value_terms, BLK, scatter_dimension=0, tiled=True),
    )
    cos_h, sin_h = rotary_tables(query_pos, rotary)
    query_send = (
        rotate_back(query_grad, cos_h, sin_h, rotary)
        .reshape(local_rows, seq_count, features)
        .astype(half_type)
    )
    key_send = (
        rotate_back(key_back.reshape(local_rows, seq_count, local_heads, HD), cos_h, sin_h, rotary)
        .reshape(local_rows, seq_count, features)
        .astype(half_type)
    )
    value_send = value_back.astype(half_type)
    query_ret, key_ret, value_ret = (
        lax.all_to_all(query_send, ULY, split_axis=0, concat_axis=2, tiled=True),
        lax.all_to_all(key_send, ULY, split_axis=0, concat_axis=2, tiled=True),
        lax.all_to_all(value_send, ULY, split_axis=0, concat_axis=2, tiled=True),
    )
    qkv_grad = jnp.concatenate([query_ret, key_ret, value_ret], axis=-1)
    qkv_w_grad = jnp.einsum("tsd,tsf->df", act_one, qkv_grad, preferred_element_type=single)
    qkv_b_grad = jnp.sum(qkv_grad.astype(single), axis=(0, 1))
    act_one_grad = jnp.einsum("tsf,df->tsd", qkv_grad, back_qkv, preferred_element_type=single)
    gain_one_grad = jnp.sum(act_one_grad * normed, axis=(0, 1))
    shift_one_grad = jnp.sum(act_one_grad, axis=(0, 1))
    input_grad = (
        grad_f
        + norm_back(act_one_grad, normed, inverse, back_gain_one)
        + norm_back(act_two_grad, normed, inverse, back_gain_two)
    )
    summed = (
        lax.psum_scatter(qkv_w_grad, AXES, scatter_dimension=0, tiled=True),
        lax.psum_scatter(qkv_b_grad, AXES, scatter_dimension=0, tiled=True),
        lax.psum_scatter(
            dense_w_grad, AXES, scatter_dimension=0, tiled=True
        ),
        lax.psum_scatter(bias_sum, AXES, scatter_dimension=0, tiled=True),
        lax.psum_scatter(
            gain_one_grad, AXES, scatter_dimension=0, tiled=True
        ),
        lax.psum_scatter(
            shift_one_grad, AXES, scatter_dimension=0, tiled=True
        ),
        lax.psum_scatter(
            gain_two_grad, AXES, scatter_dimension=0, tiled=True
        ),
        lax.psum_scatter(
            shift_two_grad, AXES, scatter_dimension=0, tiled=True
        ),
        lax.psum_scatter(up_w_grad, AXES, scatter_dimension=0, tiled=True),
        lax.psum_scatter(up_b_grad, AXES, scatter_dimension=0, tiled=True),
        lax.psum_scatter(down_w_grad, AXES, scatter_dimension=0, tiled=True),
        lax.psum_scatter(bias_sum, AXES, scatter_dimension=0, tiled=True),
    )
    return (
        output,
        input_grad,
        summed[0],
        summed[1],
        summed[2],
        summed[3],
        summed[4],
        summed[5],
        summed[6],
        summed[7],
        summed[8],
        summed[9],
        summed[10],
        summed[11],
    )


MESH = pl.DeviceIdType.MESH


class Place:
    def __init__(self, planes):
        self.planes = planes
        self.b = lax.axis_index(BATCH)
        self.u = lax.axis_index(ULY)
        k = lax.axis_index(BLK)
        self.y, self.c = k // 2, k % 2
        self.t = self.u * 4 + k
        self.xn, self.yn, self.pn = self.peer(4), self.peer(2), self.peer(1)

    def rank(self, d):
        u = 1 - self.u if d & 4 else self.u
        y = 1 - self.y if d & 2 else self.y
        c = 1 - self.c if d & 1 else self.c
        return u * 4 + y * 2 + c

    def chip(self, d):
        return self.rank(d) // 2

    def peer(self, d):
        u = 1 - self.u if d & 4 else self.u
        y = 1 - self.y if d & 2 else self.y
        c = 1 - self.c if d & 1 else self.c
        return {BATCH: self.b, ULY: u, BLK: y * 2 + c}

    def along(self, step):
        return {BATCH: self.b + step, ULY: self.u, BLK: self.y * 2 + self.c}

    def barrier(self):
        sem = pltpu.get_barrier_semaphore()
        for d in range(1, 8):
            pl.semaphore_signal(sem, inc=1, device_id=self.peer(d), device_id_type=MESH)

        @pl.when(self.b > 0)
        def _():
            pl.semaphore_signal(sem, inc=1, device_id=self.along(-1), device_id_type=MESH)

        @pl.when(self.b < self.planes - 1)
        def _():
            pl.semaphore_signal(sem, inc=1, device_id=self.along(1), device_id_type=MESH)

        below = (self.b > 0).astype(jnp.int32)
        above = (self.b < self.planes - 1).astype(jnp.int32)
        pl.semaphore_wait(sem, 7 + below + above)


class Mail:
    def __init__(self, send, recv):
        self.send, self.recv, self.used, self.open = send, recv, 0, []

    def slots(self, n):
        first = self.used
        self.used += n
        return first

    def copy(self, src, dst, slot, device, recv_slot=None):
        return pltpu.make_async_remote_copy(
            src_ref=src,
            dst_ref=dst,
            send_sem=self.send.at[slot],
            recv_sem=self.recv.at[slot if recv_slot is None else recv_slot],
            device_id=device,
            device_id_type=MESH,
        )

    def post(self, src, dst, slot, device):
        made = self.copy(src, dst, slot, device)
        made.start()
        self.open.append(made)

    def arrived(self, dst, slot, device):
        self.copy(dst, dst, slot, device).wait_recv()

    def close(self):
        for made in self.open:
            made.wait_send()


class PlaneGather:
    def __init__(self, at, mail, shard, whole):
        self.at, self.mail, self.shard, self.whole = at, mail, shard, whole
        self.rows = shard.shape[1]
        self.base = mail.slots(8)

    def block(self, d, half=None):
        rows = pl.ds(pl.multiple_of(self.at.rank(d) * self.rows, self.rows), self.rows)
        halves = self.shard.shape[0] // 2
        if half is None:
            return self.whole.at[:, rows, :]
        return self.whole.at[pl.ds(half * halves, halves), rows, :]

    def start(self):
        at, mail, s = self.at, self.mail, self.base
        mine = self.block(0)
        mail.post(self.shard, mine, s, at.xn)
        mail.post(self.shard, mine, s + 1, at.yn)
        mail.post(self.shard, mine, s + 2, at.pn)
        mine[...] = self.shard[...]

    def relay(self):
        at, mail, s = self.at, self.mail, self.base
        mail.arrived(self.block(2), s + 1, at.yn)
        mail.post(self.block(2, 0), self.block(2, 0), s + 3, at.xn)
        mail.arrived(self.block(4), s, at.xn)
        mail.post(self.block(4, 1), self.block(4, 1), s + 4, at.yn)
        mail.post(self.block(2), self.block(2), s + 5, at.pn)
        mail.post(self.block(4), self.block(4), s + 6, at.pn)

    def finish(self):
        at, mail, s = self.at, self.mail, self.base
        mail.arrived(self.block(6, 0), s + 3, at.xn)
        mail.arrived(self.block(6, 1), s + 4, at.yn)
        mail.post(self.block(6), self.block(6), s + 7, at.pn)
        mail.arrived(self.block(1), s + 2, at.pn)
        mail.arrived(self.block(3), s + 5, at.pn)
        mail.arrived(self.block(5), s + 6, at.pn)
        mail.arrived(self.block(7), s + 7, at.pn)


class LineGather:
    def __init__(self, at, mail, held):
        self.at, self.mail, self.held = at, mail, held
        self.up, self.down = mail.slots(at.planes), mail.slots(at.planes)

    def pass_on(self, slot, src=None):
        at = self.at
        part = self.held.at[slot]
        src = part if src is None else src

        @pl.when((slot <= at.b) & (at.b < at.planes - 1))
        def _():
            self.mail.copy(src, part, self.up + slot, at.along(1)).start()

        @pl.when((slot >= at.b) & (at.b > 0))
        def _():
            self.mail.copy(src, part, self.down + slot, at.along(-1)).start()

    def start(self, src=None):
        self.pass_on(self.at.b, src)

    def take(self, distance):
        at = self.at

        @pl.when(at.b >= distance)
        def _():
            slot = at.b - distance
            self.mail.arrived(self.held.at[slot], self.up + slot, at.along(-1))
            self.pass_on(slot)

        @pl.when(at.b + distance < at.planes)
        def _():
            slot = at.b + distance
            self.mail.arrived(self.held.at[slot], self.down + slot, at.along(1))
            self.pass_on(slot)

    def close(self):
        at = self.at
        for slot in range(at.planes):
            part = self.held.at[slot]

            @pl.when((slot <= at.b) & (at.b < at.planes - 1))
            def _():
                self.mail.copy(part, part, self.up + slot, at.along(1)).wait_send()

            @pl.when((slot >= at.b) & (at.b > 0))
            def _():
                self.mail.copy(part, part, self.down + slot, at.along(-1)).wait_send()


class PlaneExchange:
    def __init__(self, at, mail, piece, landing):
        self.at, self.mail, self.piece, self.landing = at, mail, piece, landing
        self.base = mail.slots(8)

    def start(self):
        at = self.at
        for d in range(1, 8):
            self.mail.post(
                self.piece(at.rank(d)), self.landing(at.t), self.base + d, at.peer(d)
            )
        self.landing(at.t)[...] = self.piece(at.t)[...]

    def finish(self):
        at = self.at
        for d in range(1, 8):
            self.mail.arrived(self.landing(at.rank(d)), self.base + d, at.peer(d))


class PairExchange:
    def __init__(self, at, mail, src, dst, landed):
        self.at, self.mail, self.src, self.dst, self.landed = at, mail, src, dst, landed
        self.base = mail.slots(1)

    def start(self):
        self.mail.post(self.src, self.dst, self.base, self.at.pn)

    def finish(self):
        self.mail.arrived(self.landed, self.base, self.at.pn)


GATHER_SLOTS = 16 + 5 * 8 + 3 * 8 + 1


def gather_kernel(planes, x, cot, wq_s, wu_s, wd_s, wo_s, vec, xa, ca, wq, wu, wd, wo2, va, wo, send, recv):
    at = Place(planes)
    at.barrier()
    mail = Mail(send, recv)
    b, t, c = at.b, at.t, at.c
    rows = wq_s.shape[1]
    depth = wd_s.shape[0]
    pair = planes // 2
    gx = PlaneGather(at, mail, x, xa)
    gc = PlaneGather(at, mail, cot, ca)
    line_wd, line_wo, line_v = LineGather(at, mail, wd), LineGather(at, mail, wo), LineGather(at, mail, va)
    line_wq, line_wu = LineGather(at, mail, wq), LineGather(at, mail, wu)

    def strip(whole):
        return lambda rank: whole.at[b, pl.ds(pl.multiple_of(rank * rows, rows), rows), :]

    ex_q = PlaneExchange(at, mail, lambda rank: wq_s.at[rank], strip(wq))
    ex_u = PlaneExchange(at, mail, lambda rank: wu_s.at[rank], strip(wu))
    ex_v = PlaneExchange(at, mail, lambda rank: vec, lambda rank: va.at[b, rank])
    line_wd.start(wd_s)
    ex_q.start()
    gx.start()
    ex_u.start()
    ex_v.start()
    line_wo.start(wo_s)
    gc.start()
    wd[b] = wd_s[...]
    wo[b] = wo_s[...]
    ex_q.finish()
    line_wq.start()
    gx.relay()
    ex_u.finish()
    line_wu.start()
    ex_v.finish()
    line_v.start()
    gx.finish()
    gc.relay()
    lines = (line_wd, line_wo, line_wq, line_wu, line_v)
    for distance in range(1, planes):
        for line in lines:
            line.take(distance)
        if distance == 1:
            gc.finish()
    mine = wo2.at[:, c]
    swap = PairExchange(
        at, mail, wo.at[pl.ds(pair * (1 - c), pair)], mine, wo2.at[:, 1 - c]
    )
    swap.start()
    mine[...] = wo[pl.ds(pair * c, pair)]
    swap.finish()
    mail.close()
    for line in lines:
        line.close()


class PlaneReduce:
    def __init__(self, at, mail, terms, out, pairs, sums, side):
        self.at, self.mail, self.terms, self.out = at, mail, terms, out
        self.pairs, self.sums, self.side = pairs, sums, side
        self.base = mail.slots(8)
        self.order = (6, 4, 2, 0)
        self.halves = terms.shape[0] // 2

    def start(self):
        at = self.at
        for i, d in enumerate(self.order):
            chip = at.chip(d)
            self.mail.post(
                self.terms.at[:, chip, 1 - at.c], self.pairs.at[:, chip], self.base + i, at.pn
            )

    def half(self, ref, i):
        return ref.at[pl.ds(i * self.halves, self.halves)]

    def fold(self):
        at, mail, s = self.at, self.mail, self.base
        for i, d in enumerate(self.order):
            chip = at.chip(d)
            mail.arrived(self.pairs.at[:, chip], s + i, at.pn)
            total = self.terms[:, chip, at.c].astype(jnp.float32) + self.pairs[:, chip].astype(
                jnp.float32
            )
            self.sums[:, chip] = total.astype(self.sums.dtype)
            if d == 6:
                far = self.sums.at[:, chip]
                mail.post(self.half(far, 0), self.half(self.side.at[0], 0), s + 4, at.xn)
                mail.post(self.half(far, 1), self.half(self.side.at[0], 1), s + 5, at.yn)

    def turn(self):
        at, mail, s = self.at, self.mail, self.base
        for i, d, other, slot, nbr in ((1, 4, at.yn, 5, at.xn), (0, 2, at.xn, 4, at.yn)):
            chip = at.chip(d)
            landed = self.half(self.side.at[0], i)
            mail.arrived(landed, s + slot, other)
            part = self.half(self.sums.at[:, chip], i)
            part[...] = (part[...].astype(jnp.float32) + landed[...].astype(jnp.float32)).astype(
                self.sums.dtype
            )
            whole = self.sums.at[:, chip]
            mail.post(whole, self.side.at[2 - i], s + 6 + i, nbr)

    def finish(self):
        at, mail, s = self.at, self.mail, self.base
        mail.arrived(self.side.at[1], s + 7, at.xn)
        mail.arrived(self.side.at[2], s + 6, at.yn)
        self.out[...] = (
            self.sums[:, at.chip(0)].astype(jnp.float32)
            + self.side[1].astype(jnp.float32)
            + self.side[2].astype(jnp.float32)
        )


class LineReduce:
    def __init__(self, at, mail, terms, above, below):
        self.at, self.mail, self.terms = at, mail, terms
        self.above, self.below = above, below
        self.up, self.down = mail.slots(at.planes), mail.slots(at.planes)

    def run(self, rank):
        last = self.at.planes - 1
        self.forward_up(last - rank)
        self.forward_down(rank)

    def forward_up(self, slot):
        self._forward(slot, self.below, self.up, 1, self.at.b < slot, self.at.b == 0)

    def forward_down(self, slot):
        self._forward(
            slot, self.above, self.down, -1, self.at.b > slot, self.at.b == self.at.planes - 1
        )

    def _forward(self, slot, held, base, step, ahead, edge):
        at, mail = self.at, self.mail
        part = held.at[slot]

        @pl.when(ahead & edge)
        def _():
            mail.copy(self.terms.at[slot], part, base + slot, at.along(step)).start()

        @pl.when(ahead & jnp.logical_not(edge))
        def _():
            mail.arrived(part, base + slot, at.along(-step))
            total = self.terms[slot].astype(jnp.float32) + part[...].astype(jnp.float32)
            part[...] = total.astype(part.dtype)
            mail.copy(part, part, base + slot, at.along(step)).start()

    def finish(self, out):
        at, mail = self.at, self.mail
        b = at.b
        kind = out.dtype

        @pl.when(b == 0)
        def _():
            mail.arrived(self.above.at[b], self.down + b, at.along(1))
            out[...] = (
                self.terms[b].astype(jnp.float32) + self.above[b].astype(jnp.float32)
            ).astype(kind)

        @pl.when(b == at.planes - 1)
        def _():
            mail.arrived(self.below.at[b], self.up + b, at.along(-1))
            out[...] = (
                self.terms[b].astype(jnp.float32) + self.below[b].astype(jnp.float32)
            ).astype(kind)

        @pl.when((b > 0) & (b < at.planes - 1))
        def _():
            mail.arrived(self.below.at[b], self.up + b, at.along(-1))
            mail.arrived(self.above.at[b], self.down + b, at.along(1))
            out[...] = (
                self.terms[b].astype(jnp.float32)
                + self.below[b].astype(jnp.float32)
                + self.above[b].astype(jnp.float32)
            ).astype(kind)

    def close(self):
        at = self.at
        for slot in range(at.planes):
            part = self.terms.at[slot]

            @pl.when(at.b < slot)
            def _():
                self.mail.copy(part, part, self.up + slot, at.along(1)).wait_send()

            @pl.when(at.b > slot)
            def _():
                self.mail.copy(part, part, self.down + slot, at.along(-1)).wait_send()


REDUCE_SLOTS = 16 + 5 * 8 + 3 * 8 + 1


def reduce_kernel(
    planes, po, pg, gq, gu, gd, go, vec,
    out, gin, dq, du, dd, do, dv,
    pairs_o, sums_o, side_o, pairs_g, sums_g, side_g,
    go4, go_in, vec_in, vec_sum, fq, fu, aq, bq, au, bu, ad, bd, ao, bo, av, bv, send, recv,
):
    at = Place(planes)
    at.barrier()
    mail = Mail(send, recv)
    t, c = at.t, at.c
    rows = dq.shape[1]
    pair = planes // 2
    ro = PlaneReduce(at, mail, po, out, pairs_o, sums_o, side_o)
    rg = PlaneReduce(at, mail, pg, gin, pairs_g, sums_g, side_g)
    swap = PairExchange(
        at, mail, go.at[:, 1 - c], go4.at[pl.ds(pair * c, pair)], go4.at[pl.ds(pair * (1 - c), pair)]
    )
    ex_v = PlaneExchange(at, mail, lambda rank: vec.at[:, rank], lambda rank: vec_in.at[rank])
    line_d, line_o = LineReduce(at, mail, gd, ad, bd), LineReduce(at, mail, go4, ao, bo)
    line_q, line_u = LineReduce(at, mail, gq, aq, bq), LineReduce(at, mail, gu, au, bu)
    line_v = LineReduce(at, mail, vec_sum, av, bv)

    def strip(whole):
        return lambda rank: whole.at[pl.ds(pl.multiple_of(rank * rows, rows), rows), :]

    ex_q = PlaneExchange(at, mail, strip(fq), lambda rank: dq.at[rank])
    ex_u = PlaneExchange(at, mail, strip(fu), lambda rank: du.at[rank])
    line_u.run(0)
    line_q.run(0)
    swap.start()
    ex_v.start()
    ro.start()
    rg.start()
    go4[pl.ds(pair * c, pair)] = go[:, c]
    line_u.run(1)
    line_q.run(1)
    line_u.run(2)
    line_q.run(2)
    line_d.run(0)
    ex_v.finish()
    swap.finish()
    vec_sum[...] = jnp.sum(vec_in[...], axis=0)
    line_o.run(0)
    line_v.run(0)
    ro.fold()
    rg.fold()
    line_d.run(1)
    ro.turn()
    rg.turn()
    for line in (line_o, line_v):
        line.run(1)
    for line in (line_d, line_o, line_v):
        line.run(2)
    line_u.finish(fu)
    ex_u.start()
    line_q.finish(fq)
    ex_q.start()
    ro.finish()
    rg.finish()
    line_d.finish(dd)
    line_o.finish(do)
    line_v.finish(dv)
    ex_u.finish()
    ex_q.finish()
    mail.close()
    for line in (line_u, line_q, line_d, line_o, line_v):
        line.close()


VMEM = pl.BlockSpec(memory_space=pltpu.VMEM)


def call(kernel, outs, scratch, slots, number, *operands):
    return pl.pallas_call(
        kernel,
        out_shape=[jax.ShapeDtypeStruct(shape, kind) for shape, kind in outs],
        in_specs=[VMEM] * len(operands),
        out_specs=[VMEM] * len(outs),
        scratch_shapes=[pltpu.VMEM(shape, kind) for shape, kind in scratch]
        + [pltpu.SemaphoreType.DMA((slots,)), pltpu.SemaphoreType.DMA((slots,))],
        compiler_params=pltpu.CompilerParams(
            collective_id=number, has_side_effects=True, vmem_limit_bytes=60 * 2**20
        ),
    )(*operands)


def body(shape, *operands):
    residual_in, qkv_weight, down_weight = operands[0], operands[1], operands[11]
    planes = shape[BATCH]
    ranks = shape[ULY] * shape[BLK]
    heads = residual_in.shape[2] // HD
    fits = (
        shape[ULY] == 2
        and shape[BLK] == 4
        and planes % 2 == 0
        and residual_in.shape[1] % 2 == 0
        and 2 * qkv_weight.shape[0] == HD
        and heads == ranks * planes // 2
        and down_weight.shape[0] % 128 == 0
    )
    return fast_body(planes, *operands) if fits else general_body(*operands)


def fast_body(
    planes,
    residual_in,
    qkv_weight,
    qkv_bias,
    dense_weight,
    dense_bias,
    norm1_gain,
    norm1_bias,
    norm2_gain,
    norm2_bias,
    up_weight,
    up_bias,
    down_weight,
    down_bias,
    cotangent,
):
    single = jnp.float32
    half_type = jnp.bfloat16
    ranks = 8
    tok_rows, seqs, width = residual_in.shape
    rows = qkv_weight.shape[0]
    depth = down_weight.shape[0]
    hidden = planes * depth
    pair = planes // 2
    own_heads = pair
    head_cols = own_heads * HD
    length = ranks * tok_rows
    rotary = HD // 4
    scale_factor = 1.0 / math.sqrt(HD)
    k_index = lax.axis_index(BLK)
    rank = lax.axis_index(ULY) * 4 + k_index
    chip, core = rank // 2, rank % 2

    x_own = jnp.transpose(residual_in, (1, 0, 2))
    cot_own = jnp.transpose(cotangent, (1, 0, 2))
    wq_send = jnp.transpose(
        qkv_weight.reshape(rows, 3, 2, pair, ranks // 2, HD), (4, 2, 0, 1, 3, 5)
    ).reshape(ranks, rows, 3 * head_cols)
    wu_send = jnp.transpose(
        up_weight.reshape(rows, planes, ranks, depth), (2, 0, 1, 3)
    ).reshape(ranks, rows, hidden)
    vectors = (
        qkv_bias, up_bias, dense_bias, norm1_gain, norm1_bias, norm2_gain, norm2_bias, down_bias,
    )
    sizes = [v.shape[0] for v in vectors]
    room = -(-sum(sizes) // 1024) * 1024
    lanes = (room // 128, 128)
    vec = jnp.concatenate(
        [v.astype(single) for v in vectors] + [jnp.zeros((room - sum(sizes),), single)]
    ).reshape(lanes)

    x_all, cot_all, wq, wu, wd, wo, vec_all = call(
        functools.partial(gather_kernel, planes),
        [
            ((seqs, length, width), half_type),
            ((seqs, length, width), half_type),
            ((planes, ranks * rows, 3 * head_cols), half_type),
            ((planes, ranks * rows, hidden), half_type),
            ((planes, depth, width), half_type),
            ((pair, 2, rows, width), half_type),
            ((planes, ranks) + lanes, single),
        ],
        [((planes, rows, width), half_type)],
        GATHER_SLOTS,
        0,
        x_own,
        cot_own,
        wq_send,
        wu_send,
        down_weight,
        dense_weight,
        vec,
    )
    wq = wq.reshape(width, 3 * head_cols)
    wu = wu.reshape(width, hidden)
    wd = wd.reshape(hidden, width)
    wo = wo.reshape(head_cols, width)
    flat = vec_all.reshape(planes * ranks, room)
    ends = [sum(sizes[:i]) for i in range(len(sizes) + 1)]
    b_qkv, b_up, b_dense, gain_one, shift_one, gain_two, shift_two, b_down = [
        flat[:, ends[i] : ends[i + 1]].reshape(-1) for i in range(len(sizes))
    ]
    bq = lax.dynamic_slice(
        b_qkv.reshape(3, 2, pair, ranks // 2, HD), (0, core, 0, chip, 0), (3, 1, pair, 1, HD)
    ).reshape(3 * head_cols)
    bu = lax.dynamic_slice(
        b_up.reshape(planes, ranks, depth), (0, rank, 0), (planes, 1, depth)
    ).reshape(hidden)

    inputs_f = x_all.astype(single)
    normed, inverse = layer_norm(inputs_f)
    act_one = (normed * gain_one + shift_one).astype(half_type)
    act_two = (normed * gain_two + shift_two).astype(half_type)
    qkv = jnp.einsum("std,df->tsf", act_one, wq, preferred_element_type=single) + bq
    cosine, sine_table = rotary_tables(jnp.arange(length, dtype=jnp.int32), rotary)
    qkv = qkv.reshape(length, seqs, 3, own_heads, HD)
    query = rotate_fwd(qkv[:, :, 0], cosine, sine_table, rotary).astype(half_type)
    key = rotate_fwd(qkv[:, :, 1], cosine, sine_table, rotary).astype(half_type)
    value = qkv[:, :, 2].astype(half_type)
    scores = jnp.einsum("qshd,kshd->shqk", query, key, preferred_element_type=single) * scale_factor
    places = jnp.arange(length, dtype=jnp.int32)
    scores = jnp.where((places[None, :] <= places[:, None])[None, None], scores, -jnp.inf)
    top = jnp.max(scores, axis=-1, keepdims=True)
    log_total = top + jnp.log(jnp.sum(jnp.exp(scores - top), axis=-1, keepdims=True))
    probs = jnp.exp(scores - log_total)
    probs_b = probs.astype(half_type)
    attn = jnp.einsum("shqk,kshd->sqhd", probs_b, value, preferred_element_type=single).astype(
        half_type
    )
    attn_flat = attn.reshape(seqs, length, head_cols)
    pre = jnp.einsum("std,df->stf", act_two, wu, preferred_element_type=single) + bu
    gelu_out = gelu_value(pre).astype(half_type)
    out_terms = jnp.einsum("std,de->ste", attn_flat, wo, preferred_element_type=single) + jnp.einsum(
        "stf,fd->std", gelu_out, wd, preferred_element_type=single
    )
    down_w_grad = jnp.einsum("stf,std->fd", gelu_out, cot_all, preferred_element_type=single)
    gelu_grad = jnp.einsum("std,fd->stf", cot_all, wd, preferred_element_type=single)
    pre_grad = (gelu_grad * gelu_slope(pre)).astype(half_type)
    up_w_grad = jnp.einsum("std,stf->df", act_two, pre_grad, preferred_element_type=single)
    up_b_grad = jnp.sum(pre_grad.astype(single), axis=(0, 1))
    act_two_grad = jnp.einsum("stf,df->std", pre_grad, wu, preferred_element_type=single)
    dense_w_grad = jnp.einsum("std,ste->de", attn_flat, cot_all, preferred_element_type=single)
    attn_grad = jnp.einsum("ste,de->std", cot_all, wo, preferred_element_type=single).astype(
        half_type
    ).reshape(seqs, length, own_heads, HD)
    value_grad = jnp.einsum("shqk,sqhd->kshd", probs_b, attn_grad, preferred_element_type=single)
    grad_prob = jnp.einsum("sqhd,kshd->shqk", attn_grad, value, preferred_element_type=single)
    delta = jnp.transpose(
        jnp.sum(attn_grad.astype(single) * attn.astype(single), axis=-1), (0, 2, 1)
    )
    grad_score = (probs * (grad_prob - delta[..., None]) * scale_factor).astype(half_type)
    query_grad = jnp.einsum("shqk,kshd->qshd", grad_score, key, preferred_element_type=single)
    key_grad = jnp.einsum("shqk,qshd->kshd", grad_score, query, preferred_element_type=single)
    qkv_grad = jnp.stack(
        [
            rotate_back(query_grad, cosine, sine_table, rotary),
            rotate_back(key_grad, cosine, sine_table, rotary),
            value_grad,
        ],
        axis=2,
    ).astype(half_type).reshape(length, seqs, 3 * head_cols)
    qkv_w_grad = jnp.einsum("std,tsf->df", act_one, qkv_grad, preferred_element_type=single)
    qkv_b_grad = jnp.sum(qkv_grad.astype(single), axis=(0, 1))
    act_one_grad = jnp.einsum("tsf,df->std", qkv_grad, wq, preferred_element_type=single)
    in_terms = act_one_grad * gain_one + act_two_grad * gain_two
    bias_sum = jnp.sum(cot_own.astype(single), axis=(0, 1))
    small = (
        lax.dynamic_update_slice(
            jnp.zeros((3, 2, pair, ranks // 2, HD), single),
            qkv_b_grad.reshape(3, 1, pair, 1, HD),
            (0, core, 0, chip, 0),
        ),
        lax.dynamic_update_slice(
            jnp.zeros((planes, ranks, depth), single),
            up_b_grad.reshape(planes, 1, depth),
            (0, rank, 0),
        ),
        bias_sum,
        jnp.sum(act_one_grad * normed, axis=(0, 1)),
        jnp.sum(act_one_grad, axis=(0, 1)),
        jnp.sum(act_two_grad * normed, axis=(0, 1)),
        jnp.sum(act_two_grad, axis=(0, 1)),
    )
    small_vec = jnp.concatenate(
        [v.reshape(planes, ranks, -1) for v in small]
        + [jnp.zeros((planes, ranks, room - sum(sizes[:-1])), single)],
        axis=-1,
    ).reshape((planes, ranks) + lanes)

    plane_terms = (seqs, ranks // 2, 2, tok_rows, width)
    shard = (seqs, tok_rows, width)
    plane_scratch = [
        ((seqs, ranks // 2, tok_rows, width), half_type),
        ((seqs, ranks // 2, tok_rows, width), half_type),
        ((3,) + shard, half_type),
    ]
    q_shape = (planes, ranks * rows, 3 * head_cols)
    u_shape = (planes, ranks * rows, hidden)
    d_shape = (planes, depth, width)
    o_shape = (planes, rows, width)
    v_shape = (planes,) + lanes
    out_sum, in_sum, dq, du, dd, do, dv = call(
        functools.partial(reduce_kernel, planes),
        [
            (shard, single),
            (shard, single),
            ((ranks, rows, 3 * head_cols), half_type),
            ((ranks, rows, hidden), half_type),
            ((depth, width), single),
            ((rows, width), single),
            (lanes, single),
        ],
        plane_scratch * 2
        + [
            (o_shape, half_type),
            (o_shape, half_type),
            ((ranks,) + v_shape, single),
            (v_shape, single),
            (q_shape[1:], half_type),
            (u_shape[1:], half_type),
        ]
        + [
            (s, k)
            for s, k in (
                (q_shape, half_type),
                (u_shape, half_type),
                (d_shape, half_type),
                (o_shape, half_type),
                (v_shape, single),
            )
            for _ in range(2)
        ],
        REDUCE_SLOTS,
        1,
        out_terms.astype(half_type).reshape(plane_terms),
        in_terms.astype(half_type).reshape(plane_terms),
        qkv_w_grad.astype(half_type).reshape(q_shape),
        up_w_grad.astype(half_type).reshape(u_shape),
        down_w_grad.astype(half_type).reshape(d_shape),
        dense_w_grad.astype(half_type).reshape(pair, 2, rows, width),
        small_vec,
    )
    x_f = x_own.astype(single)
    own_normed, own_inverse = layer_norm(x_f)
    output = jnp.transpose((x_f + out_sum + b_dense + b_down).astype(half_type), (1, 0, 2))
    input_grad = jnp.transpose(
        cot_own.astype(single) + norm_back(in_sum, own_normed, own_inverse, 1.0), (1, 0, 2)
    )
    qkv_grad_out = jnp.transpose(
        dq.reshape(ranks // 2, 2, rows, 3, pair, HD), (2, 3, 1, 4, 0, 5)
    ).reshape(qkv_weight.shape).astype(single)
    up_grad_out = jnp.transpose(
        du.reshape(ranks, rows, planes, depth), (1, 2, 0, 3)
    ).reshape(up_weight.shape).astype(single)
    flat_v = dv.reshape(room)
    pieces = [flat_v[ends[i] : ends[i + 1]] for i in range(7)]
    return (
        output,
        input_grad,
        qkv_grad_out,
        pieces[0],
        do,
        pieces[2],
        pieces[3],
        pieces[4],
        pieces[5],
        pieces[6],
        up_grad_out,
        pieces[1],
        dd,
        pieces[2],
    )


def solution(mesh):
    placed = (
        P(TOKENS, BATCH, None),
        P(AXES, None),
        P(AXES),
        P(AXES, None),
        P(AXES),
        P(AXES),
        P(AXES),
        P(AXES),
        P(AXES),
        P(AXES, None),
        P(AXES),
        P(AXES, None),
        P(AXES),
        P(TOKENS, BATCH, None),
    )
    return jax.shard_map(
        functools.partial(body, dict(mesh.shape)),
        mesh=mesh,
        in_specs=placed,
        out_specs=(
            P(TOKENS, BATCH, None),
            P(TOKENS, BATCH, None),
            P(AXES, None),
            P(AXES),
            P(AXES, None),
            P(AXES),
            P(AXES),
            P(AXES),
            P(AXES),
            P(AXES),
            P(AXES, None),
            P(AXES),
            P(AXES, None),
            P(AXES),
        ),
        check_vma=False,
    )
```

profile of v0, /device:TPU:9, one launch (start us, length us, event | category | flops | bytes accessed | tf_op | source)
XLA Modules:
  0.0 232.9 jit_solution(12626761253894821105)
XLA Ops:
  0.8 2.0 copy_bitcast_fusion.5
  2.7 1.2 reshape.222
  4.3 0.9 reshape.223.wq_s
  5.2 1.0 copy.89
  6.3 0.8 reshape.225.wu_s
  7.2 0.7 concatenate.38
  7.9 66.0 %shard_map.245 = (bf16[2,512,1024]{2,1,0:T(8,128)(2,1)}, bf16[2,512,1024]{2,1,0:T(8,128)(2,1)}, bf16[4,256,384]{2,1,0:T(8,128)(2,1)}, bf16[4,256,512]{2,1,0:T(8,...) custom-call(bf16[2,64,1024]{2,1,0:T(8,128)(2,1)} %get-tuple-element.120.x, ...), custom_call_target="tpu_custom_call" | custom-call | tf_op jit(solution)/shard_map/pallas_call | solution.py:907
  73.9 1.1 copy.129
  75.2 1.9 convert_reduce_fusion
  77.1 2.3 fusion.12
  79.5 0.7 fusion.58
  80.3 1.4 convolution_add_fusion
  82.3 0.9 fusion.16
  83.2 0.9 exponential_reduce_fusion
  84.2 0.8 convolution_convert_fusion
  85.1 2.0 multiply_reduce_fusion
  87.0 1.6 multiply_convert_fusion
  89.1 0.7 convolution_bitcast_fusion.2
  90.1 1.2 convolution_bitcast_fusion.1
  91.6 0.9 copy-done.6
  92.5 3.5 %fusion.62 = (f32[1024]{0:T(1024)S(1)}, f32[1024,512,2]{0,1,2:T(8,128)}) fusion(bf16[1024,384,1]{1,0,2:T(8,128)(2,1)S(1)} %bitcast.177, bf16[512,2,384]{0,2,1:T(8,128)(2,1)S(1)} %bitcast.153), kind=kOutput, calls=%fused_computation.129 | convolution fusion | flops 806353920 | bytes 5771264 | tf_op jit(solution)/shard_map/tsf,df->std/dot_general | solution.py:1081
  96.2 3.4 %multiply_convert_fusion.1 = (bf16[2,512,512]{2,1,0:T(8,128)(2,1)S(1)}, f32[2,512,512]{2,1,0:T(8,128)S(1)}) fusion(f32[512]{0:T(512)S(1)} %bitcast.192, bf16[1024,512,1]{1,0,2:T(8,128)(2,1)} %bitcast.198, bf16[2,512,1024]{2,1,0:T(8,128)(2,1)} %get-tuple-element.29, f32[1024]{0:T(1024)S(1)} %add.160, f32[1024]{0:T(1024)S(1)} %mul.240, ...), kind=kOutput, calls=%fused_computation.35 | convolution fusion | flops 1083179008 | bytes 6309888 | tf_op jit(solution)/shard_map/std,df->stf/dot_general | solution.py:1048
  99.6 2.0 convert_reduce_fusion.1
  101.7 0.7 copy-done.5
  102.9 3.2 %fusion.55 = (f32[1024]{0:T(1024)S(1)}, f32[1024]{0:T(1024)S(1)}, f32[1024]{0:T(1024)S(1)}, bf16[2,512,1024]{2,1,0:T(8,128)(2,1)}) fusion(f32[2,512]{1,0:T(2,128)S(1)} %add_rsqrt_fusion, f32[2,512]{1,0:T(2,128)S(1)} %broadcast_multiply_fusion, bf16[2,512,1024]{2,1,0:T(8,128)(2,1)S(1)} %copy-done.2, f32[1024,512,2]{0,1,2:T(8,128)S(1)} %copy-done.5, ...), kind=kOutput, calls=%fused_computation.122 | convolution fusion | flops 1086321664 | bytes 10514432 | tf_op jit(solution)/shard_map/stf,df->std/dot_general | solution.py:1058
  106.1 0.7 reshape.245
  106.8 0.7 reshape.247
  107.5 0.7 reshape.248
  108.1 0.7 reshape.246
  108.8 0.7 reshape.242
  109.6 0.7 reshape.244
  111.0 1.1 concatenate.49
  112.1 0.7 copy.128
  112.8 4.5 %bitcast_convert_fusion.1 = bf16[1024,512]{1,0:T(8,128)(2,1)} fusion(bf16[2,512,512]{2,1,0:T(8,128)(2,1)} %copy-done.42, bf16[2,512,1024]{2,1,0:T(8,128)(2,1)} %get-tuple-element.29, f32[1024]{0:T(1024)} %copy-done.28, f32[1024]{0:T(1024)} %copy-done.27, f32[2,512]{1,0:T(2,128)} %copy-done.29, f32[2,512]{1,0:T(2,128)} %copy-done.21), kind=kOutput, calls=%fused_computation.33 | convolution fusion | flops 1080557568 | bytes 4210688 | tf_op jit(solution)/shard_map/std,stf->df/dot_general | solution.py:1056
  117.4 2.6 %bitcast_convert_fusion.2 = bf16[1024,384]{1,0:T(8,128)(2,1)} fusion(bf16[512,2,384]{0,2,1:T(8,128)(2,1)S(1)} %bitcast.154, bf16[2,512,1024]{2,1,0:T(8,128)(2,1)S(1)} %copy-done.3, f32[1024]{0:T(1024)S(1)} %copy-done.26, f32[1024]{0:T(1024)S(1)} %copy-done.24, f32[2,512]{1,0:T(2,128)S(1)} %copy-done.30, f32[2,512]{1,0:T(2,128)S(1)} %copy-done.22), kind=kOutput, calls=%fused_computation.38 | convolution fusion | flops 811991040 | bytes 3686400 | tf_op jit(solution)/shard_map/std,tsf->df/dot_general | solution.py:1079
  120.0 1.2 fusion.23
  121.2 0.7 fusion.63
  121.9 2.6 %add_convert_fusion = bf16[2,512,1024]{2,1,0:T(8,128)(2,1)} fusion(f32[2,512,1024]{2,1,0:T(8,128)S(1)} %fusion.63, bf16[2,512,512]{2,1,0:T(8,128)(2,1)S(1)} %get-tuple-element.111, bf16[512,1024,1]{1,0,2:T(8,128)(2,1)S(1)} %bitcast.175), kind=kOutput, calls=%fused_computation.19 | convolution fusion | flops 1075838976 | bytes 8388608 | tf_op jit(solution)/shard_map/stf,fd->std/dot_general | solution.py:1050
  124.5 2.3 bitcast_convert_fusion
  126.8 93.1 %shard_map.246 = (f32[2,64,1024]{2,1,0:T(8,128)}, f32[2,64,1024]{2,1,0:T(8,128)}, bf16[8,32,384]{2,1,0:T(8,128)(2,1)}, bf16[8,32,512]{2,1,0:T(8,128)(2,1)}, f32[...) custom-call(bf16[2,4,2,64,1024]{4,3,2,1,0:T(8,128)(2,1)} %bitcast.151, ...), custom_call_target="tpu_custom_call" | custom-call | tf_op jit(solution)/shard_map/pallas_call | solution.py:907
  219.9 1.5 reshape.253
  222.0 1.3 reshape.251
  223.3 1.2 reshape.254
  224.8 1.1 copy.123
  227.0 1.2 copy.72
  228.2 1.0 copy.71
  231.4 0.7 copy.136
  232.1 0.8 copy.137
  (146 shorter events, 7.9 us)
Async XLA Ops:
  0.6 6.5 %copy-start.32 = (bf16[96]{0:T(256)(128)(2,1)S(1)}, bf16[96]{0:T(256)(128)(2,1)}, u32[]{:S(2)}) copy-start(bf16[96]{0:T(256)(128)(2,1)} %param.16) | copy-start | bytes 580
  0.7 6.5 %copy-start.34 = (bf16[32]{0:T(256)(128)(2,1)S(1)}, bf16[32]{0:T(256)(128)(2,1)}, u32[]{:S(2)}) copy-start(bf16[32]{0:T(256)(128)(2,1)} %param.18) | copy-start | bytes 196
  0.7 6.5 %copy-start.35 = (bf16[32]{0:T(256)(128)(2,1)S(1)}, bf16[32]{0:T(256)(128)(2,1)}, u32[]{:S(2)}) copy-start(bf16[32]{0:T(256)(128)(2,1)} %param.19) | copy-start | bytes 196
  0.7 6.5 %copy-start.36 = (bf16[32]{0:T(256)(128)(2,1)S(1)}, bf16[32]{0:T(256)(128)(2,1)}, u32[]{:S(2)}) copy-start(bf16[32]{0:T(256)(128)(2,1)} %param.20) | copy-start | bytes 196
  0.7 6.5 %copy-start.37 = (bf16[32]{0:T(256)(128)(2,1)S(1)}, bf16[32]{0:T(256)(128)(2,1)}, u32[]{:S(2)}) copy-start(bf16[32]{0:T(256)(128)(2,1)} %param.21) | copy-start | bytes 196
  0.7 6.5 %copy-start.38 = (bf16[32]{0:T(256)(128)(2,1)S(1)}, bf16[32]{0:T(256)(128)(2,1)}, u32[]{:S(2)}) copy-start(bf16[32]{0:T(256)(128)(2,1)} %param.22) | copy-start | bytes 196
  0.7 6.5 %copy-start.33 = (bf16[128]{0:T(256)(128)(2,1)S(1)}, bf16[128]{0:T(256)(128)(2,1)}, u32[]{:S(2)}) copy-start(bf16[128]{0:T(256)(128)(2,1)} %param.24) | copy-start | bytes 772
  0.7 6.5 %copy-start.39 = (bf16[32]{0:T(256)(128)(2,1)S(1)}, bf16[32]{0:T(256)(128)(2,1)}, u32[]{:S(2)}) copy-start(bf16[32]{0:T(256)(128)(2,1)} %param.26) | copy-start | bytes 196
  73.9 6.4 %copy-start.1 = (bf16[2,512,1024]{2,1,0:T(8,128)(2,1)S(1)}, bf16[2,512,1024]{2,1,0:T(8,128)(2,1)}, u32[]{:S(2)}) copy-start(bf16[2,512,1024]{2,1,0:T(8,128)(2,1)} %get-tuple-element.29) | copy-start | bytes 6291460
  73.9 6.4 %copy-start.15 = (bf16[4,256,384]{2,1,0:T(8,128)(2,1)S(1)}, bf16[4,256,384]{2,1,0:T(8,128)(2,1)}, u32[]{:S(2)}) copy-start(bf16[4,256,384]{2,1,0:T(8,128)(2,1)} %get-tuple-element.28) | copy-start | bytes 2359300
  77.1 24.5 %copy-start.21 = (f32[2,512]{1,0:T(2,128)}, f32[2,512]{1,0:T(2,128)S(1)}, u32[]{:S(2)}) copy-start(f32[2,512]{1,0:T(2,128)S(1)} %broadcast_multiply_fusion) | copy-start | bytes 12292
  79.4 22.2 %copy-start.29 = (f32[2,512]{1,0:T(2,128)}, f32[2,512]{1,0:T(2,128)S(1)}, u32[]{:S(2)}) copy-start(f32[2,512]{1,0:T(2,128)S(1)} %add_rsqrt_fusion) | copy-start | bytes 12292
  80.2 21.5 %copy-start.23 = (f32[1024]{0:T(1024)}, f32[1024]{0:T(1024)S(1)}, u32[]{:S(2)}) copy-start(f32[1024]{0:T(1024)S(1)} %mul.225) | copy-start | bytes 12292
  80.3 1.4 copy-start.25
  82.3 1.9 copy-start
  82.3 1.9 copy-start.10
  91.6 0.9 copy-start.6
  96.1 5.6 %copy-start.27 = (f32[1024]{0:T(1024)}, f32[1024]{0:T(1024)S(1)}, u32[]{:S(2)}) copy-start(f32[1024]{0:T(1024)S(1)} %mul.240) | copy-start | bytes 12292
  96.2 3.4 %copy-start.28 = (f32[1024]{0:T(1024)}, f32[1024]{0:T(1024)S(1)}, u32[]{:S(2)}) copy-start(f32[1024]{0:T(1024)S(1)} %add.160) | copy-start | bytes 12292
  96.2 3.4 %copy-start.13 = (bf16[4,128,1024]{2,1,0:T(8,128)(2,1)S(1)}, bf16[4,128,1024]{2,1,0:T(8,128)(2,1)}, u32[]{:S(2)}) copy-start(bf16[4,128,1024]{2,1,0:T(8,128)(2,1)} %get-tuple-element.33) | copy-start | bytes 3145732
  99.6 2.1 copy-start.2
  99.6 2.8 %copy-start.5 = (f32[1024,512,2]{0,1,2:T(8,128)S(1)}, f32[1024,512,2]{0,1,2:T(8,128)}, u32[]{:S(2)}) copy-start(f32[1024,512,2]{0,1,2:T(8,128)} %get-tuple-element.118) | copy-start | bytes 12582916
  99.6 3.3 %copy-start.41 = (bf16[4,256,512]{2,1,0:T(8,128)(2,1)S(1)}, bf16[4,256,512]{2,1,0:T(8,128)(2,1)}, u32[]{:S(2)}) copy-start(bf16[4,256,512]{2,1,0:T(8,128)(2,1)} %get-tuple-element.32) | copy-start | bytes 3145732
  101.6 4.5 %copy-start.42 = (bf16[2,512,512]{2,1,0:T(8,128)(2,1)}, bf16[2,512,512]{2,1,0:T(8,128)(2,1)S(1)}, u32[]{:S(2)}) copy-start(bf16[2,512,512]{2,1,0:T(8,128)(2,1)S(1)} %get-tuple-element.116) | copy-start | bytes 3145732
  102.9 6.7 %copy-start.8 = (bf16[64,2,1024]{2,1,0:T(2,128)(2,1)S(1)}, bf16[64,2,1024]{2,1,0:T(2,128)(2,1)}, u32[]{:S(2)}) copy-start(bf16[64,2,1024]{2,1,0:T(2,128)(2,1)} %param.27) | copy-start | bytes 786436
  109.6 0.8 copy-start.20
  112.7 4.6 %copy-start.3 = (bf16[2,512,1024]{2,1,0:T(8,128)(2,1)S(1)}, bf16[2,512,1024]{2,1,0:T(8,128)(2,1)}, u32[]{:S(2)}) copy-start(bf16[2,512,1024]{2,1,0:T(8,128)(2,1)} %get-tuple-element.29) | copy-start | bytes 6291460
  112.7 4.6 %copy-start.7 = (bf16[512,2,3,2,64]{0,4,3,2,1:T(8,128)(2,1)S(1)}, bf16[512,2,3,2,64]{0,4,3,2,1:T(8,128)(2,1)}, u32[]{:S(2)}) copy-start(bf16[512,2,3,2,64]{0,4,3,2,1:T(8,128)(2,1)} %copy-done.6) | copy-start | bytes 2359300
  112.8 4.6 %copy-start.22 = (f32[2,512]{1,0:T(2,128)S(1)}, f32[2,512]{1,0:T(2,128)}, u32[]{:S(2)}) copy-start(f32[2,512]{1,0:T(2,128)} %copy-done.21) | copy-start | bytes 12292
  112.8 4.6 %copy-start.24 = (f32[1024]{0:T(1024)S(1)}, f32[1024]{0:T(1024)}, u32[]{:S(2)}) copy-start(f32[1024]{0:T(1024)} %copy-done.23) | copy-start | bytes 12292
  112.8 4.6 %copy-start.26 = (f32[1024]{0:T(1024)S(1)}, f32[1024]{0:T(1024)}, u32[]{:S(2)}) copy-start(f32[1024]{0:T(1024)} %copy-done.25) | copy-start | bytes 12292
  112.8 4.6 %copy-start.30 = (f32[2,512]{1,0:T(2,128)S(1)}, f32[2,512]{1,0:T(2,128)}, u32[]{:S(2)}) copy-start(f32[2,512]{1,0:T(2,128)} %copy-done.29) | copy-start | bytes 12292
  117.4 2.7 %copy-start.12 = (bf16[2,2,64,512]{3,2,1,0:T(8,128)(2,1)S(1)}, bf16[2,2,64,512]{3,2,1,0:T(8,128)(2,1)}, u32[]{:S(2)}) copy-start(bf16[2,2,64,512]{3,2,1,0:T(8,128)(2,1)} %get-tuple-element.114) | copy-start | bytes 786436
  117.4 3.8 %copy-start.11 = (bf16[2,2,32,1024]{3,2,1,0:T(8,128)(2,1)S(1)}, bf16[2,2,32,1024]{3,2,1,0:T(8,128)(2,1)}, u32[]{:S(2)}) copy-start(bf16[2,2,32,1024]{3,2,1,0:T(8,128)(2,1)} %get-tuple-element.31) | copy-start | bytes 786436
  120.0 1.9 copy-start.14
  219.9 6.0 %copy-start.4 = (bf16[64,2,1024]{2,1,0:T(2,128)(2,1)S(1)}, bf16[64,2,1024]{2,1,0:T(2,128)(2,1)}, u32[]{:S(2)}) copy-start(bf16[64,2,1024]{2,1,0:T(2,128)(2,1)} %param.14) | copy-start | bytes 786436
  219.9 6.4 %copy-start.9 = (f32[2,64,1024]{2,1,0:T(8,128)S(1)}, f32[2,64,1024]{2,1,0:T(8,128)}, u32[]{:S(2)}) copy-start(f32[2,64,1024]{2,1,0:T(8,128)} %get-tuple-element.36) | copy-start | bytes 1572868
  219.9 6.7 %copy-start.19 = (f32[32,32]{1,0:T(8,128)S(1)}, f32[32,32]{1,0:T(8,128)}, u32[]{:S(2)}) copy-start(f32[32,32]{1,0:T(8,128)} %get-tuple-element.86) | copy-start | bytes 12292
  223.3 3.4 %copy-start.17 = (f32[2,64,1024]{2,1,0:T(8,128)S(1)}, f32[2,64,1024]{2,1,0:T(8,128)}, u32[]{:S(2)}) copy-start(f32[2,64,1024]{2,1,0:T(8,128)} %get-tuple-element.35) | copy-start | bytes 1572868
  223.3 5.9 %copy-start.31 = (f32[8,128]{1,0:T(8,128)S(1)}, f32[8,128]{1,0:T(8,128)}, u32[]{:S(2)}) copy-start(f32[8,128]{1,0:T(8,128)} %get-tuple-element.38) | copy-start | bytes 12292
  223.3 8.1 %copy-start.18 = (f32[32,1024]{1,0:T(8,128)S(1)}, f32[32,1024]{1,0:T(8,128)}, u32[]{:S(2)}) copy-start(f32[32,1024]{1,0:T(8,128)} %get-tuple-element.169) | copy-start | bytes 393220
  223.3 8.8 %copy-start.16 = (f32[128,1024]{1,0:T(8,128)S(1)}, f32[128,1024]{1,0:T(8,128)}, u32[]{:S(2)}) copy-start(f32[128,1024]{1,0:T(8,128)} %get-tuple-element.177) | copy-start | bytes 1572868
  229.8 3.1 %copy-start.40 = (f32[32]{0:T(128)}, f32[32]{0:T(128)S(1)}, u32[]{:S(2)}) copy-start(f32[32]{0:T(128)S(1)} %get-tuple-element.170) | copy-start | bytes 388
where the time goes:
time: 233 us
  Pallas kernels  159 us (68%)
  matrix products  35.2 us (15%)
  local copies, waits for them, and re-layouts  30.4 us (13%)
  other arithmetic  6.77 us (3%)
    pallas_call x2, Pallas kernels, call(): pl.pallas_call(kernel, out_shape=[jax.ShapeDtypeStruct(shape, kind) for s...  159 us
    unnamed x97, local copies, waits for them, and re-layouts  10.3 us

commit v1 on v0

--- a/solution.py
+++ b/solution.py
@@ -3,6 +3,7 @@
 
 import jax
 import jax.numpy as jnp
+import numpy as np
 from jax import lax
 from jax.experimental import pallas as pl
 from jax.experimental.pallas import tpu as pltpu
@@ -636,67 +637,9 @@
         self.mail.arrived(self.landed, self.base, self.at.pn)
 
 
-GATHER_SLOTS = 16 + 5 * 8 + 3 * 8 + 1
-
-
-def gather_kernel(planes, x, cot, wq_s, wu_s, wd_s, wo_s, vec, xa, ca, wq, wu, wd, wo2, va, wo, send, recv):
-    at = Place(planes)
-    at.barrier()
-    mail = Mail(send, recv)
-    b, t, c = at.b, at.t, at.c
-    rows = wq_s.shape[1]
-    depth = wd_s.shape[0]
-    pair = planes // 2
-    gx = PlaneGather(at, mail, x, xa)
-    gc = PlaneGather(at, mail, cot, ca)
-    line_wd, line_wo, line_v = LineGather(at, mail, wd), LineGather(at, mail, wo), LineGather(at, mail, va)
-    line_wq, line_wu = LineGather(at, mail, wq), LineGather(at, mail, wu)
-
-    def strip(whole):
-        return lambda rank: whole.at[b, pl.ds(pl.multiple_of(rank * rows, rows), rows), :]
-
-    ex_q = PlaneExchange(at, mail, lambda rank: wq_s.at[rank], strip(wq))
-    ex_u = PlaneExchange(at, mail, lambda rank: wu_s.at[rank], strip(wu))
-    ex_v = PlaneExchange(at, mail, lambda rank: vec, lambda rank: va.at[b, rank])
-    line_wd.start(wd_s)
-    ex_q.start()
-    gx.start()
-    ex_u.start()
-    ex_v.start()
-    line_wo.start(wo_s)
-    gc.start()
-    wd[b] = wd_s[...]
-    wo[b] = wo_s[...]
-    ex_q.finish()
-    line_wq.start()
-    gx.relay()
-    ex_u.finish()
-    line_wu.start()
-    ex_v.finish()
-    line_v.start()
-    gx.finish()
-    gc.relay()
-    lines = (line_wd, line_wo, line_wq, line_wu, line_v)
-    for distance in range(1, planes):
-        for line in lines:
-            line.take(distance)
-        if distance == 1:
-            gc.finish()
-    mine = wo2.at[:, c]
-    swap = PairExchange(
-        at, mail, wo.at[pl.ds(pair * (1 - c), pair)], mine, wo2.at[:, 1 - c]
-    )
-    swap.start()
-    mine[...] = wo[pl.ds(pair * c, pair)]
-    swap.finish()
-    mail.close()
-    for line in lines:
-        line.close()
-
-
 class PlaneReduce:
-    def __init__(self, at, mail, terms, out, pairs, sums, side):
-        self.at, self.mail, self.terms, self.out = at, mail, terms, out
+    def __init__(self, at, mail, terms, pairs, sums, side):
+        self.at, self.mail, self.terms = at, mail, terms
         self.pairs, self.sums, self.side = pairs, sums, side
         self.base = mail.slots(8)
         self.order = (6, 4, 2, 0)
@@ -744,7 +687,7 @@
         at, mail, s = self.at, self.mail, self.base
         mail.arrived(self.side.at[1], s + 7, at.xn)
         mail.arrived(self.side.at[2], s + 6, at.yn)
-        self.out[...] = (
+        return (
             self.sums[:, at.chip(0)].astype(jnp.float32)
             + self.side[1].astype(jnp.float32)
             + self.side[2].astype(jnp.float32)
@@ -757,28 +700,34 @@
         self.above, self.below = above, below
         self.up, self.down = mail.slots(at.planes), mail.slots(at.planes)
 
-    def run(self, rank):
+    def edges(self):
+        at, last = self.at, self.at.planes - 1
+
+        @pl.when(at.b == 0)
+        def _():
+            for slot in range(last, 0, -1):
+                self.mail.copy(
+                    self.terms.at[slot], self.below.at[slot], self.up + slot, at.along(1)
+                ).start()
+
+        @pl.when(at.b == last)
+        def _():
+            for slot in range(last):
+                self.mail.copy(
+                    self.terms.at[slot], self.above.at[slot], self.down + slot, at.along(-1)
+                ).start()
+
+    def hop(self, hop, rank):
         last = self.at.planes - 1
-        self.forward_up(last - rank)
-        self.forward_down(rank)
-
-    def forward_up(self, slot):
-        self._forward(slot, self.below, self.up, 1, self.at.b < slot, self.at.b == 0)
-
-    def forward_down(self, slot):
-        self._forward(
-            slot, self.above, self.down, -1, self.at.b > slot, self.at.b == self.at.planes - 1
-        )
-
-    def _forward(self, slot, held, base, step, ahead, edge):
+        if last - rank > hop:
+            self._forward(last - rank, self.below, self.up, 1, self.at.b == hop)
+            self._forward(rank, self.above, self.down, -1, self.at.b == last - hop)
+
+    def _forward(self, slot, held, base, step, here):
         at, mail = self.at, self.mail
         part = held.at[slot]
 
-        @pl.when(ahead & edge)
-        def _():
-            mail.copy(self.terms.at[slot], part, base + slot, at.along(step)).start()
-
-        @pl.when(ahead & jnp.logical_not(edge))
+        @pl.when(here)
         def _():
             mail.arrived(part, base + slot, at.along(-step))
             total = self.terms[slot].astype(jnp.float32) + part[...].astype(jnp.float32)
@@ -828,108 +777,496 @@
                 self.mail.copy(part, part, self.down + slot, at.along(-1)).wait_send()
 
 
-REDUCE_SLOTS = 16 + 5 * 8 + 3 * 8 + 1
-
-
-def reduce_kernel(
-    planes, po, pg, gq, gu, gd, go, vec,
-    out, gin, dq, du, dd, do, dv,
-    pairs_o, sums_o, side_o, pairs_g, sums_g, side_g,
-    go4, go_in, vec_in, vec_sum, fq, fu, aq, bq, au, bu, ad, bd, ao, bo, av, bv, send, recv,
-):
+TILE = 256
+LANES = 128
+
+
+def dot_nn(a, b):
+    return lax.dot_general(a, b, (((1,), (0,)), ((), ())), preferred_element_type=jnp.float32)
+
+
+def dot_nt(a, b):
+    return lax.dot_general(a, b, (((1,), (1,)), ((), ())), preferred_element_type=jnp.float32)
+
+
+def dot_tn(a, b):
+    return lax.dot_general(a, b, (((0,), (0,)), ((), ())), preferred_element_type=jnp.float32)
+
+
+def turn(value, tables, rows, sign):
+    straight, early, late = (table[rows, :] for table in tables)
+    ahead = pltpu.roll(value, LANES - HD // 8, 1)
+    behind = pltpu.roll(value, HD // 8, 1)
+    return value * straight + sign * (ahead * early + behind * late)
+
+
+def of_head(value, head):
+    lane = lax.broadcasted_iota(jnp.int32, value.shape, 1)
+    return jnp.where(lane // HD == head, value, jnp.zeros_like(value))
+
+
+def total_rows(value):
+    return jnp.sum(value, axis=0, keepdims=True)
+
+
+class Layer:
+    def __init__(self, refs):
+        self.__dict__.update(refs)
+        self.seqs, self.length, self.width = self.xa.shape
+        self.per_seq = self.length // TILE
+        self.tiles = self.seqs * self.per_seq
+        self.heads = LANES // HD
+
+    def rows(self, tile):
+        return pl.ds(pl.multiple_of(tile * TILE, TILE), TILE)
+
+    def in_seq(self, ref, tile):
+        rows = pl.ds(pl.multiple_of(tile % self.per_seq * TILE, TILE), TILE)
+        return ref[tile // self.per_seq, rows, :]
+
+    def loop(self, count, step):
+        def run(i, carry):
+            step(i)
+            return carry
+
+        lax.fori_loop(0, count, run, 0)
+
+    def wide(self, row):
+        planes = self.va.shape[0]
+        return jnp.concatenate(
+            [self.va[b, pl.ds(2 * row + a, 1), :] for b in range(planes) for a in range(2)], axis=1
+        )
+
+    def statistics(self):
+        def step(i):
+            x = self.in_seq(self.xa, i).astype(jnp.float32)
+            center = jnp.mean(x, axis=1, keepdims=True)
+            shifted = x - center
+            spread = jnp.mean(shifted * shifted, axis=1, keepdims=True)
+            self.center[self.rows(i), :] = center
+            self.inverse[self.rows(i), :] = lax.rsqrt(spread + EPSILON)
+
+        self.loop(self.tiles, step)
+
+    def normed(self, i):
+        x = self.in_seq(self.xa, i).astype(jnp.float32)
+        return (x - self.center[self.rows(i), :]) * self.inverse[self.rows(i), :]
+
+    def activations(self):
+        gain_one, shift_one, gain_two, shift_two = (self.wide(j) for j in (1, 2, 3, 4))
+
+        def step(i):
+            normed = self.normed(i)
+            self.act_one[self.rows(i), :] = (normed * gain_one + shift_one).astype(jnp.bfloat16)
+            self.act_two[self.rows(i), :] = (normed * gain_two + shift_two).astype(jnp.bfloat16)
+
+        self.loop(self.tiles, step)
+
+    def bias(self, first, count):
+        rows = sum(self.va[b, pl.ds(first, count), :] for b in range(self.va.shape[0]))
+        return jnp.concatenate([rows[i : i + 1] for i in range(count)], axis=1)
+
+    def project(self):
+        bias = self.bias(12, 3)
+
+        def step(i):
+            weight = self.wq[...].reshape(self.width, 3 * LANES)
+            qkv = dot_nn(self.act_one[self.rows(i), :], weight) + bias
+            rows = pl.ds(pl.multiple_of(i % self.per_seq * TILE, TILE), TILE)
+            query = turn(qkv[:, :LANES], self.tables, rows, 1.0).astype(jnp.bfloat16)
+            self.query[self.rows(i), :] = query * jnp.asarray(1.0 / math.sqrt(HD), jnp.bfloat16)
+            self.key[self.rows(i), :] = turn(
+                qkv[:, LANES : 2 * LANES], self.tables, rows, 1.0
+            ).astype(jnp.bfloat16)
+            self.value[self.rows(i), :] = qkv[:, 2 * LANES :].astype(jnp.bfloat16)
+
+        self.loop(self.tiles, step)
+
+    def keys(self, seq, block):
+        start = pl.multiple_of(seq * self.length, TILE)
+        return pl.ds(start, (block + 1) * TILE)
+
+    def attend(self):
+        def step(seq):
+            for block in range(self.per_seq):
+                rows = self.rows(seq * self.per_seq + block)
+                keys = self.keys(seq, block)
+                key, value, query = self.key[keys, :], self.value[keys, :], self.query[rows, :]
+                out = None
+                for head in range(self.heads):
+                    scores = dot_nt(of_head(query, head), key)
+                    at = lax.broadcasted_iota(jnp.int32, scores.shape, 0) + block * TILE
+                    to = lax.broadcasted_iota(jnp.int32, scores.shape, 1)
+                    scores = jnp.where(to <= at, scores, -jnp.inf)
+                    top = jnp.max(scores, axis=1, keepdims=True)
+                    weight = jnp.exp(scores - top)
+                    weight = weight * (1.0 / jnp.sum(weight, axis=1, keepdims=True))
+                    self.probs[block][seq * self.heads + head] = weight
+                    part = dot_nn(weight.astype(jnp.bfloat16), value)
+                    out = of_head(part, head) if out is None else out + of_head(part, head)
+                self.attn[rows, :] = out.astype(jnp.bfloat16)
+
+        self.loop(self.seqs, step)
+
+    def attend_out_grad(self):
+        def step(i):
+            weight = self.wo2[...].reshape(LANES, self.width)
+            self.attn_grad[self.rows(i), :] = dot_nt(self.in_seq(self.ca, i), weight).astype(
+                jnp.bfloat16
+            )
+
+        self.loop(self.tiles, step)
+
+    def attend_grad(self, seq):
+        key_grad, value_grad = [None] * self.per_seq, [None] * self.per_seq
+        start = seq * self.per_seq
+        for block in range(self.per_seq):
+            rows = self.rows(start + block)
+            keys = self.keys(seq, block)
+            key, value, query = self.key[keys, :], self.value[keys, :], self.query[rows, :]
+            grad = self.attn_grad[rows, :]
+            inner = grad.astype(jnp.float32) * self.attn[rows, :].astype(jnp.float32)
+            query_grad = None
+            for head in range(self.heads):
+                own_grad = of_head(grad, head)
+                delta = jnp.sum(of_head(inner, head), axis=1, keepdims=True)
+                probs = self.probs[block][seq * self.heads + head]
+                grad_prob = dot_nt(own_grad, value)
+                grad_score = (probs * (grad_prob - delta)).astype(jnp.bfloat16)
+                part = dot_nn(grad_score, of_head(key, head))
+                query_grad = part if query_grad is None else query_grad + part
+                key_part = dot_tn(grad_score, of_head(query, head))
+                value_part = dot_tn(probs.astype(jnp.bfloat16), own_grad)
+                for b in range(block + 1):
+                    cut = slice(b * TILE, (b + 1) * TILE)
+                    key_grad[b] = key_part[cut] if key_grad[b] is None else key_grad[b] + key_part[cut]
+                    value_grad[b] = (
+                        value_part[cut] if value_grad[b] is None else value_grad[b] + value_part[cut]
+                    )
+            back = pl.ds(block * TILE, TILE)
+            self.qkv_grad[rows, :LANES] = turn(
+                query_grad * (1.0 / math.sqrt(HD)), self.tables, back, -1.0
+            ).astype(jnp.bfloat16)
+        for block in range(self.per_seq):
+            rows = self.rows(start + block)
+            back = pl.ds(block * TILE, TILE)
+            self.qkv_grad[rows, LANES : 2 * LANES] = turn(
+                key_grad[block], self.tables, back, -1.0
+            ).astype(jnp.bfloat16)
+            self.qkv_grad[rows, 2 * LANES :] = value_grad[block].astype(jnp.bfloat16)
+
+    def attend_grads(self):
+        self.loop(self.seqs, self.attend_grad)
+
+    def cot_flat(self):
+        return self.ca[...].reshape(self.seqs * self.length, self.width)
+
+    def qkv_weight_grad(self):
+        def step(i):
+            rows = self.gq.shape[1]
+            act = self.act_one[:, pl.ds(pl.multiple_of(i * rows, rows), rows)]
+            self.gq[i] = dot_tn(act, self.qkv_grad[...]).astype(jnp.bfloat16)
+
+        self.loop(self.gq.shape[0], step)
+
+    def dense_weight_grad(self):
+        self.go[...] = (
+            dot_tn(self.attn[...], self.cot_flat()).astype(jnp.bfloat16).reshape(self.go.shape)
+        )
+
+    def expand(self):
+        bias = self.bias(16, 4)
+
+        def step(i):
+            weight = self.wu[...].reshape(self.width, self.hidden)
+            pre = dot_nn(self.act_two[self.rows(i), :], weight) + bias
+            cdf = 0.5 * (1.0 + lax.erf(pre * INV_ROOT_TWO))
+            self.gelu[self.rows(i), :] = (pre * cdf).astype(jnp.bfloat16)
+            self.slope[self.rows(i), :] = cdf + pre * jnp.exp(-0.5 * pre * pre) * INV_ROOT_TWO_PI
+
+        self.loop(self.tiles, step)
+
+    def down_weight_grad(self):
+        def step(i):
+            depth = self.gd.shape[1]
+            part = self.gelu[:, pl.ds(pl.multiple_of(i * depth, depth), depth)]
+            self.gd[i] = dot_tn(part, self.cot_flat()).astype(jnp.bfloat16)
+
+        self.loop(self.gd.shape[0], step)
+
+    def hidden_grad(self):
+        def step(i):
+            weight = self.wd[...].reshape(self.hidden, self.width)
+            grad = dot_nt(self.in_seq(self.ca, i), weight)
+            self.pre_grad[self.rows(i), :] = (grad * self.slope[self.rows(i), :]).astype(
+                jnp.bfloat16
+            )
+
+        self.loop(self.tiles, step)
+
+    def up_weight_grad(self):
+        def step(i):
+            rows = self.gu.shape[1]
+            act = self.act_two[:, pl.ds(pl.multiple_of(i * rows, rows), rows)]
+            self.gu[i] = dot_tn(act, self.pre_grad[...]).astype(jnp.bfloat16)
+
+        self.loop(self.gu.shape[0], step)
+
+    def put_terms(self, terms, i, value):
+        seq, chips, cores, rows, width = terms.shape
+        n = TILE // (cores * rows)
+        terms[i // self.per_seq, pl.ds(i % self.per_seq * n, n)] = value.astype(
+            jnp.bfloat16
+        ).reshape(n, cores, rows, width)
+
+    def out_terms(self):
+        def step(i):
+            dense = self.wo2[...].reshape(LANES, self.width)
+            down = self.wd[...].reshape(self.hidden, self.width)
+            self.put_terms(
+                self.po,
+                i,
+                dot_nn(self.attn[self.rows(i), :], dense) + dot_nn(self.gelu[self.rows(i), :], down),
+            )
+
+        self.loop(self.tiles, step)
+
+    def in_terms(self):
+        gain_one, gain_two = self.wide(1), self.wide(3)
+        self.sums[...] = jnp.zeros_like(self.sums)
+
+        def step(i):
+            normed = self.normed(i)
+            weight = self.wq[...].reshape(self.width, 3 * LANES)
+            one = dot_nt(self.qkv_grad[self.rows(i), :], weight)
+            weight = self.wu[...].reshape(self.width, self.hidden)
+            two = dot_nt(self.pre_grad[self.rows(i), :], weight)
+            self.put_terms(self.pg, i, one * gain_one + two * gain_two)
+            for j, value in enumerate((one * normed, one, two * normed, two)):
+                self.sums[j : j + 1, :] += total_rows(value)
+
+        self.loop(self.tiles, step)
+
+    def small_terms(self):
+        ranks = self.sm.shape[0]
+        cot = total_rows(jnp.sum(self.cot_own[...].astype(jnp.float32), axis=0))
+        for rank in range(ranks):
+            cut = slice(rank * LANES, (rank + 1) * LANES)
+            self.sm[rank, 0:1, :] = cot[:, cut]
+            self.sm[rank, 1:5, :] = self.sums[0:4, cut]
+
+    def small_plane(self, slot):
+        total = jnp.sum(self.sm_in[...], axis=0)
+        self.vz[slot, 0:8, :] = total
+        qkv = total_rows(self.qkv_grad[...].astype(jnp.float32))
+        pre = total_rows(self.pre_grad[...].astype(jnp.float32))
+        for j in range(3):
+            self.vz[slot, 8 + j : 9 + j, :] = qkv[:, j * LANES : (j + 1) * LANES]
+        for j in range(self.hidden // LANES):
+            self.vz[slot, 12 + j : 13 + j, :] = pre[:, j * LANES : (j + 1) * LANES]
+
+    def result(self, out_sum, in_sum, out, in_grad):
+        x = self.x_own[...].astype(jnp.float32)
+        center = jnp.mean(x, axis=2, keepdims=True)
+        shifted = x - center
+        inverse = lax.rsqrt(jnp.mean(shifted * shifted, axis=2, keepdims=True) + EPSILON)
+        normed = shifted * inverse
+        bias = (self.wide(0) + self.wide(5))[None]
+        out[...] = (x + out_sum + bias).astype(jnp.bfloat16)
+        in_grad[...] = self.cot_own[...].astype(jnp.float32) + inverse * (
+            in_sum
+            - jnp.mean(in_sum, axis=2, keepdims=True)
+            - normed * jnp.mean(in_sum * normed, axis=2, keepdims=True)
+        )
+
+
+LAYER_SLOTS = 4 * 8 + 10 * 8 + 7 * 8 + 2
+
+
+def layer_kernel(names, planes, *refs):
+    refs = dict(zip(names, refs))
+    send, recv = refs.pop(names[-2]), refs.pop(names[-1])
+    refs.update(
+        tables=tuple(refs["table"].at[i] for i in range(3)),
+        probs=tuple(refs[name] for name in names if name.startswith("probs")),
+        hidden=refs["gelu"].shape[1],
+    )
+    do = Layer(refs)
     at = Place(planes)
+    mail = Mail(send, recv)
+    b, c = at.b, at.c
+    rows = do.wq_s.shape[1]
+    pair = planes // 2
+
+    def strip(whole):
+        return lambda rank: whole.at[b, pl.ds(pl.multiple_of(rank * rows, rows), rows), :]
+
+    def band(whole):
+        return lambda rank: whole.at[pl.ds(pl.multiple_of(rank * rows, rows), rows), :]
+
+    gather_x = PlaneGather(at, mail, do.x_own, do.xa)
+    gather_c = PlaneGather(at, mail, do.cot_own, do.ca)
+    line_v, line_o = LineGather(at, mail, do.va), LineGather(at, mail, do.wo)
+    line_q, line_u = LineGather(at, mail, do.wq), LineGather(at, mail, do.wu)
+    line_d = LineGather(at, mail, do.wd)
+    ex_v = PlaneExchange(at, mail, lambda rank: do.vec_s.at[rank], lambda rank: do.vec_in.at[rank])
+    ex_q = PlaneExchange(at, mail, lambda rank: do.wq_s.at[rank], strip(do.wq))
+    ex_u = PlaneExchange(at, mail, lambda rank: do.wu_s.at[rank], strip(do.wu))
+    mine = do.wo2.at[:, c]
+    swap_w = PairExchange(
+        at, mail, do.wo.at[pl.ds(pair * (1 - c), pair)], mine, do.wo2.at[:, 1 - c]
+    )
+    sum_o = LineReduce(at, mail, do.go4, do.above_o, do.below_o)
+    sum_q = LineReduce(at, mail, do.gq, do.above_q, do.below_q)
+    sum_u = LineReduce(at, mail, do.gu, do.above_u, do.below_u)
+    sum_d = LineReduce(at, mail, do.gd, do.above_d, do.below_d)
+    swap_g = PairExchange(
+        at,
+        mail,
+        do.go.at[:, 1 - c],
+        do.go4.at[pl.ds(pair * c, pair)],
+        do.go4.at[pl.ds(pair * (1 - c), pair)],
+    )
+    back_q = PlaneExchange(at, mail, band(do.fq), lambda rank: do.dq.at[rank])
+    back_u = PlaneExchange(at, mail, band(do.fu), lambda rank: do.du.at[rank])
+    fold_v = PlaneExchange(at, mail, lambda rank: do.sm.at[rank], lambda rank: do.sm_in.at[rank])
+    line_s = LineGather(at, mail, do.vz)
+    share_v = PlaneExchange(at, mail, lambda rank: do.vt, lambda rank: do.dv.at[rank])
+    plane_o = PlaneReduce(at, mail, do.po, do.pairs_o, do.sums_o, do.side_o)
+    plane_g = PlaneReduce(at, mail, do.pg, do.pairs_g, do.sums_g, do.side_g)
+
     at.barrier()
-    mail = Mail(send, recv)
-    t, c = at.t, at.c
-    rows = dq.shape[1]
-    pair = planes // 2
-    ro = PlaneReduce(at, mail, po, out, pairs_o, sums_o, side_o)
-    rg = PlaneReduce(at, mail, pg, gin, pairs_g, sums_g, side_g)
-    swap = PairExchange(
-        at, mail, go.at[:, 1 - c], go4.at[pl.ds(pair * c, pair)], go4.at[pl.ds(pair * (1 - c), pair)]
-    )
-    ex_v = PlaneExchange(at, mail, lambda rank: vec.at[:, rank], lambda rank: vec_in.at[rank])
-    line_d, line_o = LineReduce(at, mail, gd, ad, bd), LineReduce(at, mail, go4, ao, bo)
-    line_q, line_u = LineReduce(at, mail, gq, aq, bq), LineReduce(at, mail, gu, au, bu)
-    line_v = LineReduce(at, mail, vec_sum, av, bv)
-
-    def strip(whole):
-        return lambda rank: whole.at[pl.ds(pl.multiple_of(rank * rows, rows), rows), :]
-
-    ex_q = PlaneExchange(at, mail, strip(fq), lambda rank: dq.at[rank])
-    ex_u = PlaneExchange(at, mail, strip(fu), lambda rank: du.at[rank])
-    line_u.run(0)
-    line_q.run(0)
-    swap.start()
     ex_v.start()
-    ro.start()
-    rg.start()
-    go4[pl.ds(pair * c, pair)] = go[:, c]
-    line_u.run(1)
-    line_q.run(1)
-    line_u.run(2)
-    line_q.run(2)
-    line_d.run(0)
+    ex_q.start()
+    gather_x.start()
+    line_o.start(do.wo_s)
+    do.wo[b] = do.wo_s[...]
+    ex_u.start()
+    gather_c.start()
+    do.wd[b] = do.wd_s[...]
     ex_v.finish()
-    swap.finish()
-    vec_sum[...] = jnp.sum(vec_in[...], axis=0)
-    line_o.run(0)
-    line_v.run(0)
-    ro.fold()
-    rg.fold()
-    line_d.run(1)
-    ro.turn()
-    rg.turn()
-    for line in (line_o, line_v):
-        line.run(1)
-    for line in (line_d, line_o, line_v):
-        line.run(2)
-    line_u.finish(fu)
-    ex_u.start()
-    line_q.finish(fq)
-    ex_q.start()
-    ro.finish()
-    rg.finish()
-    line_d.finish(dd)
-    line_o.finish(do)
-    line_v.finish(dv)
+    do.va[b] = jnp.sum(do.vec_in[...], axis=0)
+    line_v.start()
+    ex_q.finish()
+    line_q.start()
+    gather_x.relay()
+    line_v.take(1)
+    line_o.take(1)
+    gather_x.finish()
+    line_q.take(1)
+    do.statistics()
+    line_v.take(2)
+    line_o.take(2)
+    line_q.take(2)
+    gather_c.relay()
     ex_u.finish()
-    ex_q.finish()
+    line_v.take(3)
+    do.activations()
+    line_o.take(3)
+    line_q.take(3)
+    line_u.start()
+    line_d.start(do.wd_s)
+    swap_w.start()
+    mine[...] = do.wo[pl.ds(pair * c, pair)]
+    do.project()
+    gather_c.finish()
+    do.attend()
+    line_u.take(1)
+    swap_w.finish()
+    do.attend_out_grad()
+    line_d.take(1)
+    do.attend_grads()
+    line_u.take(2)
+    do.dense_weight_grad()
+    swap_g.start()
+    do.go4[pl.ds(pair * c, pair)] = do.go[:, c]
+    do.qkv_weight_grad()
+    sum_q.edges()
+    swap_g.finish()
+    sum_o.edges()
+    line_d.take(2)
+    line_u.take(3)
+    do.expand()
+    sum_q.hop(1, 0)
+    sum_o.hop(1, 0)
+    do.down_weight_grad()
+    sum_d.edges()
+    sum_q.hop(1, 1)
+    sum_o.hop(1, 1)
+    sum_q.hop(2, 0)
+    sum_o.hop(2, 0)
+    line_d.take(3)
+    do.hidden_grad()
+    sum_d.hop(1, 0)
+    do.up_weight_grad()
+    sum_u.edges()
+    sum_d.hop(1, 1)
+    do.out_terms()
+    plane_o.start()
+    sum_d.hop(2, 0)
+    sum_q.finish(do.fq)
+    back_q.start()
+    do.in_terms()
+    plane_g.start()
+    do.small_terms()
+    fold_v.start()
+    plane_o.fold()
+    sum_u.hop(1, 0)
+    plane_g.fold()
+    fold_v.finish()
+    do.small_plane(b)
+    line_s.start()
+    plane_o.turn()
+    plane_g.turn()
+    sum_u.hop(1, 1)
+    line_s.take(1)
+    line_s.take(2)
+    sum_u.hop(2, 0)
+    line_s.take(3)
+    do.vt[...] = jnp.sum(do.vz[...], axis=0)
+    share_v.start()
+    do.result(plane_o.finish(), plane_g.finish(), do.out, do.in_grad)
+    sum_o.finish(do.dd_o)
+    sum_d.finish(do.dd)
+    sum_u.finish(do.fu)
+    back_u.start()
+    back_q.finish()
+    share_v.finish()
+    back_u.finish()
     mail.close()
-    for line in (line_u, line_q, line_d, line_o, line_v):
+    for line in (line_v, line_o, line_q, line_u, line_d, line_s, sum_o, sum_q, sum_u, sum_d):
         line.close()
 
 
 VMEM = pl.BlockSpec(memory_space=pltpu.VMEM)
 
 
-def call(kernel, outs, scratch, slots, number, *operands):
-    return pl.pallas_call(
-        kernel,
-        out_shape=[jax.ShapeDtypeStruct(shape, kind) for shape, kind in outs],
-        in_specs=[VMEM] * len(operands),
-        out_specs=[VMEM] * len(outs),
-        scratch_shapes=[pltpu.VMEM(shape, kind) for shape, kind in scratch]
-        + [pltpu.SemaphoreType.DMA((slots,)), pltpu.SemaphoreType.DMA((slots,))],
-        compiler_params=pltpu.CompilerParams(
-            collective_id=number, has_side_effects=True, vmem_limit_bytes=60 * 2**20
-        ),
-    )(*operands)
+def rotary_rows(length):
+    half = HD // 8
+    frequency = 1.0 / 10000.0 ** (np.arange(half) * (1.0 / half))
+    angles = np.arange(length)[:, None] * frequency[None, :]
+    table = np.zeros((3, length, HD))
+    table[0] = 1.0
+    table[0, :, :half] = table[0, :, half : 2 * half] = np.cos(angles)
+    table[1, :, :half] = -np.sin(angles)
+    table[2, :, half : 2 * half] = np.sin(angles)
+    return np.tile(table, (1, 1, LANES // HD)).astype(np.float32)
 
 
 def body(shape, *operands):
     residual_in, qkv_weight, down_weight = operands[0], operands[1], operands[11]
     planes = shape[BATCH]
     ranks = shape[ULY] * shape[BLK]
-    heads = residual_in.shape[2] // HD
+    tok_rows, seqs, width = residual_in.shape
     fits = (
-        shape[ULY] == 2
-        and shape[BLK] == 4
-        and planes % 2 == 0
-        and residual_in.shape[1] % 2 == 0
+        (shape[ULY], shape[BLK]) == (2, 4)
+        and planes == 4
+        and seqs % 2 == 0
         and 2 * qkv_weight.shape[0] == HD
-        and heads == ranks * planes // 2
-        and down_weight.shape[0] % 128 == 0
+        and width == ranks * LANES
+        and ranks * tok_rows % TILE == 0
+        and TILE % (2 * tok_rows) == 0
+        and down_weight.shape[0] == LANES
     )
     return fast_body(planes, *operands) if fits else general_body(*operands)
 
@@ -953,239 +1290,178 @@
 ):
     single = jnp.float32
     half_type = jnp.bfloat16
-    ranks = 8
     tok_rows, seqs, width = residual_in.shape
+    ranks = width // LANES
     rows = qkv_weight.shape[0]
     depth = down_weight.shape[0]
     hidden = planes * depth
     pair = planes // 2
-    own_heads = pair
-    head_cols = own_heads * HD
     length = ranks * tok_rows
-    rotary = HD // 4
-    scale_factor = 1.0 / math.sqrt(HD)
-    k_index = lax.axis_index(BLK)
-    rank = lax.axis_index(ULY) * 4 + k_index
-    chip, core = rank // 2, rank % 2
+    tokens = seqs * length
+    rank = lax.axis_index(ULY) * lax.axis_size(BLK) + lax.axis_index(BLK)
+    owner = lax.axis_index(BATCH) * ranks + rank
 
     x_own = jnp.transpose(residual_in, (1, 0, 2))
     cot_own = jnp.transpose(cotangent, (1, 0, 2))
     wq_send = jnp.transpose(
         qkv_weight.reshape(rows, 3, 2, pair, ranks // 2, HD), (4, 2, 0, 1, 3, 5)
-    ).reshape(ranks, rows, 3 * head_cols)
+    ).reshape(ranks, rows, 3 * LANES)
     wu_send = jnp.transpose(
         up_weight.reshape(rows, planes, ranks, depth), (2, 0, 1, 3)
     ).reshape(ranks, rows, hidden)
-    vectors = (
-        qkv_bias, up_bias, dense_bias, norm1_gain, norm1_bias, norm2_gain, norm2_bias, down_bias,
-    )
-    sizes = [v.shape[0] for v in vectors]
-    room = -(-sum(sizes) // 1024) * 1024
-    lanes = (room // 128, 128)
-    vec = jnp.concatenate(
-        [v.astype(single) for v in vectors] + [jnp.zeros((room - sum(sizes),), single)]
-    ).reshape(lanes)
-
-    x_all, cot_all, wq, wu, wd, wo, vec_all = call(
-        functools.partial(gather_kernel, planes),
-        [
-            ((seqs, length, width), half_type),
-            ((seqs, length, width), half_type),
-            ((planes, ranks * rows, 3 * head_cols), half_type),
-            ((planes, ranks * rows, hidden), half_type),
-            ((planes, depth, width), half_type),
-            ((pair, 2, rows, width), half_type),
-            ((planes, ranks) + lanes, single),
+    at_rank = (jnp.arange(ranks) == rank).astype(single)[:, None]
+    at_owner = (jnp.arange(ranks * planes) == owner).astype(single)[:, None]
+    placed = [
+        (at_rank * v.astype(single)[None]).reshape(1, 2, LANES)
+        for v in (dense_bias, norm1_gain, norm1_bias, norm2_gain, norm2_bias, down_bias)
+    ]
+    placed_qkv = jnp.transpose(
+        (at_owner * qkv_bias.astype(single)[None]).reshape(3, 2, pair, ranks // 2, HD),
+        (3, 1, 0, 2, 4),
+    ).reshape(ranks, 3, LANES)
+    placed_up = jnp.transpose(
+        (at_owner * up_bias.astype(single)[None]).reshape(planes, ranks, LANES), (1, 0, 2)
+    )
+    vec_send = jnp.concatenate(
+        [jnp.broadcast_to(p, (ranks, 2, LANES)) for p in placed]
+        + [
+            placed_qkv,
+            jnp.zeros((ranks, 1, LANES), single),
+            placed_up,
+            jnp.zeros((ranks, 4, LANES), single),
         ],
-        [((planes, rows, width), half_type)],
-        GATHER_SLOTS,
-        0,
-        x_own,
-        cot_own,
-        wq_send,
-        wu_send,
-        down_weight,
-        dense_weight,
-        vec,
-    )
-    wq = wq.reshape(width, 3 * head_cols)
-    wu = wu.reshape(width, hidden)
-    wd = wd.reshape(hidden, width)
-    wo = wo.reshape(head_cols, width)
-    flat = vec_all.reshape(planes * ranks, room)
-    ends = [sum(sizes[:i]) for i in range(len(sizes) + 1)]
-    b_qkv, b_up, b_dense, gain_one, shift_one, gain_two, shift_two, b_down = [
-        flat[:, ends[i] : ends[i + 1]].reshape(-1) for i in range(len(sizes))
-    ]
-    bq = lax.dynamic_slice(
-        b_qkv.reshape(3, 2, pair, ranks // 2, HD), (0, core, 0, chip, 0), (3, 1, pair, 1, HD)
-    ).reshape(3 * head_cols)
-    bu = lax.dynamic_slice(
-        b_up.reshape(planes, ranks, depth), (0, rank, 0), (planes, 1, depth)
-    ).reshape(hidden)
-
-    inputs_f = x_all.astype(single)
-    normed, inverse = layer_norm(inputs_f)
-    act_one = (normed * gain_one + shift_one).astype(half_type)
-    act_two = (normed * gain_two + shift_two).astype(half_type)
-    qkv = jnp.einsum("std,df->tsf", act_one, wq, preferred_element_type=single) + bq
-    cosine, sine_table = rotary_tables(jnp.arange(length, dtype=jnp.int32), rotary)
-    qkv = qkv.reshape(length, seqs, 3, own_heads, HD)
-    query = rotate_fwd(qkv[:, :, 0], cosine, sine_table, rotary).astype(half_type)
-    key = rotate_fwd(qkv[:, :, 1], cosine, sine_table, rotary).astype(half_type)
-    value = qkv[:, :, 2].astype(half_type)
-    scores = jnp.einsum("qshd,kshd->shqk", query, key, preferred_element_type=single) * scale_factor
-    places = jnp.arange(length, dtype=jnp.int32)
-    scores = jnp.where((places[None, :] <= places[:, None])[None, None], scores, -jnp.inf)
-    top = jnp.max(scores, axis=-1, keepdims=True)
-    log_total = top + jnp.log(jnp.sum(jnp.exp(scores - top), axis=-1, keepdims=True))
-    probs = jnp.exp(scores - log_total)
-    probs_b = probs.astype(half_type)
-    attn = jnp.einsum("shqk,kshd->sqhd", probs_b, value, preferred_element_type=single).astype(
-        half_type
-    )
-    attn_flat = attn.reshape(seqs, length, head_cols)
-    pre = jnp.einsum("std,df->stf", act_two, wu, preferred_element_type=single) + bu
-    gelu_out = gelu_value(pre).astype(half_type)
-    out_terms = jnp.einsum("std,de->ste", attn_flat, wo, preferred_element_type=single) + jnp.einsum(
-        "stf,fd->std", gelu_out, wd, preferred_element_type=single
-    )
-    down_w_grad = jnp.einsum("stf,std->fd", gelu_out, cot_all, preferred_element_type=single)
-    gelu_grad = jnp.einsum("std,fd->stf", cot_all, wd, preferred_element_type=single)
-    pre_grad = (gelu_grad * gelu_slope(pre)).astype(half_type)
-    up_w_grad = jnp.einsum("std,stf->df", act_two, pre_grad, preferred_element_type=single)
-    up_b_grad = jnp.sum(pre_grad.astype(single), axis=(0, 1))
-    act_two_grad = jnp.einsum("stf,df->std", pre_grad, wu, preferred_element_type=single)
-    dense_w_grad = jnp.einsum("std,ste->de", attn_flat, cot_all, preferred_element_type=single)
-    attn_grad = jnp.einsum("ste,de->std", cot_all, wo, preferred_element_type=single).astype(
-        half_type
-    ).reshape(seqs, length, own_heads, HD)
-    value_grad = jnp.einsum("shqk,sqhd->kshd", probs_b, attn_grad, preferred_element_type=single)
-    grad_prob = jnp.einsum("sqhd,kshd->shqk", attn_grad, value, preferred_element_type=single)
-    delta = jnp.transpose(
-        jnp.sum(attn_grad.astype(single) * attn.astype(single), axis=-1), (0, 2, 1)
-    )
-    grad_score = (probs * (grad_prob - delta[..., None]) * scale_factor).astype(half_type)
-    query_grad = jnp.einsum("shqk,kshd->qshd", grad_score, key, preferred_element_type=single)
-    key_grad = jnp.einsum("shqk,qshd->kshd", grad_score, query, preferred_element_type=single)
-    qkv_grad = jnp.stack(
-        [
-            rotate_back(query_grad, cosine, sine_table, rotary),
-            rotate_back(key_grad, cosine, sine_table, rotary),
-            value_grad,
-        ],
-        axis=2,
-    ).astype(half_type).reshape(length, seqs, 3 * head_cols)
-    qkv_w_grad = jnp.einsum("std,tsf->df", act_one, qkv_grad, preferred_element_type=single)
-    qkv_b_grad = jnp.sum(qkv_grad.astype(single), axis=(0, 1))
-    act_one_grad = jnp.einsum("tsf,df->std", qkv_grad, wq, preferred_element_type=single)
-    in_terms = act_one_grad * gain_one + act_two_grad * gain_two
-    bias_sum = jnp.sum(cot_own.astype(single), axis=(0, 1))
-    small = (
-        lax.dynamic_update_slice(
-            jnp.zeros((3, 2, pair, ranks // 2, HD), single),
-            qkv_b_grad.reshape(3, 1, pair, 1, HD),
-            (0, core, 0, chip, 0),
-        ),
-        lax.dynamic_update_slice(
-            jnp.zeros((planes, ranks, depth), single),
-            up_b_grad.reshape(planes, 1, depth),
-            (0, rank, 0),
-        ),
-        bias_sum,
-        jnp.sum(act_one_grad * normed, axis=(0, 1)),
-        jnp.sum(act_one_grad, axis=(0, 1)),
-        jnp.sum(act_two_grad * normed, axis=(0, 1)),
-        jnp.sum(act_two_grad, axis=(0, 1)),
-    )
-    small_vec = jnp.concatenate(
-        [v.reshape(planes, ranks, -1) for v in small]
-        + [jnp.zeros((planes, ranks, room - sum(sizes[:-1])), single)],
-        axis=-1,
-    ).reshape((planes, ranks) + lanes)
-
-    plane_terms = (seqs, ranks // 2, 2, tok_rows, width)
+        axis=1,
+    )
+    table = jnp.asarray(rotary_rows(length))
+    inputs = dict(
+        x_own=x_own,
+        cot_own=cot_own,
+        wq_s=wq_send,
+        wu_s=wu_send,
+        wd_s=down_weight,
+        wo_s=dense_weight,
+        vec_s=vec_send,
+        table=table,
+    )
     shard = (seqs, tok_rows, width)
-    plane_scratch = [
-        ((seqs, ranks // 2, tok_rows, width), half_type),
-        ((seqs, ranks // 2, tok_rows, width), half_type),
-        ((3,) + shard, half_type),
-    ]
-    q_shape = (planes, ranks * rows, 3 * head_cols)
+    lanes_in = vec_send.shape[1]
+    outputs = dict(
+        out=(shard, half_type),
+        in_grad=(shard, single),
+        dq=((ranks, rows, 3 * LANES), half_type),
+        du=((ranks, rows, hidden), half_type),
+        dd=((depth, width), single),
+        dd_o=((rows, width), single),
+        dv=((ranks, 16, LANES), single),
+    )
+    q_shape = (planes, ranks * rows, 3 * LANES)
     u_shape = (planes, ranks * rows, hidden)
     d_shape = (planes, depth, width)
     o_shape = (planes, rows, width)
-    v_shape = (planes,) + lanes
-    out_sum, in_sum, dq, du, dd, do, dv = call(
-        functools.partial(reduce_kernel, planes),
-        [
-            (shard, single),
-            (shard, single),
-            ((ranks, rows, 3 * head_cols), half_type),
-            ((ranks, rows, hidden), half_type),
-            ((depth, width), single),
-            ((rows, width), single),
-            (lanes, single),
-        ],
-        plane_scratch * 2
-        + [
-            (o_shape, half_type),
-            (o_shape, half_type),
-            ((ranks,) + v_shape, single),
-            (v_shape, single),
-            (q_shape[1:], half_type),
-            (u_shape[1:], half_type),
-        ]
-        + [
-            (s, k)
-            for s, k in (
-                (q_shape, half_type),
-                (u_shape, half_type),
-                (d_shape, half_type),
-                (o_shape, half_type),
-                (v_shape, single),
-            )
-            for _ in range(2)
-        ],
-        REDUCE_SLOTS,
-        1,
-        out_terms.astype(half_type).reshape(plane_terms),
-        in_terms.astype(half_type).reshape(plane_terms),
-        qkv_w_grad.astype(half_type).reshape(q_shape),
-        up_w_grad.astype(half_type).reshape(u_shape),
-        down_w_grad.astype(half_type).reshape(d_shape),
-        dense_w_grad.astype(half_type).reshape(pair, 2, rows, width),
-        small_vec,
-    )
-    x_f = x_own.astype(single)
-    own_normed, own_inverse = layer_norm(x_f)
-    output = jnp.transpose((x_f + out_sum + b_dense + b_down).astype(half_type), (1, 0, 2))
-    input_grad = jnp.transpose(
-        cot_own.astype(single) + norm_back(in_sum, own_normed, own_inverse, 1.0), (1, 0, 2)
-    )
+    chips = ranks // 2
+    scratch = dict(
+        xa=((seqs, length, width), half_type),
+        ca=((seqs, length, width), half_type),
+        wq=(q_shape, half_type),
+        wu=(u_shape, half_type),
+        wd=(d_shape, half_type),
+        wo=(o_shape, half_type),
+        wo2=((pair, 2, rows, width), half_type),
+        vec_in=((ranks, lanes_in, LANES), single),
+        va=((planes, lanes_in, LANES), single),
+        center=((tokens, 1), single),
+        inverse=((tokens, 1), single),
+        act_one=((tokens, width), half_type),
+        act_two=((tokens, width), half_type),
+        query=((tokens, LANES), half_type),
+        key=((tokens, LANES), half_type),
+        value=((tokens, LANES), half_type),
+        attn=((tokens, LANES), half_type),
+        attn_grad=((tokens, LANES), half_type),
+        qkv_grad=((tokens, 3 * LANES), half_type),
+        gelu=((tokens, hidden), half_type),
+        slope=((tokens, hidden), single),
+        pre_grad=((tokens, hidden), half_type),
+        gq=(q_shape, half_type),
+        gu=(u_shape, half_type),
+        gd=(d_shape, half_type),
+        go=((pair, 2, rows, width), half_type),
+        go4=(o_shape, half_type),
+        above_q=(q_shape, half_type),
+        below_q=(q_shape, half_type),
+        above_u=(u_shape, half_type),
+        below_u=(u_shape, half_type),
+        above_d=(d_shape, half_type),
+        below_d=(d_shape, half_type),
+        above_o=(o_shape, half_type),
+        below_o=(o_shape, half_type),
+        fq=(q_shape[1:], half_type),
+        fu=(u_shape[1:], half_type),
+        po=((seqs, chips, 2, tok_rows, width), half_type),
+        pg=((seqs, chips, 2, tok_rows, width), half_type),
+        pairs_o=((seqs, chips, tok_rows, width), half_type),
+        pairs_g=((seqs, chips, tok_rows, width), half_type),
+        sums_o=((seqs, chips, tok_rows, width), half_type),
+        sums_g=((seqs, chips, tok_rows, width), half_type),
+        side_o=((3,) + shard, half_type),
+        side_g=((3,) + shard, half_type),
+        sums=((8, width), single),
+        sm=((ranks, 8, LANES), single),
+        sm_in=((ranks, 8, LANES), single),
+        vz=((planes, 16, LANES), single),
+        vt=((16, LANES), single),
+    )
+    for block in range(length // TILE):
+        scratch["probs%d" % block] = ((seqs * LANES // HD, TILE, (block + 1) * TILE), single)
+    names = tuple(inputs) + tuple(outputs) + tuple(scratch) + ("send", "recv")
+    out, in_grad, dq, du, dd, dd_o, dv = pl.pallas_call(
+        functools.partial(layer_kernel, names, planes),
+        out_shape=[jax.ShapeDtypeStruct(*what) for what in outputs.values()],
+        in_specs=[VMEM] * len(inputs),
+        out_specs=[VMEM] * len(outputs),
+        scratch_shapes=[pltpu.VMEM(*what) for what in scratch.values()]
+        + [pltpu.SemaphoreType.DMA((LAYER_SLOTS,))] * 2,
+        compiler_params=pltpu.CompilerParams(
+            collective_id=0, has_side_effects=True, vmem_limit_bytes=60 * 2**20
+        ),
+    )(*inputs.values())
+
+    output = jnp.transpose(out, (1, 0, 2))
+    input_grad = jnp.transpose(in_grad, (1, 0, 2))
     qkv_grad_out = jnp.transpose(
         dq.reshape(ranks // 2, 2, rows, 3, pair, HD), (2, 3, 1, 4, 0, 5)
     ).reshape(qkv_weight.shape).astype(single)
     up_grad_out = jnp.transpose(
         du.reshape(ranks, rows, planes, depth), (1, 2, 0, 3)
     ).reshape(up_weight.shape).astype(single)
-    flat_v = dv.reshape(room)
-    pieces = [flat_v[ends[i] : ends[i + 1]] for i in range(7)]
+    wide = [
+        lax.dynamic_slice(dv[:, j].reshape(width), (owner * rows,), (rows,)) for j in range(5)
+    ]
+    qkv_bias_grad = lax.dynamic_slice(
+        jnp.transpose(
+            dv[:, 8:11].reshape(ranks // 2, 2, 3, pair, HD), (2, 1, 3, 0, 4)
+        ).reshape(3 * width),
+        (owner * qkv_bias.shape[0],),
+        qkv_bias.shape,
+    )
+    up_bias_grad = lax.dynamic_slice(
+        dv, (rank, 12 + lax.axis_index(BATCH), 0), (1, 1, LANES)
+    ).reshape(up_bias.shape)
     return (
         output,
         input_grad,
         qkv_grad_out,
-        pieces[0],
-        do,
-        pieces[2],
-        pieces[3],
-        pieces[4],
-        pieces[5],
-        pieces[6],
+        qkv_bias_grad,
+        dd_o,
+        wide[0],
+        wide[1],
+        wide[2],
+        wide[3],
+        wide[4],
         up_grad_out,
-        pieces[1],
+        up_bias_grad,
         dd,
-        pieces[2],
+        wide[0],
     )
 
 

time: 233 us -> 154 us (0.66)
  the two profiles are of different devices: /device:TPU:9 before, /device:TPU:0 now
where the time goes in v1:
time: 154 us
  Pallas kernels  131 us (85%)
  local copies, waits for them, and re-layouts  21.1 us (14%)
    pallas_call x1, Pallas kernels, fast_body(): pl.pallas_call(functools.partial(layer_kernel, names, planes), out_shape=...  131 us
    unnamed x45, local copies, waits for them, and re-layouts  5.91 us

profile of v1, /device:TPU:0, one launch (start us, length us, event | category | flops | bytes accessed | tf_op | source)
XLA Modules:
  0.0 153.7 jit_solution(9778101394973128033)
XLA Ops:
  0.7 0.0 copy-start.6
  0.8 0.6 copy-done.16
  1.3 0.1 broadcast_multiply_fusion.1
  1.4 0.1 mul.197
  1.5 0.1 reshape.248
  1.6 0.1 broadcast_multiply_fusion
  1.7 0.1 mul.167
  1.8 0.1 mul.168
  1.9 0.1 mul.170
  2.0 0.1 mul.174
  2.1 0.1 mul.178
  2.2 0.1 mul.182
  2.3 0.1 mul.186
  2.3 0.0 copy-done.15
  2.3 0.1 mul.190
  2.5 1.9 %concatenate.3.refs_6_ = f32[8,24,128]{2,1,0:T(8,128)} concatenate(f32[8,2,128]{2,1,0:T(2,128)S(1)} %broadcast_in_dim.16, f32[8,2,128]{2,1,0:T(2,128)S(1)} %broadcast_in_dim.17, f32[8,2,128]{2,1,0:T(2,128)S(1)} %broadcast_in_dim.18, f32[8,2,128]{2,1,0:T(2,128)S(1)} %broadcast_in_dim.19, f32[8,2,128]{2,1,0:T(2,128)S(1)} %broadcast_in_dim.20, f32[8,2,128]{2,1,0:T(2,128)S(1)} %broadcast_in_dim.21, ...), dimensions={1} | concatenate | bytes 196608 | tf_op jit(solution)/shard_map/concatenate | solution.py:1325
  4.5 0.0 copy-done.5
  4.5 0.9 copy_bitcast_fusion.3
  5.4 0.0 copy-done.7
  5.4 0.3 reshape.236
  5.7 0.3 copy.59
  6.0 0.0 copy-start.3
  6.0 0.9 reshape.237.refs_2_
  7.0 0.1 copy.60
  7.1 0.8 reshape.239.refs_3_
  7.9 131.4 %shard_map.254 = (bf16[2,64,1024]{2,1,0:T(8,128)(2,1)}, f32[2,64,1024]{2,1,0:T(8,128)}, bf16[8,32,384]{2,1,0:T(8,128)(2,1)}, bf16[8,32,512]{2,1,0:T(8,128)(2,1)}...) custom-call(bf16[2,64,1024]{2,1,0:T(8,128)(2,1)} %get-tuple-element.68.refs_0_, ...), custom_call_target="tpu_custom_call" | custom-call | tf_op jit(solution)/shard_map/pallas_call | solution.py:1417
  139.3 0.8 slice.18
  140.1 0.1 reshape.241
  140.2 0.1 reshape.242
  140.3 0.6 dynamic_slice.21
  140.9 1.0 fusion.1
  142.0 0.1 dynamic_slice.22
  142.0 0.6 dynamic_slice.23
  142.6 0.6 dynamic_slice.24
  143.2 0.6 dynamic_slice.25
  143.8 0.6 dynamic_slice.26
  144.4 1.2 dynamic-slice_bitcast_fusion
  145.6 0.5 reshape.246
  146.1 0.5 copy.43
  146.6 1.3 reshape.244
  147.9 0.2 reshape.247
  148.1 0.3 copy.46
  148.4 1.1 copy.58
  149.6 1.2 copy.48
  150.8 1.0 copy.47
  151.7 0.5 copy.64
  152.2 0.7 copy.65
  152.9 0.8 copy.66
  (56 shorter events, 0.2 us)
Async XLA Ops:
  0.7 1.0 copy-start.17
  0.7 0.7 copy-start.16
  0.7 1.2 copy-start.10
  0.7 1.3 copy-start.11
  0.7 1.4 copy-start.12
  0.7 1.4 copy-start.13
  0.7 1.5 copy-start.14
  0.7 1.6 %copy-start.15 = (bf16[32]{0:T(256)(128)(2,1)S(1)}, bf16[32]{0:T(256)(128)(2,1)}, u32[]{:S(2)}) copy-start(bf16[32]{0:T(256)(128)(2,1)} %param.27) | copy-start | bytes 196
  0.7 3.7 %copy-start.6 = (bf16[64,2,1024]{2,1,0:T(2,128)(2,1)S(1)}, bf16[64,2,1024]{2,1,0:T(2,128)(2,1)}, u32[]{:S(2)}) copy-start(bf16[64,2,1024]{2,1,0:T(2,128)(2,1)} %param.15) | copy-start | bytes 786436
  0.8 3.7 %copy-start.5 = (bf16[64,2,1024]{2,1,0:T(2,128)(2,1)S(1)}, bf16[64,2,1024]{2,1,0:T(2,128)(2,1)}, u32[]{:S(2)}) copy-start(bf16[64,2,1024]{2,1,0:T(2,128)(2,1)} %param.28) | copy-start | bytes 786436
  4.5 0.9 copy-start.7
  6.0 1.0 copy-start.3
  139.3 6.2 %copy-start.8 = (bf16[8,32,384]{2,1,0:T(8,128)(2,1)S(1)}, bf16[8,32,384]{2,1,0:T(8,128)(2,1)}, u32[]{:S(2)}) copy-start(bf16[8,32,384]{2,1,0:T(8,128)(2,1)} %get-tuple-element.23) | copy-start | bytes 589828
  142.0 9.7 %copy-start.18 = (f32[32]{0:T(128)}, f32[32]{0:T(128)S(1)}, u32[]{:S(2)}) copy-start(f32[32]{0:T(128)S(1)} %dynamic_slice.22) | copy-start | bytes 388
  146.6 1.3 copy-start.2
  148.4 1.1 copy-start.1
  149.5 1.2 copy-start.4
  149.5 2.7 %copy-start.9 = (f32[32,1024]{1,0:T(8,128)S(1)}, f32[32,1024]{1,0:T(8,128)}, u32[]{:S(2)}) copy-start(f32[32,1024]{1,0:T(8,128)} %get-tuple-element.115) | copy-start | bytes 393220
  150.7 2.2 %copy-start = (f32[128,1024]{1,0:T(8,128)S(1)}, f32[128,1024]{1,0:T(8,128)}, u32[]{:S(2)}) copy-start(f32[128,1024]{1,0:T(8,128)} %get-tuple-element.123) | copy-start | bytes 1572868

commit v2 on v1

--- a/solution.py
+++ b/solution.py
@@ -536,20 +536,26 @@
         mail.post(self.shard, mine, s + 2, at.pn)
         mine[...] = self.shard[...]
 
-    def relay(self):
+    def relay_y(self):
         at, mail, s = self.at, self.mail, self.base
         mail.arrived(self.block(2), s + 1, at.yn)
         mail.post(self.block(2, 0), self.block(2, 0), s + 3, at.xn)
+        mail.post(self.block(2), self.block(2), s + 5, at.pn)
+
+    def relay_x(self):
+        at, mail, s = self.at, self.mail, self.base
         mail.arrived(self.block(4), s, at.xn)
         mail.post(self.block(4, 1), self.block(4, 1), s + 4, at.yn)
-        mail.post(self.block(2), self.block(2), s + 5, at.pn)
         mail.post(self.block(4), self.block(4), s + 6, at.pn)
 
-    def finish(self):
+    def far(self):
         at, mail, s = self.at, self.mail, self.base
         mail.arrived(self.block(6, 0), s + 3, at.xn)
         mail.arrived(self.block(6, 1), s + 4, at.yn)
         mail.post(self.block(6), self.block(6), s + 7, at.pn)
+
+    def finish(self):
+        at, mail, s = self.at, self.mail, self.base
         mail.arrived(self.block(1), s + 2, at.pn)
         mail.arrived(self.block(3), s + 5, at.pn)
         mail.arrived(self.block(5), s + 6, at.pn)
@@ -557,14 +563,18 @@
 
 
 class LineGather:
-    def __init__(self, at, mail, held):
+    def __init__(self, at, mail, held, first=0, count=None):
         self.at, self.mail, self.held = at, mail, held
+        self.rows = pl.ds(first, held.shape[1] - first if count is None else count)
         self.up, self.down = mail.slots(at.planes), mail.slots(at.planes)
+
+    def part(self, slot):
+        return self.held.at[slot, self.rows]
 
     def pass_on(self, slot, src=None):
         at = self.at
-        part = self.held.at[slot]
-        src = part if src is None else src
+        part = self.part(slot)
+        src = part if src is None else src.at[self.rows]
 
         @pl.when((slot <= at.b) & (at.b < at.planes - 1))
         def _():
@@ -583,19 +593,19 @@
         @pl.when(at.b >= distance)
         def _():
             slot = at.b - distance
-            self.mail.arrived(self.held.at[slot], self.up + slot, at.along(-1))
+            self.mail.arrived(self.part(slot), self.up + slot, at.along(-1))
             self.pass_on(slot)
 
         @pl.when(at.b + distance < at.planes)
         def _():
             slot = at.b + distance
-            self.mail.arrived(self.held.at[slot], self.down + slot, at.along(1))
+            self.mail.arrived(self.part(slot), self.down + slot, at.along(1))
             self.pass_on(slot)
 
     def close(self):
         at = self.at
         for slot in range(at.planes):
-            part = self.held.at[slot]
+            part = self.part(slot)
 
             @pl.when((slot <= at.b) & (at.b < at.planes - 1))
             def _():
@@ -700,22 +710,20 @@
         self.above, self.below = above, below
         self.up, self.down = mail.slots(at.planes), mail.slots(at.planes)
 
-    def edges(self):
+    def edge(self, slot):
         at, last = self.at, self.at.planes - 1
 
-        @pl.when(at.b == 0)
+        @pl.when((at.b == 0) & (slot > 0))
         def _():
-            for slot in range(last, 0, -1):
-                self.mail.copy(
-                    self.terms.at[slot], self.below.at[slot], self.up + slot, at.along(1)
-                ).start()
-
-        @pl.when(at.b == last)
+            self.mail.copy(
+                self.terms.at[slot], self.below.at[slot], self.up + slot, at.along(1)
+            ).start()
+
+        @pl.when((at.b == last) & (slot < last))
         def _():
-            for slot in range(last):
-                self.mail.copy(
-                    self.terms.at[slot], self.above.at[slot], self.down + slot, at.along(-1)
-                ).start()
+            self.mail.copy(
+                self.terms.at[slot], self.above.at[slot], self.down + slot, at.along(-1)
+            ).start()
 
     def hop(self, hop, rank):
         last = self.at.planes - 1
@@ -812,10 +820,11 @@
 class Layer:
     def __init__(self, refs):
         self.__dict__.update(refs)
-        self.seqs, self.length, self.width = self.xa.shape
-        self.per_seq = self.length // TILE
-        self.tiles = self.seqs * self.per_seq
         self.heads = LANES // HD
+        if "xa" in refs:
+            self.seqs, self.length, self.width = self.xa.shape
+            self.per_seq = self.length // TILE
+            self.tiles = self.seqs * self.per_seq
 
     def rows(self, tile):
         return pl.ds(pl.multiple_of(tile * TILE, TILE), TILE)
@@ -961,13 +970,10 @@
     def cot_flat(self):
         return self.ca[...].reshape(self.seqs * self.length, self.width)
 
-    def qkv_weight_grad(self):
-        def step(i):
-            rows = self.gq.shape[1]
-            act = self.act_one[:, pl.ds(pl.multiple_of(i * rows, rows), rows)]
-            self.gq[i] = dot_tn(act, self.qkv_grad[...]).astype(jnp.bfloat16)
-
-        self.loop(self.gq.shape[0], step)
+    def qkv_weight_grad(self, i):
+        rows = self.gq.shape[1]
+        act = self.act_one[:, pl.ds(pl.multiple_of(i * rows, rows), rows)]
+        self.gq[i] = dot_tn(act, self.qkv_grad[...]).astype(jnp.bfloat16)
 
     def dense_weight_grad(self):
         self.go[...] = (
@@ -986,13 +992,10 @@
 
         self.loop(self.tiles, step)
 
-    def down_weight_grad(self):
-        def step(i):
-            depth = self.gd.shape[1]
-            part = self.gelu[:, pl.ds(pl.multiple_of(i * depth, depth), depth)]
-            self.gd[i] = dot_tn(part, self.cot_flat()).astype(jnp.bfloat16)
-
-        self.loop(self.gd.shape[0], step)
+    def down_weight_grad(self, i):
+        depth = self.gd.shape[1]
+        part = self.gelu[:, pl.ds(pl.multiple_of(i * depth, depth), depth)]
+        self.gd[i] = dot_tn(part, self.cot_flat()).astype(jnp.bfloat16)
 
     def hidden_grad(self):
         def step(i):
@@ -1004,13 +1007,10 @@
 
         self.loop(self.tiles, step)
 
-    def up_weight_grad(self):
-        def step(i):
-            rows = self.gu.shape[1]
-            act = self.act_two[:, pl.ds(pl.multiple_of(i * rows, rows), rows)]
-            self.gu[i] = dot_tn(act, self.pre_grad[...]).astype(jnp.bfloat16)
-
-        self.loop(self.gu.shape[0], step)
+    def up_weight_grad(self, i):
+        rows = self.gu.shape[1]
+        act = self.act_two[:, pl.ds(pl.multiple_of(i * rows, rows), rows)]
+        self.gu[i] = dot_tn(act, self.pre_grad[...]).astype(jnp.bfloat16)
 
     def put_terms(self, terms, i, value):
         seq, chips, cores, rows, width = terms.shape
@@ -1080,7 +1080,7 @@
         )
 
 
-LAYER_SLOTS = 4 * 8 + 10 * 8 + 7 * 8 + 2
+LAYER_SLOTS = 4 * 8 + 11 * 8 + 7 * 8 + 2
 
 
 def layer_kernel(names, planes, *refs):
@@ -1108,7 +1108,9 @@
     gather_c = PlaneGather(at, mail, do.cot_own, do.ca)
     line_v, line_o = LineGather(at, mail, do.va), LineGather(at, mail, do.wo)
     line_q, line_u = LineGather(at, mail, do.wq), LineGather(at, mail, do.wu)
-    line_d = LineGather(at, mail, do.wd)
+    half = do.wd.shape[1] // 2
+    line_da = LineGather(at, mail, do.wd, 0, half)
+    line_db = LineGather(at, mail, do.wd, half, half)
     ex_v = PlaneExchange(at, mail, lambda rank: do.vec_s.at[rank], lambda rank: do.vec_in.at[rank])
     ex_q = PlaneExchange(at, mail, lambda rank: do.wq_s.at[rank], strip(do.wq))
     ex_u = PlaneExchange(at, mail, lambda rank: do.wu_s.at[rank], strip(do.wu))
@@ -1135,107 +1137,199 @@
     plane_o = PlaneReduce(at, mail, do.po, do.pairs_o, do.sums_o, do.side_o)
     plane_g = PlaneReduce(at, mail, do.pg, do.pairs_g, do.sums_g, do.side_g)
 
+    slots = [s + b // pair * (planes - 1 - 2 * s) for s in (3, 0, 2, 1)]
+
     at.barrier()
+    line_da.start(do.wd_s)
+    do.wd[b] = do.wd_s[...]
     ex_v.start()
     ex_q.start()
     gather_x.start()
     line_o.start(do.wo_s)
     do.wo[b] = do.wo_s[...]
-    ex_u.start()
-    gather_c.start()
-    do.wd[b] = do.wd_s[...]
     ex_v.finish()
     do.va[b] = jnp.sum(do.vec_in[...], axis=0)
     line_v.start()
+    line_db.start(do.wd_s)
+    line_v.take(1)
+    ex_u.start()
     ex_q.finish()
     line_q.start()
-    gather_x.relay()
-    line_v.take(1)
     line_o.take(1)
+    gather_x.relay_y()
+    line_q.take(1)
+    gather_x.relay_x()
+    gather_c.start()
+    line_o.take(2)
+    line_v.take(2)
+    gather_x.far()
+    line_v.take(3)
+    line_q.take(2)
     gather_x.finish()
-    line_q.take(1)
+    line_o.take(3)
     do.statistics()
-    line_v.take(2)
-    line_o.take(2)
-    line_q.take(2)
-    gather_c.relay()
+    line_da.take(1)
+    do.activations()
+    gather_c.relay_y()
+    gather_c.relay_x()
     ex_u.finish()
-    line_v.take(3)
-    do.activations()
-    line_o.take(3)
-    line_q.take(3)
     line_u.start()
-    line_d.start(do.wd_s)
     swap_w.start()
     mine[...] = do.wo[pl.ds(pair * c, pair)]
+    line_q.take(3)
     do.project()
+    swap_w.finish()
+    gather_c.far()
+    line_da.take(2)
+    do.attend()
     gather_c.finish()
-    do.attend()
-    line_u.take(1)
-    swap_w.finish()
-    do.attend_out_grad()
-    line_d.take(1)
-    do.attend_grads()
-    line_u.take(2)
     do.dense_weight_grad()
     swap_g.start()
     do.go4[pl.ds(pair * c, pair)] = do.go[:, c]
-    do.qkv_weight_grad()
-    sum_q.edges()
+    do.attend_out_grad()
     swap_g.finish()
-    sum_o.edges()
-    line_d.take(2)
+    for slot in slots:
+        sum_o.edge(slot)
+    line_u.take(1)
+    do.attend_grads()
+    do.qkv_weight_grad(slots[0])
+    sum_q.edge(slots[0])
+    do.qkv_weight_grad(slots[1])
+    sum_q.edge(slots[1])
+    do.qkv_weight_grad(slots[2])
+    sum_q.edge(slots[2])
+    do.qkv_weight_grad(slots[3])
+    sum_q.edge(slots[3])
+    line_u.take(2)
+    line_da.take(3)
     line_u.take(3)
     do.expand()
+    do.down_weight_grad(slots[0])
+    sum_d.edge(slots[0])
+    line_db.take(1)
+    sum_o.hop(1, 0)
     sum_q.hop(1, 0)
-    sum_o.hop(1, 0)
-    do.down_weight_grad()
-    sum_d.edges()
+    line_db.take(2)
+    line_db.take(3)
+    do.hidden_grad()
+    do.up_weight_grad(slots[0])
+    sum_u.edge(slots[0])
     sum_q.hop(1, 1)
-    sum_o.hop(1, 1)
+    do.in_terms()
+    plane_g.start()
     sum_q.hop(2, 0)
-    sum_o.hop(2, 0)
-    line_d.take(3)
-    do.hidden_grad()
-    sum_d.hop(1, 0)
-    do.up_weight_grad()
-    sum_u.edges()
-    sum_d.hop(1, 1)
+    do.up_weight_grad(slots[1])
+    sum_u.edge(slots[1])
+    do.up_weight_grad(slots[2])
+    sum_u.edge(slots[2])
+    sum_q.finish(do.fq)
+    back_q.start()
     do.out_terms()
     plane_o.start()
-    sum_d.hop(2, 0)
-    sum_q.finish(do.fq)
-    back_q.start()
-    do.in_terms()
-    plane_g.start()
+    plane_g.fold()
+    sum_o.hop(2, 0)
+    sum_o.hop(1, 1)
+    do.up_weight_grad(slots[3])
+    sum_u.edge(slots[3])
+    sum_u.hop(1, 0)
+    do.down_weight_grad(slots[1])
+    sum_d.edge(slots[1])
     do.small_terms()
     fold_v.start()
     plane_o.fold()
-    sum_u.hop(1, 0)
-    plane_g.fold()
+    plane_g.turn()
+    sum_o.finish(do.dd_o)
     fold_v.finish()
     do.small_plane(b)
     line_s.start()
+    do.down_weight_grad(slots[2])
+    sum_d.edge(slots[2])
+    do.down_weight_grad(slots[3])
+    sum_d.edge(slots[3])
+    sum_d.hop(1, 0)
     plane_o.turn()
-    plane_g.turn()
+    sum_u.hop(2, 0)
+    line_s.take(1)
     sum_u.hop(1, 1)
-    line_s.take(1)
     line_s.take(2)
-    sum_u.hop(2, 0)
+    back_q.finish()
     line_s.take(3)
+    sum_d.hop(1, 1)
     do.vt[...] = jnp.sum(do.vz[...], axis=0)
     share_v.start()
-    do.result(plane_o.finish(), plane_g.finish(), do.out, do.in_grad)
-    sum_o.finish(do.dd_o)
-    sum_d.finish(do.dd)
+    sum_d.hop(2, 0)
     sum_u.finish(do.fu)
     back_u.start()
-    back_q.finish()
+    do.result(plane_o.finish(), plane_g.finish(), do.out, do.in_grad)
     share_v.finish()
+    sum_d.finish(do.dd)
     back_u.finish()
     mail.close()
-    for line in (line_v, line_o, line_q, line_u, line_d, line_s, sum_o, sum_q, sum_u, sum_d):
+    for line in (line_v, line_o, line_q, line_u, line_da, line_db, line_s, sum_o, sum_q, sum_u, sum_d):
         line.close()
+
+
+def finish_kernel(names, planes, *refs):
+    do = Layer(dict(zip(names, refs)))
+    at = Place(planes)
+    ranks, rows = do.dq.shape[:2]
+    lane = lax.broadcasted_iota(jnp.int32, (rows, LANES), 1)
+    low = lane < HD
+    for part in range(3):
+        for core in range(2):
+            for pair in range(ranks // 4):
+                near, far = (
+                    do.dq[2 * (2 * pair + i) + core, :, part * LANES : (part + 1) * LANES].astype(
+                        jnp.float32
+                    )
+                    for i in range(2)
+                )
+                for j in range(2):
+                    both = (
+                        jnp.where(low, near, pltpu.roll(far, HD, 1))
+                        if j == 0
+                        else jnp.where(low, pltpu.roll(near, HD, 1), far)
+                    )
+                    first = (part * 4 + core * 2 + j) * ranks // 2 * HD + pair * LANES
+                    do.qkv_out[:, first : first + LANES] = both
+    for rank in range(ranks):
+        for b in range(planes):
+            first = (b * ranks + rank) * LANES
+            do.up_out[:, first : first + LANES] = do.du[
+                rank, :, b * LANES : (b + 1) * LANES
+            ].astype(jnp.float32)
+    do.down_out[...] = do.dd[...]
+    do.dense_out[...] = do.dd_o[...]
+    for seq in range(do.out.shape[0]):
+        do.in_grad_out[:, seq, :] = do.in_grad[seq]
+        do.out_out[:, seq, :] = do.out[seq]
+    piece = lax.rem(at.t, 4)
+    row = (at.b * ranks + at.t) // 4
+    values = do.dv[pl.ds(row, 1), 0:8, :].reshape(8, LANES)
+    front = jnp.zeros((8, rows), jnp.float32)
+    for i in range(4):
+        cut = values[:, i * rows : (i + 1) * rows]
+        front = front + jnp.where(piece == i, cut, jnp.zeros_like(cut))
+    for j, ref in enumerate(
+        (do.dense_bias, do.gain_one, do.shift_one, do.gain_two, do.shift_two)
+    ):
+        ref[...] = front[j].reshape(rows)
+    do.down_bias[...] = front[0].reshape(rows)
+    do.up_bias[...] = do.dv[pl.ds(at.t, 1), pl.ds(12 + at.b, 1), :].reshape(LANES)
+    pieces = []
+    for i in range(3):
+        index = (at.b * ranks + at.t) * 3 + i
+        part, inner = index // 32, lax.rem(index, 32)
+        head, half = inner // 2, lax.rem(inner, 2)
+        core, j, chip = head // 8, lax.rem(head // 4, 2), lax.rem(head, 4)
+        value = do.dv[pl.ds(chip * 2 + core, 1), pl.ds(8 + part, 1), :].reshape(1, LANES)
+        spot = 2 * j + half
+        total = jnp.zeros((1, rows), jnp.float32)
+        for k in range(4):
+            cut = value[:, k * rows : (k + 1) * rows]
+            total = total + jnp.where(spot == k, cut, jnp.zeros_like(cut))
+        pieces.append(total)
+    do.qkv_bias[...] = jnp.concatenate(pieces, axis=1).reshape(3 * rows)
 
 
 VMEM = pl.BlockSpec(memory_space=pltpu.VMEM)
@@ -1426,42 +1520,29 @@
         ),
     )(*inputs.values())
 
-    output = jnp.transpose(out, (1, 0, 2))
-    input_grad = jnp.transpose(in_grad, (1, 0, 2))
-    qkv_grad_out = jnp.transpose(
-        dq.reshape(ranks // 2, 2, rows, 3, pair, HD), (2, 3, 1, 4, 0, 5)
-    ).reshape(qkv_weight.shape).astype(single)
-    up_grad_out = jnp.transpose(
-        du.reshape(ranks, rows, planes, depth), (1, 2, 0, 3)
-    ).reshape(up_weight.shape).astype(single)
-    wide = [
-        lax.dynamic_slice(dv[:, j].reshape(width), (owner * rows,), (rows,)) for j in range(5)
-    ]
-    qkv_bias_grad = lax.dynamic_slice(
-        jnp.transpose(
-            dv[:, 8:11].reshape(ranks // 2, 2, 3, pair, HD), (2, 1, 3, 0, 4)
-        ).reshape(3 * width),
-        (owner * qkv_bias.shape[0],),
-        qkv_bias.shape,
-    )
-    up_bias_grad = lax.dynamic_slice(
-        dv, (rank, 12 + lax.axis_index(BATCH), 0), (1, 1, LANES)
-    ).reshape(up_bias.shape)
-    return (
-        output,
-        input_grad,
-        qkv_grad_out,
-        qkv_bias_grad,
-        dd_o,
-        wide[0],
-        wide[1],
-        wide[2],
-        wide[3],
-        wide[4],
-        up_grad_out,
-        up_bias_grad,
-        dd,
-        wide[0],
+    results = dict(
+        out_out=(residual_in.shape, half_type),
+        in_grad_out=(residual_in.shape, single),
+        qkv_out=(qkv_weight.shape, single),
+        qkv_bias=(qkv_bias.shape, single),
+        dense_out=(dense_weight.shape, single),
+        dense_bias=(dense_bias.shape, single),
+        gain_one=(norm1_gain.shape, single),
+        shift_one=(norm1_bias.shape, single),
+        gain_two=(norm2_gain.shape, single),
+        shift_two=(norm2_bias.shape, single),
+        up_out=(up_weight.shape, single),
+        up_bias=(up_bias.shape, single),
+        down_out=(down_weight.shape, single),
+        down_bias=(down_bias.shape, single),
+    )
+    return tuple(
+        pl.pallas_call(
+            functools.partial(finish_kernel, tuple(outputs) + tuple(results), planes),
+            out_shape=[jax.ShapeDtypeStruct(*what) for what in results.values()],
+            in_specs=[VMEM] * len(outputs),
+            out_specs=[VMEM] * len(results),
+        )(out, in_grad, dq, du, dd, dd_o, dv)
     )
 
 

time: 154 us -> 112 us (0.73)
  Pallas kernels: 131 us -> 103 us
  local copies, waits for them, and re-layouts: 21.1 us -> 7.02 us
    pallas_call x1, Pallas kernels: 131 us -> 100 us  [fast_body(): pl.pallas_call(functools.partial(layer_kernel, names, planes), out_shape=...]
    unnamed x45 -> x25, local copies, waits for them, and re-layouts: 5.91 us -> 0.85 us
    pallas_call x0 -> x1, Pallas kernels: none -> 3.18 us  [fast_body(): pl.pallas_call(functools.partial(finish_kernel, tuple(outputs) + tuple(re...]
    dynamic_slice x6 -> x0, local copies, waits for them, and re-layouts: 2.99 us -> none  [the longest x5 2.41 us: fast_body(): lax.dynamic_slice(dv[:, j].reshape(width), (owner * rows,), (rows,))]
    convert_element_type x5 -> x0, local copies, waits for them, and re-layouts: 2.83 us -> none  [the longest x3 2.36 us: fast_body(): qkv_grad_out = jnp.transpose(dq.reshape(ranks // 2, 2, rows, 3, pair, HD)...]
    slice x3 -> x0, local copies, waits for them, and re-layouts: 1.83 us -> none  [the longest x1 1.03 us: fast_body(): dv[:, j].reshape(width)]
where the time goes in v2:
time: 112 us; the launch traced here: 111 us
  Pallas kernels  103 us (92%)
  local copies, waits for them, and re-layouts  7.02 us (6%)
    pallas_call x1, Pallas kernels, fast_body(): pl.pallas_call(functools.partial(layer_kernel, names, planes), out_shape=...  100 us
    pallas_call x1, Pallas kernels, fast_body(): pl.pallas_call(functools.partial(finish_kernel, tuple(outputs) + tuple(re...  3.18 us

profile of v2, /device:TPU:0, one launch (start us, length us, event | category | flops | bytes accessed | tf_op | source)
XLA Modules:
  0.0 111.4 jit_solution(9585493286763395571)
XLA Ops:
  0.7 0.0 copy-start.10
  0.7 0.0 copy-start.11
  0.7 0.0 copy-start.4
  0.7 0.0 copy-start.5
  0.7 0.0 copy-start.6
  0.7 0.0 copy-start.7
  0.7 0.0 copy-start.8
  0.7 0.0 copy-start.9
  0.7 0.6 copy-done.10
  1.3 0.0 copy-start
  1.3 0.0 copy-done.11
  1.4 0.0 copy-done.4
  1.4 0.1 mul.160
  1.5 0.0 copy-done.5
  1.5 0.1 mul.164
  1.5 0.0 copy-done.6
  1.6 0.1 mul.168
  1.6 0.0 copy-done.7
  1.6 0.1 mul.172
  1.7 0.0 copy-done.8
  1.7 0.1 mul.176
  1.8 0.0 copy-done.9
  1.8 0.1 mul.180
  1.9 0.1 mul.157
  2.0 0.1 mul.158
  2.2 0.1 broadcast_multiply_fusion
  2.3 0.1 broadcast_multiply_fusion.1
  2.3 0.1 mul.187
  2.4 0.1 reshape.220
  2.5 1.9 %concatenate.3.refs_6_ = f32[8,24,128]{2,1,0:T(8,128)} concatenate(f32[8,2,128]{2,1,0:T(2,128)S(1)} %broadcast_in_dim.16, f32[8,2,128]{2,1,0:T(2,128)S(1)} %broadcast_in_dim.17, f32[8,2,128]{2,1,0:T(2,128)S(1)} %broadcast_in_dim.18, f32[8,2,128]{2,1,0:T(2,128)S(1)} %broadcast_in_dim.19, f32[8,2,128]{2,1,0:T(2,128)S(1)} %broadcast_in_dim.20, f32[8,2,128]{2,1,0:T(2,128)S(1)} %broadcast_in_dim.21, ...), dimensions={1} | concatenate | bytes 196608 | tf_op jit(solution)/shard_map/concatenate | solution.py:1419
  4.5 0.0 copy-done
  4.5 0.1 copy.47
  4.6 0.0 copy-start.3
  4.6 0.8 reshape.218.refs_3_
  5.4 0.1 copy-done.3
  5.6 0.3 reshape.215
  5.8 0.3 copy.46
  6.2 0.0 copy-start.1
  6.2 0.0 copy-start.2
  6.2 0.9 reshape.216.refs_2_
  7.1 0.0 copy-done.1
  7.1 0.1 copy-done.2
  7.2 0.9 copy_bitcast_fusion.2
  8.1 100.0 %shard_map.254 = (bf16[2,64,1024]{2,1,0:T(8,128)(2,1)}, f32[2,64,1024]{2,1,0:T(8,128)}, bf16[8,32,384]{2,1,0:T(8,128)(2,1)}, bf16[8,32,512]{2,1,0:T(8,128)(2,1)}...) custom-call(bf16[2,64,1024]{2,1,0:T(8,128)(2,1)} %get-tuple-element.35.refs_0_, ...), custom_call_target="tpu_custom_call" | custom-call | tf_op jit(solution)/shard_map/pallas_call | solution.py:1511
  108.1 3.2 %shard_map.255 = (bf16[64,2,1024]{2,1,0:T(2,128)(2,1)}, f32[64,2,1024]{2,1,0:T(2,128)}, f32[32,3072]{1,0:T(8,128)}, f32[96]{0:T(128)}, f32[32,1024]{1,0:T(8,128)...) custom-call(bf16[2,64,1024]{2,1,0:T(8,128)(2,1)} %get-tuple-element., ...), custom_call_target="tpu_custom_call" | custom-call | tf_op jit(solution)/shard_map/pallas_call | solution.py:1540
  (22 shorter events, 0.1 us)
Async XLA Ops:
  0.7 0.7 copy-start.10
  0.7 0.7 copy-start.11
  0.7 0.7 copy-start.4
  0.7 0.8 copy-start.5
  0.7 0.9 copy-start.6
  0.7 0.9 copy-start.7
  0.7 1.0 copy-start.8
  0.7 1.1 copy-start.9
  1.3 3.2 %copy-start = (bf16[32,4096]{1,0:T(8,128)(2,1)S(1)}, bf16[32,4096]{1,0:T(8,128)(2,1)}, u32[]{:S(2)}) copy-start(bf16[32,4096]{1,0:T(8,128)(2,1)} %param.24) | copy-start | bytes 786436
  4.6 0.9 copy-start.3
  6.2 1.0 copy-start.1
  6.2 1.0 copy-start.2

commit v3 on v2

--- a/solution.py
+++ b/solution.py
@@ -470,22 +470,29 @@
         for d in range(1, 8):
             pl.semaphore_signal(sem, inc=1, device_id=self.peer(d), device_id_type=MESH)
 
-        @pl.when(self.b > 0)
-        def _():
-            pl.semaphore_signal(sem, inc=1, device_id=self.along(-1), device_id_type=MESH)
-
-        @pl.when(self.b < self.planes - 1)
-        def _():
-            pl.semaphore_signal(sem, inc=1, device_id=self.along(1), device_id_type=MESH)
-
-        below = (self.b > 0).astype(jnp.int32)
-        above = (self.b < self.planes - 1).astype(jnp.int32)
-        pl.semaphore_wait(sem, 7 + below + above)
+        for step in range(1, self.planes):
+
+            @pl.when(self.b >= step)
+            def _():
+                pl.semaphore_signal(sem, inc=1, device_id=self.along(-step), device_id_type=MESH)
+
+            @pl.when(self.b + step < self.planes)
+            def _():
+                pl.semaphore_signal(sem, inc=1, device_id=self.along(step), device_id_type=MESH)
+
+        pl.semaphore_wait(sem, 7 + self.planes - 1)
 
 
 class Mail:
-    def __init__(self, send, recv):
+    def __init__(self, send, recv, near):
         self.send, self.recv, self.used, self.open = send, recv, 0, []
+        self.near, self.near_used = near, 0
+
+    def bring(self, src, dst):
+        made = pltpu.make_async_copy(src, dst, self.near.at[self.near_used])
+        self.near_used += 1
+        made.start()
+        return made
 
     def slots(self, n):
         first = self.used
@@ -519,33 +526,42 @@
     def __init__(self, at, mail, shard, whole):
         self.at, self.mail, self.shard, self.whole = at, mail, shard, whole
         self.rows = shard.shape[1]
-        self.base = mail.slots(8)
+        self.halves = shard.shape[0] // 2
+        self.base = mail.slots(10)
+
+    def half(self, i):
+        return self.shard.at[pl.ds(i * self.halves, self.halves)]
 
     def block(self, d, half=None):
         rows = pl.ds(pl.multiple_of(self.at.rank(d) * self.rows, self.rows), self.rows)
-        halves = self.shard.shape[0] // 2
         if half is None:
             return self.whole.at[:, rows, :]
-        return self.whole.at[pl.ds(half * halves, halves), rows, :]
+        return self.whole.at[pl.ds(half * self.halves, self.halves), rows, :]
 
     def start(self):
         at, mail, s = self.at, self.mail, self.base
-        mine = self.block(0)
-        mail.post(self.shard, mine, s, at.xn)
-        mail.post(self.shard, mine, s + 1, at.yn)
-        mail.post(self.shard, mine, s + 2, at.pn)
-        mine[...] = self.shard[...]
+        mail.post(self.half(1), self.block(0, 1), s, at.xn)
+        mail.post(self.half(0), self.block(0, 0), s + 1, at.yn)
+        mail.post(self.half(0), self.block(0, 0), s + 8, at.xn)
+        mail.post(self.half(1), self.block(0, 1), s + 9, at.yn)
+        mail.post(self.shard, self.block(0), s + 2, at.pn)
+        self.own = mail.bring(self.shard, self.block(0))
 
     def relay_y(self):
         at, mail, s = self.at, self.mail, self.base
-        mail.arrived(self.block(2), s + 1, at.yn)
+        mail.arrived(self.block(2, 0), s + 1, at.yn)
         mail.post(self.block(2, 0), self.block(2, 0), s + 3, at.xn)
-        mail.post(self.block(2), self.block(2), s + 5, at.pn)
 
     def relay_x(self):
         at, mail, s = self.at, self.mail, self.base
-        mail.arrived(self.block(4), s, at.xn)
+        mail.arrived(self.block(4, 1), s, at.xn)
         mail.post(self.block(4, 1), self.block(4, 1), s + 4, at.yn)
+
+    def share(self):
+        at, mail, s = self.at, self.mail, self.base
+        mail.arrived(self.block(2, 1), s + 9, at.yn)
+        mail.post(self.block(2), self.block(2), s + 5, at.pn)
+        mail.arrived(self.block(4, 0), s + 8, at.xn)
         mail.post(self.block(4), self.block(4), s + 6, at.pn)
 
     def far(self):
@@ -560,6 +576,7 @@
         mail.arrived(self.block(3), s + 5, at.pn)
         mail.arrived(self.block(5), s + 6, at.pn)
         mail.arrived(self.block(7), s + 7, at.pn)
+        self.own.wait()
 
 
 class LineGather:
@@ -616,23 +633,76 @@
                 self.mail.copy(part, part, self.down + slot, at.along(-1)).wait_send()
 
 
+class StarGather:
+    def __init__(self, at, mail, held):
+        self.at, self.mail, self.held = at, mail, held
+        self.base = mail.slots(2 * at.planes)
+
+    def each(self, action):
+        at = self.at
+        for step in range(1, at.planes):
+
+            @pl.when(at.b + step < at.planes)
+            def _():
+                action(step, self.base + step)
+
+            @pl.when(at.b >= step)
+            def _():
+                action(-step, self.base + at.planes + step)
+
+    def start(self):
+        part = self.held.at[self.at.b]
+        self.each(
+            lambda step, slot: self.mail.copy(part, part, slot, self.at.along(step)).start()
+        )
+
+    def finish(self):
+        n = self.at.planes
+        for step in range(1, n):
+
+            @pl.when(self.at.b + step < n)
+            def _():
+                part = self.held.at[self.at.b + step]
+                self.mail.arrived(part, self.base + n + step, self.at.along(step))
+
+            @pl.when(self.at.b >= step)
+            def _():
+                part = self.held.at[self.at.b - step]
+                self.mail.arrived(part, self.base + step, self.at.along(-step))
+
+    def close(self):
+        part = self.held.at[self.at.b]
+        self.each(
+            lambda step, slot: self.mail.copy(part, part, slot, self.at.along(step)).wait_send()
+        )
+
+
 class PlaneExchange:
-    def __init__(self, at, mail, piece, landing):
-        self.at, self.mail, self.piece, self.landing = at, mail, piece, landing
-        self.base = mail.slots(8)
+    def __init__(self, at, mail, pieces, landings, parts=1):
+        self.at, self.mail, self.parts = at, mail, parts
+        self.pieces = (lambda rank: [pieces(rank)]) if parts == 1 else pieces
+        self.landings = (lambda rank: [landings(rank)]) if parts == 1 else landings
+        self.base = mail.slots(8 * parts)
 
     def start(self):
-        at = self.at
+        at, n = self.at, self.parts
         for d in range(1, 8):
-            self.mail.post(
-                self.piece(at.rank(d)), self.landing(at.t), self.base + d, at.peer(d)
-            )
-        self.landing(at.t)[...] = self.piece(at.t)[...]
+            for i, (piece, landing) in enumerate(
+                zip(self.pieces(at.rank(d)), self.landings(at.t))
+            ):
+                self.mail.post(piece, landing, self.base + d * n + i, at.peer(d))
+        self.own = [
+            self.mail.bring(piece, landing)
+            for piece, landing in zip(self.pieces(at.t), self.landings(at.t))
+        ]
 
     def finish(self):
-        at = self.at
+        at, n = self.at, self.parts
         for d in range(1, 8):
-            self.mail.arrived(self.landing(at.rank(d)), self.base + d, at.peer(d))
+            for i, landing in enumerate(self.landings(at.rank(d))):
+                self.mail.arrived(landing, self.base + d * n + i, at.peer(d))
+        for own in self.own:
+            own.wait()
 
 
 class PairExchange:
@@ -846,6 +916,47 @@
             [self.va[b, pl.ds(2 * row + a, 1), :] for b in range(planes) for a in range(2)], axis=1
         )
 
+    def own_vectors(self, rank):
+        lane = lax.broadcasted_iota(jnp.int32, (2, LANES), 1)
+        row = lax.broadcasted_iota(jnp.int32, (2, LANES), 0)
+        for j, ref in enumerate(self.vectors):
+            piece = ref[...].astype(jnp.float32).reshape(1, ref.shape[0])
+            piece = jnp.concatenate([piece] * (LANES // ref.shape[0]), axis=1)
+            here = (lane // ref.shape[0] == rank % 4) & (row == rank // 4)
+            self.vec_s[2 * j : 2 * j + 2, :] = jnp.where(here, jnp.broadcast_to(piece, here.shape), 0.0)
+        bias = self.b_qkv[...].astype(jnp.float32).reshape(1, self.b_qkv.shape[0])
+        self.vec_s[12:13, :] = jnp.concatenate(
+            [bias, jnp.zeros((1, LANES - bias.shape[1]), jnp.float32)], axis=1
+        )
+        self.vec_s[13:14, :] = self.b_up[...].astype(jnp.float32).reshape(1, LANES)
+
+    def plane_vectors(self, slot):
+        total = jnp.sum(self.vec_in[...], axis=0)
+        self.va[slot, 0:16, :] = total
+        for rank in range(self.vec_in.shape[0]):
+            self.va[slot, 16 + rank : 17 + rank, :] = self.vec_in[rank, 12:13, :]
+            self.va[slot, 24 + rank : 25 + rank, :] = self.vec_in[rank, 13:14, :]
+
+    def sort_weight(self):
+        rows = self.wq_raw.shape[0]
+        low = lax.broadcasted_iota(jnp.int32, (rows, LANES), 1) < HD
+        for part in range(3):
+            for core in range(2):
+                for pair in range(2):
+                    first, second = (
+                        self.wq_raw[
+                            :, pl.ds(part * self.width + (core * 2 + j) * 4 * HD + pair * LANES, LANES)
+                        ].astype(jnp.float32)
+                        for j in range(2)
+                    )
+                    cut = slice(part * LANES, (part + 1) * LANES)
+                    self.wq_s[4 * pair + core, :, cut] = jnp.where(
+                        low, first, pltpu.roll(second, HD, 1)
+                    ).astype(jnp.bfloat16)
+                    self.wq_s[4 * pair + 2 + core, :, cut] = jnp.where(
+                        low, pltpu.roll(first, HD, 1), second
+                    ).astype(jnp.bfloat16)
+
     def statistics(self):
         def step(i):
             x = self.in_seq(self.xa, i).astype(jnp.float32)
@@ -871,12 +982,32 @@
 
         self.loop(self.tiles, step)
 
-    def bias(self, first, count):
-        rows = sum(self.va[b, pl.ds(first, count), :] for b in range(self.va.shape[0]))
-        return jnp.concatenate([rows[i : i + 1] for i in range(count)], axis=1)
-
-    def project(self):
-        bias = self.bias(12, 3)
+    def qkv_bias(self, rank):
+        size = HD // 2
+        held = self.b_qkv.shape[0] // size
+        ranks = self.vec_in.shape[0]
+        pieces = []
+        for i in range(3 * LANES // size):
+            part, j, half = i // 4, i // 2 % 2, i % 2
+            head = (rank % 2 * 2 + j) * 4 + rank // 2
+            index = part * (self.width // size) + head * 2 + half
+            owner, spot = index // held, index % held
+            row = self.va[owner // ranks, pl.ds(16 + owner % ranks, 1), :]
+            pieces.append(
+                sum(
+                    jnp.where(spot == k, row[:, k * size : (k + 1) * size], 0.0)
+                    for k in range(held)
+                )
+            )
+        return jnp.concatenate(pieces, axis=1)
+
+    def up_bias(self, rank):
+        return jnp.concatenate(
+            [self.va[b, pl.ds(24 + rank, 1), :] for b in range(self.va.shape[0])], axis=1
+        )
+
+    def project(self, rank):
+        bias = self.qkv_bias(rank)
 
         def step(i):
             weight = self.wq[...].reshape(self.width, 3 * LANES)
@@ -980,8 +1111,8 @@
             dot_tn(self.attn[...], self.cot_flat()).astype(jnp.bfloat16).reshape(self.go.shape)
         )
 
-    def expand(self):
-        bias = self.bias(16, 4)
+    def expand(self, rank):
+        bias = self.up_bias(rank)
 
         def step(i):
             weight = self.wu[...].reshape(self.width, self.hidden)
@@ -1047,13 +1178,17 @@
 
         self.loop(self.tiles, step)
 
-    def small_terms(self):
+    def own_rows(self, ref, rank):
+        rows = self.out.shape[1]
+        return ref[:, pl.ds(pl.multiple_of(rank * rows, rows), rows), :].astype(jnp.float32)
+
+    def small_terms(self, rank):
         ranks = self.sm.shape[0]
-        cot = total_rows(jnp.sum(self.cot_own[...].astype(jnp.float32), axis=0))
-        for rank in range(ranks):
-            cut = slice(rank * LANES, (rank + 1) * LANES)
-            self.sm[rank, 0:1, :] = cot[:, cut]
-            self.sm[rank, 1:5, :] = self.sums[0:4, cut]
+        cot = total_rows(jnp.sum(self.own_rows(self.ca, rank), axis=0))
+        for to in range(ranks):
+            cut = slice(to * LANES, (to + 1) * LANES)
+            self.sm[to, 0:1, :] = cot[:, cut]
+            self.sm[to, 1:5, :] = self.sums[0:4, cut]
 
     def small_plane(self, slot):
         total = jnp.sum(self.sm_in[...], axis=0)
@@ -1065,35 +1200,37 @@
         for j in range(self.hidden // LANES):
             self.vz[slot, 12 + j : 13 + j, :] = pre[:, j * LANES : (j + 1) * LANES]
 
-    def result(self, out_sum, in_sum, out, in_grad):
-        x = self.x_own[...].astype(jnp.float32)
+    def result(self, rank, out_sum, in_sum):
+        x = self.own_rows(self.xa, rank)
         center = jnp.mean(x, axis=2, keepdims=True)
         shifted = x - center
         inverse = lax.rsqrt(jnp.mean(shifted * shifted, axis=2, keepdims=True) + EPSILON)
         normed = shifted * inverse
         bias = (self.wide(0) + self.wide(5))[None]
-        out[...] = (x + out_sum + bias).astype(jnp.bfloat16)
-        in_grad[...] = self.cot_own[...].astype(jnp.float32) + inverse * (
+        self.out[...] = (x + out_sum + bias).astype(jnp.bfloat16)
+        self.in_grad[...] = self.own_rows(self.ca, rank) + inverse * (
             in_sum
             - jnp.mean(in_sum, axis=2, keepdims=True)
             - normed * jnp.mean(in_sum * normed, axis=2, keepdims=True)
         )
 
 
-LAYER_SLOTS = 4 * 8 + 11 * 8 + 7 * 8 + 2
+LAYER_SLOTS = 4 * 8 + 4 + 12 * 8 + 10 * 8 + 2
+NEAR_SLOTS = 24
 
 
 def layer_kernel(names, planes, *refs):
     refs = dict(zip(names, refs))
-    send, recv = refs.pop(names[-2]), refs.pop(names[-1])
+    send, recv, near = (refs.pop(name) for name in names[-3:])
     refs.update(
         tables=tuple(refs["table"].at[i] for i in range(3)),
         probs=tuple(refs[name] for name in names if name.startswith("probs")),
+        vectors=tuple(refs[name] for name in names if name.startswith("vector")),
         hidden=refs["gelu"].shape[1],
     )
     do = Layer(refs)
     at = Place(planes)
-    mail = Mail(send, recv)
+    mail = Mail(send, recv, near)
     b, c = at.b, at.c
     rows = do.wq_s.shape[1]
     pair = planes // 2
@@ -1104,16 +1241,29 @@
     def band(whole):
         return lambda rank: whole.at[pl.ds(pl.multiple_of(rank * rows, rows), rows), :]
 
+    def up_pieces(rank):
+        return [
+            do.wu_s.at[:, pl.ds(pl.multiple_of((p * 8 + rank) * LANES, LANES), LANES)]
+            for p in range(planes)
+        ]
+
+    def up_landings(rank):
+        strip_rows = pl.ds(pl.multiple_of(rank * rows, rows), rows)
+        return [do.wu.at[b, strip_rows, pl.ds(p * LANES, LANES)] for p in range(planes)]
+
     gather_x = PlaneGather(at, mail, do.x_own, do.xa)
     gather_c = PlaneGather(at, mail, do.cot_own, do.ca)
-    line_v, line_o = LineGather(at, mail, do.va), LineGather(at, mail, do.wo)
-    line_q, line_u = LineGather(at, mail, do.wq), LineGather(at, mail, do.wu)
+    line_v, line_o = StarGather(at, mail, do.va), LineGather(at, mail, do.wo)
+    line_q = LineGather(at, mail, do.wq)
+    half = do.wu.shape[1] // 2
+    line_ua = LineGather(at, mail, do.wu, 0, half)
+    line_ub = LineGather(at, mail, do.wu, half, half)
     half = do.wd.shape[1] // 2
     line_da = LineGather(at, mail, do.wd, 0, half)
     line_db = LineGather(at, mail, do.wd, half, half)
-    ex_v = PlaneExchange(at, mail, lambda rank: do.vec_s.at[rank], lambda rank: do.vec_in.at[rank])
+    ex_v = PlaneExchange(at, mail, lambda rank: do.vec_s, lambda rank: do.vec_in.at[rank])
     ex_q = PlaneExchange(at, mail, lambda rank: do.wq_s.at[rank], strip(do.wq))
-    ex_u = PlaneExchange(at, mail, lambda rank: do.wu_s.at[rank], strip(do.wu))
+    ex_u = PlaneExchange(at, mail, up_pieces, up_landings, planes)
     mine = do.wo2.at[:, c]
     swap_w = PairExchange(
         at, mail, do.wo.at[pl.ds(pair * (1 - c), pair)], mine, do.wo2.at[:, 1 - c]
@@ -1132,7 +1282,7 @@
     back_q = PlaneExchange(at, mail, band(do.fq), lambda rank: do.dq.at[rank])
     back_u = PlaneExchange(at, mail, band(do.fu), lambda rank: do.du.at[rank])
     fold_v = PlaneExchange(at, mail, lambda rank: do.sm.at[rank], lambda rank: do.sm_in.at[rank])
-    line_s = LineGather(at, mail, do.vz)
+    line_s = StarGather(at, mail, do.vz)
     share_v = PlaneExchange(at, mail, lambda rank: do.vt, lambda rank: do.dv.at[rank])
     plane_o = PlaneReduce(at, mail, do.po, do.pairs_o, do.sums_o, do.side_o)
     plane_g = PlaneReduce(at, mail, do.pg, do.pairs_g, do.sums_g, do.side_g)
@@ -1140,132 +1290,148 @@
     slots = [s + b // pair * (planes - 1 - 2 * s) for s in (3, 0, 2, 1)]
 
     at.barrier()
+    line_o.start(do.wo_s)
+    own_o = mail.bring(do.wo_s, do.wo.at[b])
+    ex_u.start()
     line_da.start(do.wd_s)
-    do.wd[b] = do.wd_s[...]
+    own_d = mail.bring(do.wd_s, do.wd.at[b])
+    do.own_vectors(at.t)
     ex_v.start()
+    gather_x.start()
+    line_o.take(1)
+    ex_u.finish()
+    line_ua.start()
+    ex_v.finish()
+    do.plane_vectors(b)
+    line_v.start()
+    own_raw = mail.bring(do.wq_in, do.wq_raw)
+    line_ub.start()
+    gather_x.relay_x()
+    own_raw.wait()
+    do.sort_weight()
     ex_q.start()
-    gather_x.start()
-    line_o.start(do.wo_s)
-    do.wo[b] = do.wo_s[...]
-    ex_v.finish()
-    do.va[b] = jnp.sum(do.vec_in[...], axis=0)
-    line_v.start()
-    line_db.start(do.wd_s)
-    line_v.take(1)
-    ex_u.start()
+    own_o.wait()
+    gather_x.relay_y()
+    line_ua.take(1)
+    gather_x.share()
+    gather_c.start()
+    line_ub.take(1)
+    line_v.finish()
+    gather_x.far()
+    line_ua.take(2)
+    gather_x.finish()
+    do.statistics()
+    do.activations()
+    line_ub.take(2)
+    own_table = mail.bring(do.table_in, do.table)
+    line_ua.take(3)
     ex_q.finish()
     line_q.start()
-    line_o.take(1)
-    gather_x.relay_y()
-    line_q.take(1)
-    gather_x.relay_x()
-    gather_c.start()
-    line_o.take(2)
-    line_v.take(2)
-    gather_x.far()
-    line_v.take(3)
-    line_q.take(2)
-    gather_x.finish()
-    line_o.take(3)
-    do.statistics()
-    line_da.take(1)
-    do.activations()
     gather_c.relay_y()
     gather_c.relay_x()
-    ex_u.finish()
-    line_u.start()
+    gather_c.share()
+    line_ub.take(3)
+    do.expand(at.t)
+    line_o.take(2)
+    gather_c.far()
+    gather_c.finish()
+    line_q.take(1)
+    do.down_weight_grad(slots[0])
+    sum_d.edge(slots[0])
+    own_table.wait()
+    do.down_weight_grad(slots[1])
+    sum_d.edge(slots[1])
+    line_o.take(3)
     swap_w.start()
     mine[...] = do.wo[pl.ds(pair * c, pair)]
+    swap_w.finish()
+    do.attend_out_grad()
+    line_q.take(2)
+    line_db.start(do.wd_s)
+    do.down_weight_grad(slots[2])
+    sum_d.edge(slots[2])
+    do.down_weight_grad(slots[3])
+    sum_d.edge(slots[3])
+    own_d.wait()
+    line_da.take(1)
     line_q.take(3)
-    do.project()
-    swap_w.finish()
-    gather_c.far()
-    line_da.take(2)
+    do.project(at.t)
     do.attend()
-    gather_c.finish()
     do.dense_weight_grad()
     swap_g.start()
     do.go4[pl.ds(pair * c, pair)] = do.go[:, c]
-    do.attend_out_grad()
-    swap_g.finish()
-    for slot in slots:
-        sum_o.edge(slot)
-    line_u.take(1)
+    line_db.take(1)
     do.attend_grads()
     do.qkv_weight_grad(slots[0])
     sum_q.edge(slots[0])
     do.qkv_weight_grad(slots[1])
     sum_q.edge(slots[1])
+    line_db.take(2)
+    line_db.take(3)
     do.qkv_weight_grad(slots[2])
     sum_q.edge(slots[2])
-    do.qkv_weight_grad(slots[3])
-    sum_q.edge(slots[3])
-    line_u.take(2)
+    sum_d.hop(1, 0)
+    line_da.take(2)
     line_da.take(3)
-    line_u.take(3)
-    do.expand()
-    do.down_weight_grad(slots[0])
-    sum_d.edge(slots[0])
-    line_db.take(1)
-    sum_o.hop(1, 0)
-    sum_q.hop(1, 0)
-    line_db.take(2)
-    line_db.take(3)
+    do.out_terms()
+    plane_o.start()
     do.hidden_grad()
     do.up_weight_grad(slots[0])
     sum_u.edge(slots[0])
-    sum_q.hop(1, 1)
-    do.in_terms()
-    plane_g.start()
-    sum_q.hop(2, 0)
+    plane_o.fold()
+    sum_d.hop(1, 1)
     do.up_weight_grad(slots[1])
     sum_u.edge(slots[1])
     do.up_weight_grad(slots[2])
     sum_u.edge(slots[2])
-    sum_q.finish(do.fq)
-    back_q.start()
-    do.out_terms()
-    plane_o.start()
-    plane_g.fold()
-    sum_o.hop(2, 0)
-    sum_o.hop(1, 1)
+    do.qkv_weight_grad(slots[3])
+    sum_q.edge(slots[3])
     do.up_weight_grad(slots[3])
     sum_u.edge(slots[3])
+    sum_q.hop(1, 0)
+    plane_o.turn()
+    do.in_terms()
+    plane_g.start()
+    sum_q.hop(1, 1)
+    sum_d.hop(2, 0)
     sum_u.hop(1, 0)
-    do.down_weight_grad(slots[1])
-    sum_d.edge(slots[1])
-    do.small_terms()
+    sum_q.hop(2, 0)
+    plane_g.fold()
+    sum_d.finish(do.dd)
+    out_d = mail.bring(do.dd, do.dd_to)
+    do.small_terms(at.t)
     fold_v.start()
-    plane_o.fold()
     plane_g.turn()
-    sum_o.finish(do.dd_o)
+    sum_u.hop(1, 1)
+    sum_u.hop(2, 0)
     fold_v.finish()
     do.small_plane(b)
     line_s.start()
-    do.down_weight_grad(slots[2])
-    sum_d.edge(slots[2])
-    do.down_weight_grad(slots[3])
-    sum_d.edge(slots[3])
-    sum_d.hop(1, 0)
-    plane_o.turn()
-    sum_u.hop(2, 0)
-    line_s.take(1)
-    sum_u.hop(1, 1)
-    line_s.take(2)
-    back_q.finish()
-    line_s.take(3)
-    sum_d.hop(1, 1)
+    sum_q.finish(do.fq)
+    back_q.start()
+    swap_g.finish()
+    for slot in slots:
+        sum_o.edge(slot)
+    sum_u.finish(do.fu)
+    back_u.start()
+    sum_o.hop(1, 0)
+    line_s.finish()
+    sum_o.hop(1, 1)
     do.vt[...] = jnp.sum(do.vz[...], axis=0)
     share_v.start()
-    sum_d.hop(2, 0)
-    sum_u.finish(do.fu)
-    back_u.start()
-    do.result(plane_o.finish(), plane_g.finish(), do.out, do.in_grad)
+    back_q.finish()
+    sum_o.hop(2, 0)
+    do.result(at.t, plane_o.finish(), plane_g.finish())
+    out_x = mail.bring(do.out, do.out_to)
+    out_g = mail.bring(do.in_grad, do.in_grad_to)
+    back_u.finish()
     share_v.finish()
-    sum_d.finish(do.dd)
-    back_u.finish()
+    sum_o.finish(do.dd_o)
+    out_o = mail.bring(do.dd_o, do.dd_o_to)
+    for copied in (out_o, out_d, out_x, out_g):
+        copied.wait()
     mail.close()
-    for line in (line_v, line_o, line_q, line_u, line_da, line_db, line_s, sum_o, sum_q, sum_u, sum_d):
+    for line in (line_v, line_o, line_q, line_ua, line_ub, line_da, line_db, line_s, sum_o, sum_q, sum_u, sum_d):
         line.close()
 
 
@@ -1395,57 +1561,28 @@
     rank = lax.axis_index(ULY) * lax.axis_size(BLK) + lax.axis_index(BLK)
     owner = lax.axis_index(BATCH) * ranks + rank
 
-    x_own = jnp.transpose(residual_in, (1, 0, 2))
-    cot_own = jnp.transpose(cotangent, (1, 0, 2))
-    wq_send = jnp.transpose(
-        qkv_weight.reshape(rows, 3, 2, pair, ranks // 2, HD), (4, 2, 0, 1, 3, 5)
-    ).reshape(ranks, rows, 3 * LANES)
-    wu_send = jnp.transpose(
-        up_weight.reshape(rows, planes, ranks, depth), (2, 0, 1, 3)
-    ).reshape(ranks, rows, hidden)
-    at_rank = (jnp.arange(ranks) == rank).astype(single)[:, None]
-    at_owner = (jnp.arange(ranks * planes) == owner).astype(single)[:, None]
-    placed = [
-        (at_rank * v.astype(single)[None]).reshape(1, 2, LANES)
-        for v in (dense_bias, norm1_gain, norm1_bias, norm2_gain, norm2_bias, down_bias)
-    ]
-    placed_qkv = jnp.transpose(
-        (at_owner * qkv_bias.astype(single)[None]).reshape(3, 2, pair, ranks // 2, HD),
-        (3, 1, 0, 2, 4),
-    ).reshape(ranks, 3, LANES)
-    placed_up = jnp.transpose(
-        (at_owner * up_bias.astype(single)[None]).reshape(planes, ranks, LANES), (1, 0, 2)
-    )
-    vec_send = jnp.concatenate(
-        [jnp.broadcast_to(p, (ranks, 2, LANES)) for p in placed]
-        + [
-            placed_qkv,
-            jnp.zeros((ranks, 1, LANES), single),
-            placed_up,
-            jnp.zeros((ranks, 4, LANES), single),
-        ],
-        axis=1,
-    )
-    table = jnp.asarray(rotary_rows(length))
+    anywhere = pl.BlockSpec(memory_space=pl.ANY)
     inputs = dict(
-        x_own=x_own,
-        cot_own=cot_own,
-        wq_s=wq_send,
-        wu_s=wu_send,
-        wd_s=down_weight,
-        wo_s=dense_weight,
-        vec_s=vec_send,
-        table=table,
-    )
+        x_own=(jnp.transpose(residual_in, (1, 0, 2)), anywhere),
+        cot_own=(jnp.transpose(cotangent, (1, 0, 2)), anywhere),
+        wq_in=(qkv_weight, anywhere),
+        wu_s=(up_weight, anywhere),
+        wd_s=(down_weight, anywhere),
+        wo_s=(dense_weight, anywhere),
+        table_in=(jnp.asarray(rotary_rows(length)), anywhere),
+        b_qkv=(qkv_bias, VMEM),
+        b_up=(up_bias, VMEM),
+    )
+    for i, v in enumerate((dense_bias, norm1_gain, norm1_bias, norm2_gain, norm2_bias, down_bias)):
+        inputs["vector%d" % i] = (v, VMEM)
     shard = (seqs, tok_rows, width)
-    lanes_in = vec_send.shape[1]
     outputs = dict(
-        out=(shard, half_type),
-        in_grad=(shard, single),
+        out_to=(shard, half_type),
+        in_grad_to=(shard, single),
         dq=((ranks, rows, 3 * LANES), half_type),
         du=((ranks, rows, hidden), half_type),
-        dd=((depth, width), single),
-        dd_o=((rows, width), single),
+        dd_to=((depth, width), single),
+        dd_o_to=((rows, width), single),
         dv=((ranks, 16, LANES), single),
     )
     q_shape = (planes, ranks * rows, 3 * LANES)
@@ -1461,8 +1598,16 @@
         wd=(d_shape, half_type),
         wo=(o_shape, half_type),
         wo2=((pair, 2, rows, width), half_type),
-        vec_in=((ranks, lanes_in, LANES), single),
-        va=((planes, lanes_in, LANES), single),
+        wq_raw=(qkv_weight.shape, half_type),
+        wq_s=((ranks, rows, 3 * LANES), half_type),
+        table=((3, length, LANES), single),
+        out=(shard, half_type),
+        in_grad=(shard, single),
+        dd=((depth, width), single),
+        dd_o=((rows, width), single),
+        vec_s=((16, LANES), single),
+        vec_in=((ranks, 16, LANES), single),
+        va=((planes, 32, LANES), single),
         center=((tokens, 1), single),
         inverse=((tokens, 1), single),
         act_one=((tokens, width), half_type),
@@ -1507,18 +1652,18 @@
     )
     for block in range(length // TILE):
         scratch["probs%d" % block] = ((seqs * LANES // HD, TILE, (block + 1) * TILE), single)
-    names = tuple(inputs) + tuple(outputs) + tuple(scratch) + ("send", "recv")
+    names = tuple(inputs) + tuple(outputs) + tuple(scratch) + ("send", "recv", "near")
     out, in_grad, dq, du, dd, dd_o, dv = pl.pallas_call(
         functools.partial(layer_kernel, names, planes),
         out_shape=[jax.ShapeDtypeStruct(*what) for what in outputs.values()],
-        in_specs=[VMEM] * len(inputs),
-        out_specs=[VMEM] * len(outputs),
+        in_specs=[where for _, where in inputs.values()],
+        out_specs=[anywhere] * len(outputs),
         scratch_shapes=[pltpu.VMEM(*what) for what in scratch.values()]
-        + [pltpu.SemaphoreType.DMA((LAYER_SLOTS,))] * 2,
+        + [pltpu.SemaphoreType.DMA((n,)) for n in (LAYER_SLOTS, LAYER_SLOTS, NEAR_SLOTS)],
         compiler_params=pltpu.CompilerParams(
             collective_id=0, has_side_effects=True, vmem_limit_bytes=60 * 2**20
         ),
-    )(*inputs.values())
+    )(*(value for value, _ in inputs.values()))
 
     results = dict(
         out_out=(residual_in.shape, half_type),
@@ -1538,7 +1683,9 @@
     )
     return tuple(
         pl.pallas_call(
-            functools.partial(finish_kernel, tuple(outputs) + tuple(results), planes),
+            functools.partial(
+                finish_kernel, tuple(n.removesuffix("_to") for n in outputs) + tuple(results), planes
+            ),
             out_shape=[jax.ShapeDtypeStruct(*what) for what in results.values()],
             in_specs=[VMEM] * len(outputs),
             out_specs=[VMEM] * len(results),

time: 112 us -> 109 us (0.973)
  local copies, waits for them, and re-layouts: 7.02 us -> 1.94 us
  Pallas kernels: 103 us -> 106 us
    reshape x7 -> x0, local copies, waits for them, and re-layouts: 2.54 us -> none  [the longest x1 0.95 us: fast_body(): wq_send = jnp.transpose(qkv_weight.reshape(rows, 3, 2, pair, ranks // 2,...]
    pallas_call x1, Pallas kernels: 100 us -> 103 us  [fast_body(): pl.pallas_call(functools.partial(layer_kernel, names, planes), out_shape=...]
    concatenate x1 -> x0, local copies, waits for them, and re-layouts: 1.92 us -> none  [fast_body(): jnp.concatenate([jnp.broadcast_to(p, (ranks, 2, LANES)) for p in placed]...]
where the time goes in v3:
time: 109 us; the launch traced here: 108 us
  Pallas kernels  106 us (97%)
  local copies, waits for them, and re-layouts  1.94 us (2%)
    pallas_call x1, Pallas kernels, fast_body(): pl.pallas_call(functools.partial(layer_kernel, names, planes), out_shape=...  103 us
    pallas_call x1, Pallas kernels, fast_body(): pl.pallas_call(functools.partial(finish_kernel, tuple((n.removesuffix('_t...  3.18 us

profile of v3, /device:TPU:0, one launch (start us, length us, event | category | flops | bytes accessed | tf_op | source)
XLA Modules:
  0.0 108.4 jit_solution(10665714896322634164)
XLA Ops:
  0.6 1.9 %copy_bitcast_fusion = (bf16[2,64,1024]{2,1,0:T(8,128)(2,1)}, bf16[2,64,1024]{2,1,0:T(8,128)(2,1)}) fusion(bf16[64,2,1024]{2,1,0:T(2,128)(2,1)} %param.28, bf16[64,2,1024]{2,1,0:T(2,128)(2,1)} %param.15), kind=kLoop, calls=%fused_computation | loop fusion | bytes 1048576 | tf_op jit(solution)/shard_map/transpose | solution.py:1567
  2.6 102.5 %shard_map.254 = (bf16[2,64,1024]{2,1,0:T(8,128)(2,1)}, f32[2,64,1024]{2,1,0:T(8,128)}, bf16[8,32,384]{2,1,0:T(8,128)(2,1)}, bf16[8,32,512]{2,1,0:T(8,128)(2,1)}...) custom-call(bf16[2,64,1024]{2,1,0:T(8,128)(2,1)} %get-tuple-element.29.refs_0_, ...), custom_call_target="tpu_custom_call" | custom-call | tf_op jit(solution)/shard_map/pallas_call | solution.py:1656
  105.1 3.2 %shard_map.255 = (bf16[64,2,1024]{2,1,0:T(2,128)(2,1)}, f32[64,2,1024]{2,1,0:T(2,128)}, f32[32,3072]{1,0:T(8,128)}, f32[96]{0:T(128)}, f32[32,1024]{1,0:T(8,128)...) custom-call(bf16[2,64,1024]{2,1,0:T(8,128)(2,1)} %get-tuple-element., ...), custom_call_target="tpu_custom_call" | custom-call | tf_op jit(solution)/shard_map/pallas_call | solution.py:1685

commit v4 on v3

--- a/solution.py
+++ b/solution.py
@@ -775,9 +775,11 @@
 
 
 class LineReduce:
-    def __init__(self, at, mail, terms, above, below):
+    def __init__(self, at, mail, terms, above, below, up_cut=None, down_cut=None):
         self.at, self.mail, self.terms = at, mail, terms
         self.above, self.below = above, below
+        whole = pl.ds(0, terms.shape[2])
+        self.up_cut, self.down_cut = up_cut or whole, down_cut or whole
         self.up, self.down = mail.slots(at.planes), mail.slots(at.planes)
 
     def edge(self, slot):
@@ -786,73 +788,85 @@
         @pl.when((at.b == 0) & (slot > 0))
         def _():
             self.mail.copy(
-                self.terms.at[slot], self.below.at[slot], self.up + slot, at.along(1)
+                self.terms.at[slot, :, self.up_cut],
+                self.below.at[slot, :, self.up_cut],
+                self.up + slot,
+                at.along(1),
             ).start()
 
         @pl.when((at.b == last) & (slot < last))
         def _():
             self.mail.copy(
-                self.terms.at[slot], self.above.at[slot], self.down + slot, at.along(-1)
+                self.terms.at[slot, :, self.down_cut],
+                self.above.at[slot, :, self.down_cut],
+                self.down + slot,
+                at.along(-1),
             ).start()
 
     def hop(self, hop, rank):
         last = self.at.planes - 1
         if last - rank > hop:
-            self._forward(last - rank, self.below, self.up, 1, self.at.b == hop)
-            self._forward(rank, self.above, self.down, -1, self.at.b == last - hop)
-
-    def _forward(self, slot, held, base, step, here):
+            self._forward(last - rank, self.below, self.up_cut, self.up, 1, self.at.b == hop)
+            self._forward(rank, self.above, self.down_cut, self.down, -1, self.at.b == last - hop)
+
+    def _forward(self, slot, held, cut, base, step, here):
         at, mail = self.at, self.mail
-        part = held.at[slot]
+        part = held.at[slot, :, cut]
 
         @pl.when(here)
         def _():
             mail.arrived(part, base + slot, at.along(-step))
-            total = self.terms[slot].astype(jnp.float32) + part[...].astype(jnp.float32)
-            part[...] = total.astype(part.dtype)
+            total = self.terms[slot, :, cut].astype(jnp.float32) + held[slot, :, cut].astype(
+                jnp.float32
+            )
+            held[slot, :, cut] = total.astype(held.dtype)
             mail.copy(part, part, base + slot, at.along(step)).start()
 
-    def finish(self, out):
+    def landed(self):
         at, mail = self.at, self.mail
-        b = at.b
-        kind = out.dtype
+
+        @pl.when(at.b > 0)
+        def _():
+            mail.arrived(self.below.at[at.b, :, self.up_cut], self.up + at.b, at.along(-1))
+
+        @pl.when(at.b < at.planes - 1)
+        def _():
+            mail.arrived(self.above.at[at.b, :, self.down_cut], self.down + at.b, at.along(1))
+
+    def total(self, out):
+        at = self.at
+        b, last = at.b, at.planes - 1
+
+        def put(*parts):
+            value = self.terms[b].astype(jnp.float32)
+            for part in parts:
+                value = value + part[b].astype(jnp.float32)
+            out[...] = value.astype(out.dtype)
 
         @pl.when(b == 0)
         def _():
-            mail.arrived(self.above.at[b], self.down + b, at.along(1))
-            out[...] = (
-                self.terms[b].astype(jnp.float32) + self.above[b].astype(jnp.float32)
-            ).astype(kind)
-
-        @pl.when(b == at.planes - 1)
+            put(self.above)
+
+        @pl.when(b == last)
         def _():
-            mail.arrived(self.below.at[b], self.up + b, at.along(-1))
-            out[...] = (
-                self.terms[b].astype(jnp.float32) + self.below[b].astype(jnp.float32)
-            ).astype(kind)
-
-        @pl.when((b > 0) & (b < at.planes - 1))
+            put(self.below)
+
+        @pl.when((b > 0) & (b < last))
         def _():
-            mail.arrived(self.below.at[b], self.up + b, at.along(-1))
-            mail.arrived(self.above.at[b], self.down + b, at.along(1))
-            out[...] = (
-                self.terms[b].astype(jnp.float32)
-                + self.below[b].astype(jnp.float32)
-                + self.above[b].astype(jnp.float32)
-            ).astype(kind)
+            put(self.below, self.above)
 
     def close(self):
         at = self.at
         for slot in range(at.planes):
-            part = self.terms.at[slot]
+            up, down = self.terms.at[slot, :, self.up_cut], self.terms.at[slot, :, self.down_cut]
 
             @pl.when(at.b < slot)
             def _():
-                self.mail.copy(part, part, self.up + slot, at.along(1)).wait_send()
+                self.mail.copy(up, up, self.up + slot, at.along(1)).wait_send()
 
             @pl.when(at.b > slot)
             def _():
-                self.mail.copy(part, part, self.down + slot, at.along(-1)).wait_send()
+                self.mail.copy(down, down, self.down + slot, at.along(-1)).wait_send()
 
 
 TILE = 256
@@ -1006,12 +1020,27 @@
             [self.va[b, pl.ds(24 + rank, 1), :] for b in range(self.va.shape[0])], axis=1
         )
 
-    def project(self, rank):
+    def near(self, ref, side):
+        both = ref[pl.ds(side * 2, 2)]
+        return both.reshape(both.shape[0] * both.shape[1], both.shape[2])
+
+    def half_columns(self, side, width):
+        return pl.ds(pl.multiple_of(side * (width // 2), width // 2), width // 2)
+
+    def project_near(self, side):
+        def step(i):
+            cut = self.half_columns(side, self.width)
+            self.qkv[self.rows(i), :] = dot_nn(self.act_one[self.rows(i), cut], self.near(self.wq, side))
+
+        self.loop(self.tiles, step)
+
+    def project(self, rank, side):
         bias = self.qkv_bias(rank)
 
         def step(i):
-            weight = self.wq[...].reshape(self.width, 3 * LANES)
-            qkv = dot_nn(self.act_one[self.rows(i), :], weight) + bias
+            cut = self.half_columns(side, self.width)
+            qkv = dot_nn(self.act_one[self.rows(i), cut], self.near(self.wq, side))
+            qkv = qkv + self.qkv[self.rows(i), :] + bias
             rows = pl.ds(pl.multiple_of(i % self.per_seq * TILE, TILE), TILE)
             query = turn(qkv[:, :LANES], self.tables, rows, 1.0).astype(jnp.bfloat16)
             self.query[self.rows(i), :] = query * jnp.asarray(1.0 / math.sqrt(HD), jnp.bfloat16)
@@ -1026,27 +1055,24 @@
         start = pl.multiple_of(seq * self.length, TILE)
         return pl.ds(start, (block + 1) * TILE)
 
-    def attend(self):
-        def step(seq):
-            for block in range(self.per_seq):
-                rows = self.rows(seq * self.per_seq + block)
-                keys = self.keys(seq, block)
-                key, value, query = self.key[keys, :], self.value[keys, :], self.query[rows, :]
-                out = None
-                for head in range(self.heads):
-                    scores = dot_nt(of_head(query, head), key)
-                    at = lax.broadcasted_iota(jnp.int32, scores.shape, 0) + block * TILE
-                    to = lax.broadcasted_iota(jnp.int32, scores.shape, 1)
-                    scores = jnp.where(to <= at, scores, -jnp.inf)
-                    top = jnp.max(scores, axis=1, keepdims=True)
-                    weight = jnp.exp(scores - top)
-                    weight = weight * (1.0 / jnp.sum(weight, axis=1, keepdims=True))
-                    self.probs[block][seq * self.heads + head] = weight
-                    part = dot_nn(weight.astype(jnp.bfloat16), value)
-                    out = of_head(part, head) if out is None else out + of_head(part, head)
-                self.attn[rows, :] = out.astype(jnp.bfloat16)
-
-        self.loop(self.seqs, step)
+    def attend(self, seq):
+        for block in range(self.per_seq):
+            rows = self.rows(seq * self.per_seq + block)
+            keys = self.keys(seq, block)
+            key, value, query = self.key[keys, :], self.value[keys, :], self.query[rows, :]
+            out = None
+            for head in range(self.heads):
+                scores = dot_nt(of_head(query, head), key)
+                at = lax.broadcasted_iota(jnp.int32, scores.shape, 0) + block * TILE
+                to = lax.broadcasted_iota(jnp.int32, scores.shape, 1)
+                scores = jnp.where(to <= at, scores, -jnp.inf)
+                top = jnp.max(scores, axis=1, keepdims=True)
+                weight = jnp.exp(scores - top)
+                weight = weight * (1.0 / jnp.sum(weight, axis=1, keepdims=True))
+                self.probs[block][seq * self.heads + head] = weight
+                part = dot_nn(weight.astype(jnp.bfloat16), value)
+                out = of_head(part, head) if out is None else out + of_head(part, head)
+            self.attn[rows, :] = out.astype(jnp.bfloat16)
 
     def attend_out_grad(self):
         def step(i):
@@ -1095,9 +1121,6 @@
             ).astype(jnp.bfloat16)
             self.qkv_grad[rows, 2 * LANES :] = value_grad[block].astype(jnp.bfloat16)
 
-    def attend_grads(self):
-        self.loop(self.seqs, self.attend_grad)
-
     def cot_flat(self):
         return self.ca[...].reshape(self.seqs * self.length, self.width)
 
@@ -1111,12 +1134,22 @@
             dot_tn(self.attn[...], self.cot_flat()).astype(jnp.bfloat16).reshape(self.go.shape)
         )
 
-    def expand(self, rank):
+    def expand_near(self, side):
+        def step(i):
+            cut = self.half_columns(side, self.width)
+            self.slope[self.rows(i), :] = dot_nn(
+                self.act_two[self.rows(i), cut], self.near(self.wu, side)
+            )
+
+        self.loop(self.tiles, step)
+
+    def expand(self, rank, side):
         bias = self.up_bias(rank)
 
         def step(i):
-            weight = self.wu[...].reshape(self.width, self.hidden)
-            pre = dot_nn(self.act_two[self.rows(i), :], weight) + bias
+            cut = self.half_columns(side, self.width)
+            pre = dot_nn(self.act_two[self.rows(i), cut], self.near(self.wu, side))
+            pre = pre + self.slope[self.rows(i), :] + bias
             cdf = 0.5 * (1.0 + lax.erf(pre * INV_ROOT_TWO))
             self.gelu[self.rows(i), :] = (pre * cdf).astype(jnp.bfloat16)
             self.slope[self.rows(i), :] = cdf + pre * jnp.exp(-0.5 * pre * pre) * INV_ROOT_TWO_PI
@@ -1128,20 +1161,21 @@
         part = self.gelu[:, pl.ds(pl.multiple_of(i * depth, depth), depth)]
         self.gd[i] = dot_tn(part, self.cot_flat()).astype(jnp.bfloat16)
 
-    def hidden_grad(self):
+    def hidden_grad(self, side):
         def step(i):
-            weight = self.wd[...].reshape(self.hidden, self.width)
-            grad = dot_nt(self.in_seq(self.ca, i), weight)
-            self.pre_grad[self.rows(i), :] = (grad * self.slope[self.rows(i), :]).astype(
+            cut = self.half_columns(side, self.hidden)
+            grad = dot_nt(self.in_seq(self.ca, i), self.near(self.wd, side))
+            self.pre_grad[self.rows(i), cut] = (grad * self.slope[self.rows(i), cut]).astype(
                 jnp.bfloat16
             )
 
         self.loop(self.tiles, step)
 
-    def up_weight_grad(self, i):
+    def up_weight_grad(self, i, side):
         rows = self.gu.shape[1]
         act = self.act_two[:, pl.ds(pl.multiple_of(i * rows, rows), rows)]
-        self.gu[i] = dot_tn(act, self.pre_grad[...]).astype(jnp.bfloat16)
+        cut = self.half_columns(side, self.hidden)
+        self.gu[i, :, cut] = dot_tn(act, self.pre_grad[:, cut]).astype(jnp.bfloat16)
 
     def put_terms(self, terms, i, value):
         seq, chips, cores, rows, width = terms.shape
@@ -1150,33 +1184,32 @@
             jnp.bfloat16
         ).reshape(n, cores, rows, width)
 
-    def out_terms(self):
-        def step(i):
-            dense = self.wo2[...].reshape(LANES, self.width)
-            down = self.wd[...].reshape(self.hidden, self.width)
-            self.put_terms(
-                self.po,
-                i,
-                dot_nn(self.attn[self.rows(i), :], dense) + dot_nn(self.gelu[self.rows(i), :], down),
-            )
-
-        self.loop(self.tiles, step)
-
-    def in_terms(self):
+    def out_terms(self, i):
+        dense = self.wo2[...].reshape(LANES, self.width)
+        down = self.wd[...].reshape(self.hidden, self.width)
+        self.put_terms(
+            self.po,
+            i,
+            dot_nn(self.attn[self.rows(i), :], dense) + dot_nn(self.gelu[self.rows(i), :], down),
+        )
+
+    def in_terms(self, i):
         gain_one, gain_two = self.wide(1), self.wide(3)
-        self.sums[...] = jnp.zeros_like(self.sums)
-
-        def step(i):
-            normed = self.normed(i)
-            weight = self.wq[...].reshape(self.width, 3 * LANES)
-            one = dot_nt(self.qkv_grad[self.rows(i), :], weight)
-            weight = self.wu[...].reshape(self.width, self.hidden)
-            two = dot_nt(self.pre_grad[self.rows(i), :], weight)
-            self.put_terms(self.pg, i, one * gain_one + two * gain_two)
-            for j, value in enumerate((one * normed, one, two * normed, two)):
+        normed = self.normed(i)
+        weight = self.wq[...].reshape(self.width, 3 * LANES)
+        one = dot_nt(self.qkv_grad[self.rows(i), :], weight)
+        weight = self.wu[...].reshape(self.width, self.hidden)
+        two = dot_nt(self.pre_grad[self.rows(i), :], weight)
+        self.put_terms(self.pg, i, one * gain_one + two * gain_two)
+        for j, value in enumerate((one * normed, one, two * normed, two)):
+            if i == 0:
+                self.sums[j : j + 1, :] = total_rows(value)
+            else:
                 self.sums[j : j + 1, :] += total_rows(value)
 
-        self.loop(self.tiles, step)
+    def split(self, raw, own):
+        for seq in range(own.shape[0]):
+            own[seq] = raw[:, seq, :]
 
     def own_rows(self, ref, rank):
         rows = self.out.shape[1]
@@ -1215,7 +1248,7 @@
         )
 
 
-LAYER_SLOTS = 4 * 8 + 4 + 12 * 8 + 10 * 8 + 2
+LAYER_SLOTS = 5 * 8 + 4 + 12 * 8 + 10 * 8 + 2
 NEAR_SLOTS = 24
 
 
@@ -1270,7 +1303,11 @@
     )
     sum_o = LineReduce(at, mail, do.go4, do.above_o, do.below_o)
     sum_q = LineReduce(at, mail, do.gq, do.above_q, do.below_q)
-    sum_u = LineReduce(at, mail, do.gu, do.above_u, do.below_u)
+    first, second = (pl.ds(i * do.hidden // 2, do.hidden // 2) for i in range(2))
+    sum_un = LineReduce(at, mail, do.gu, do.above_u, do.below_u, first, second)
+    sum_uf = LineReduce(at, mail, do.gu, do.above_u, do.below_u, second, first)
+    near_side = b // pair
+    far_side = 1 - near_side
     sum_d = LineReduce(at, mail, do.gd, do.above_d, do.below_d)
     swap_g = PairExchange(
         at,
@@ -1290,148 +1327,181 @@
     slots = [s + b // pair * (planes - 1 - 2 * s) for s in (3, 0, 2, 1)]
 
     at.barrier()
+    line_da.start(do.wd_s)
+    own_d = mail.bring(do.wd_s, do.wd.at[b])
+    raw_x = mail.bring(do.x_in, do.x_raw)
+    ex_u.start()
+    line_db.start(do.wd_s)
     line_o.start(do.wo_s)
     own_o = mail.bring(do.wo_s, do.wo.at[b])
-    ex_u.start()
-    line_da.start(do.wd_s)
-    own_d = mail.bring(do.wd_s, do.wd.at[b])
+    raw_x.wait()
+    do.split(do.x_raw, do.x_own)
+    own_raw = mail.bring(do.wq_in, do.wq_raw)
+    gather_x.start()
+    own_o.wait()
+    ex_u.finish()
+    line_ua.start()
+    raw_c = mail.bring(do.cot_in, do.cot_raw)
+    own_table = mail.bring(do.table_in, do.table)
     do.own_vectors(at.t)
     ex_v.start()
-    gather_x.start()
-    line_o.take(1)
-    ex_u.finish()
-    line_ua.start()
+    gather_x.relay_x()
+    line_ub.start()
+    own_raw.wait()
+    do.sort_weight()
+    ex_q.start()
+    own_table.wait()
+    gather_x.relay_y()
+    line_ua.take(1)
+    raw_c.wait()
+    do.split(do.cot_raw, do.cot_own)
     ex_v.finish()
     do.plane_vectors(b)
     line_v.start()
-    own_raw = mail.bring(do.wq_in, do.wq_raw)
-    line_ub.start()
-    gather_x.relay_x()
-    own_raw.wait()
-    do.sort_weight()
-    ex_q.start()
-    own_o.wait()
-    gather_x.relay_y()
-    line_ua.take(1)
     gather_x.share()
+    line_ub.take(1)
+    gather_x.far()
     gather_c.start()
-    line_ub.take(1)
-    line_v.finish()
-    gather_x.far()
     line_ua.take(2)
+    own_d.wait()
     gather_x.finish()
     do.statistics()
+    line_v.finish()
     do.activations()
     line_ub.take(2)
-    own_table = mail.bring(do.table_in, do.table)
-    line_ua.take(3)
+    gather_c.relay_x()
+    do.expand_near(near_side)
+    gather_c.relay_y()
     ex_q.finish()
     line_q.start()
-    gather_c.relay_y()
-    gather_c.relay_x()
+    line_o.take(1)
     gather_c.share()
     line_ub.take(3)
-    do.expand(at.t)
-    line_o.take(2)
+    line_ua.take(3)
     gather_c.far()
+    do.expand(at.t, far_side)
     gather_c.finish()
-    line_q.take(1)
     do.down_weight_grad(slots[0])
     sum_d.edge(slots[0])
-    own_table.wait()
+    line_q.take(1)
     do.down_weight_grad(slots[1])
     sum_d.edge(slots[1])
-    line_o.take(3)
-    swap_w.start()
-    mine[...] = do.wo[pl.ds(pair * c, pair)]
-    swap_w.finish()
-    do.attend_out_grad()
-    line_q.take(2)
-    line_db.start(do.wd_s)
     do.down_weight_grad(slots[2])
     sum_d.edge(slots[2])
     do.down_weight_grad(slots[3])
     sum_d.edge(slots[3])
-    own_d.wait()
+    line_o.take(2)
+    line_o.take(3)
+    swap_w.start()
+    mine[...] = do.wo[pl.ds(pair * c, pair)]
+    do.project_near(near_side)
+    swap_w.finish()
+    do.attend_out_grad()
+    line_q.take(2)
+    line_db.take(1)
     line_da.take(1)
+    do.hidden_grad(near_side)
+    do.up_weight_grad(slots[0], near_side)
+    sum_un.edge(slots[0])
     line_q.take(3)
-    do.project(at.t)
-    do.attend()
+    do.project(at.t, far_side)
+    do.attend(0)
+    do.attend(1)
     do.dense_weight_grad()
     swap_g.start()
     do.go4[pl.ds(pair * c, pair)] = do.go[:, c]
-    line_db.take(1)
-    do.attend_grads()
+    line_da.take(2)
+    do.up_weight_grad(slots[1], near_side)
+    sum_un.edge(slots[1])
+    do.up_weight_grad(slots[2], near_side)
+    sum_un.edge(slots[2])
+    do.attend_grad(0)
+    do.attend_grad(1)
     do.qkv_weight_grad(slots[0])
     sum_q.edge(slots[0])
+    do.up_weight_grad(slots[3], near_side)
+    sum_un.edge(slots[3])
+    line_da.take(3)
+    line_db.take(2)
+    line_db.take(3)
+    sum_d.hop(1, 0)
+    do.out_terms(0)
+    do.out_terms(1)
+    do.out_terms(2)
+    do.out_terms(3)
+    plane_o.start()
+    do.hidden_grad(far_side)
+    do.up_weight_grad(slots[0], far_side)
+    sum_uf.edge(slots[0])
+    do.up_weight_grad(slots[1], far_side)
+    sum_uf.edge(slots[1])
+    do.up_weight_grad(slots[2], far_side)
+    sum_uf.edge(slots[2])
+    do.up_weight_grad(slots[3], far_side)
+    sum_uf.edge(slots[3])
+    sum_d.hop(1, 1)
+    plane_o.fold()
     do.qkv_weight_grad(slots[1])
     sum_q.edge(slots[1])
-    line_db.take(2)
-    line_db.take(3)
     do.qkv_weight_grad(slots[2])
     sum_q.edge(slots[2])
-    sum_d.hop(1, 0)
-    line_da.take(2)
-    line_da.take(3)
-    do.out_terms()
-    plane_o.start()
-    do.hidden_grad()
-    do.up_weight_grad(slots[0])
-    sum_u.edge(slots[0])
-    plane_o.fold()
-    sum_d.hop(1, 1)
-    do.up_weight_grad(slots[1])
-    sum_u.edge(slots[1])
-    do.up_weight_grad(slots[2])
-    sum_u.edge(slots[2])
     do.qkv_weight_grad(slots[3])
     sum_q.edge(slots[3])
-    do.up_weight_grad(slots[3])
-    sum_u.edge(slots[3])
+    do.in_terms(0)
     sum_q.hop(1, 0)
     plane_o.turn()
-    do.in_terms()
+    do.in_terms(1)
+    do.in_terms(2)
+    do.in_terms(3)
     plane_g.start()
-    sum_q.hop(1, 1)
+    sum_un.hop(1, 0)
     sum_d.hop(2, 0)
-    sum_u.hop(1, 0)
-    sum_q.hop(2, 0)
     plane_g.fold()
-    sum_d.finish(do.dd)
-    out_d = mail.bring(do.dd, do.dd_to)
+    sum_uf.hop(1, 0)
+    sum_un.hop(2, 0)
+    sum_uf.hop(1, 1)
     do.small_terms(at.t)
     fold_v.start()
+    sum_un.hop(1, 1)
+    sum_uf.hop(2, 0)
     plane_g.turn()
-    sum_u.hop(1, 1)
-    sum_u.hop(2, 0)
     fold_v.finish()
     do.small_plane(b)
     line_s.start()
-    sum_q.finish(do.fq)
-    back_q.start()
+    sum_q.hop(1, 1)
     swap_g.finish()
     for slot in slots:
         sum_o.edge(slot)
-    sum_u.finish(do.fu)
+    sum_q.hop(2, 0)
+    sum_un.landed()
+    sum_uf.landed()
+    sum_un.total(do.fu)
     back_u.start()
-    sum_o.hop(1, 0)
-    line_s.finish()
-    sum_o.hop(1, 1)
-    do.vt[...] = jnp.sum(do.vz[...], axis=0)
-    share_v.start()
-    back_q.finish()
-    sum_o.hop(2, 0)
     do.result(at.t, plane_o.finish(), plane_g.finish())
     out_x = mail.bring(do.out, do.out_to)
     out_g = mail.bring(do.in_grad, do.in_grad_to)
+    line_s.finish()
+    sum_o.hop(1, 0)
+    do.vt[...] = jnp.sum(do.vz[...], axis=0)
+    share_v.start()
+    sum_q.landed()
+    sum_q.total(do.fq)
+    back_q.start()
+    sum_o.hop(1, 1)
+    sum_d.landed()
+    sum_d.total(do.dd)
+    out_d = mail.bring(do.dd, do.dd_to)
+    sum_o.hop(2, 0)
     back_u.finish()
     share_v.finish()
-    sum_o.finish(do.dd_o)
+    sum_o.landed()
+    sum_o.total(do.dd_o)
     out_o = mail.bring(do.dd_o, do.dd_o_to)
+    back_q.finish()
     for copied in (out_o, out_d, out_x, out_g):
         copied.wait()
     mail.close()
-    for line in (line_v, line_o, line_q, line_ua, line_ub, line_da, line_db, line_s, sum_o, sum_q, sum_u, sum_d):
+    for line in (line_v, line_o, line_q, line_ua, line_ub, line_da, line_db, line_s, sum_o, sum_q, sum_un, sum_uf, sum_d):
         line.close()
 
 
@@ -1563,8 +1633,8 @@
 
     anywhere = pl.BlockSpec(memory_space=pl.ANY)
     inputs = dict(
-        x_own=(jnp.transpose(residual_in, (1, 0, 2)), anywhere),
-        cot_own=(jnp.transpose(cotangent, (1, 0, 2)), anywhere),
+        x_in=(residual_in, anywhere),
+        cot_in=(cotangent, anywhere),
         wq_in=(qkv_weight, anywhere),
         wu_s=(up_weight, anywhere),
         wd_s=(down_weight, anywhere),
@@ -1598,6 +1668,11 @@
         wd=(d_shape, half_type),
         wo=(o_shape, half_type),
         wo2=((pair, 2, rows, width), half_type),
+        x_raw=(residual_in.shape, half_type),
+        cot_raw=(residual_in.shape, half_type),
+        x_own=(shard, half_type),
+        cot_own=(shard, half_type),
+        qkv=((tokens, 3 * LANES), single),
         wq_raw=(qkv_weight.shape, half_type),
         wq_s=((ranks, rows, 3 * LANES), half_type),
         table=((3, length, LANES), single),

time: 109 us -> 103 us (0.945)
  Pallas kernels: 106 us -> 103 us
  local copies, waits for them, and re-layouts: 1.94 us -> 0 us
    pallas_call x1, Pallas kernels: 103 us -> 99.4 us  [fast_body(): pl.pallas_call(functools.partial(layer_kernel, names, planes), out_shape=...]
    transpose x1 -> x0, local copies, waits for them, and re-layouts: 1.94 us -> none  [fast_body(): jnp.transpose(cotangent, (1, 0, 2))]
where the time goes in v4:
time: 103 us
  Pallas kernels  103 us (100%)
    pallas_call x1, Pallas kernels, fast_body(): pl.pallas_call(functools.partial(layer_kernel, names, planes), out_shape=...  99.4 us
    pallas_call x1, Pallas kernels, fast_body(): pl.pallas_call(functools.partial(finish_kernel, tuple((n.removesuffix('_t...  3.18 us

profile of v4, /device:TPU:0, one launch (start us, length us, event | category | flops | bytes accessed | tf_op | source)
XLA Modules:
  0.0 103.3 jit_solution(2878604888684514751)
XLA Ops:
  0.7 99.4 %shard_map.254 = (bf16[2,64,1024]{2,1,0:T(8,128)(2,1)}, f32[2,64,1024]{2,1,0:T(8,128)}, bf16[8,32,384]{2,1,0:T(8,128)(2,1)}, bf16[8,32,512]{2,1,0:T(8,128)(2,1)}...) custom-call(bf16[64,2,1024]{2,1,0:T(2,128)(2,1)} %refs_0_.1, bf16[64,2,1024]{2,1,0:T(2,128)(2,1)} %refs_1_.1, ...), custom_call_target="tpu_custom_call" | custom-call | tf_op jit(solution)/shard_map/pallas_call | solution.py:1731
  100.0 3.2 %shard_map.255 = (bf16[64,2,1024]{2,1,0:T(2,128)(2,1)}, f32[64,2,1024]{2,1,0:T(2,128)}, f32[32,3072]{1,0:T(8,128)}, f32[96]{0:T(128)}, f32[32,1024]{1,0:T(8,128)...) custom-call(bf16[2,64,1024]{2,1,0:T(8,128)(2,1)} %get-tuple-element., ...), custom_call_target="tpu_custom_call" | custom-call | tf_op jit(solution)/shard_map/pallas_call | solution.py:1760

commit v5 on v4

--- a/solution.py
+++ b/solution.py
@@ -469,57 +469,78 @@
         sem = pltpu.get_barrier_semaphore()
         for d in range(1, 8):
             pl.semaphore_signal(sem, inc=1, device_id=self.peer(d), device_id_type=MESH)
-
-        for step in range(1, self.planes):
-
-            @pl.when(self.b >= step)
+        self.to_neighbours(
+            lambda step: pl.semaphore_signal(
+                sem, inc=1, device_id=self.along(step), device_id_type=MESH
+            )
+        )
+        below = (self.b > 0).astype(jnp.int32)
+        above = (self.b < self.planes - 1).astype(jnp.int32)
+        pl.semaphore_wait(sem, 7 + below + above)
+
+    def to_neighbours(self, action):
+        for step in (-1, 1):
+
+            @pl.when(self.b > 0 if step < 0 else self.b < self.planes - 1)
             def _():
-                pl.semaphore_signal(sem, inc=1, device_id=self.along(-step), device_id_type=MESH)
-
-            @pl.when(self.b + step < self.planes)
+                action(step)
+
+    def reach(self, second, third):
+        b, last = self.b, self.planes - 1
+
+        @pl.when((b > 0) & (b < last))
+        def _():
+            for step in (-1, 1):
+                pl.semaphore_signal(
+                    second, inc=1, device_id=self.along(step), device_id_type=MESH
+                )
+
+        pl.semaphore_wait(second, (b >= 2).astype(jnp.int32) + (b <= last - 2).astype(jnp.int32))
+        for middle, step in ((1, -1), (2, 1)):
+
+            @pl.when(b == middle)
             def _():
-                pl.semaphore_signal(sem, inc=1, device_id=self.along(step), device_id_type=MESH)
-
-        pl.semaphore_wait(sem, 7 + self.planes - 1)
+                pl.semaphore_signal(third, inc=1, device_id=self.along(step), device_id_type=MESH)
+
+        @pl.when((b == 0) | (b == last))
+        def _():
+            pl.semaphore_wait(third, 1)
 
 
 class Mail:
     def __init__(self, send, recv, near):
-        self.send, self.recv, self.used, self.open = send, recv, 0, []
-        self.near, self.near_used = near, 0
+        self.send, self.recv, self.near = send, recv, near
+        self.sends = self.recvs = self.nears = 0
+
+    def send_slots(self, n=1):
+        self.sends += n
+        return self.sends - n
+
+    def recv_slots(self, n=1):
+        self.recvs += n
+        return self.recvs - n
 
     def bring(self, src, dst):
-        made = pltpu.make_async_copy(src, dst, self.near.at[self.near_used])
-        self.near_used += 1
+        made = pltpu.make_async_copy(src, dst, self.near.at[self.nears])
+        self.nears += 1
         made.start()
         return made
 
-    def slots(self, n):
-        first = self.used
-        self.used += n
-        return first
-
-    def copy(self, src, dst, slot, device, recv_slot=None):
+    def copy(self, src, dst, send, recv, device):
         return pltpu.make_async_remote_copy(
             src_ref=src,
             dst_ref=dst,
-            send_sem=self.send.at[slot],
-            recv_sem=self.recv.at[slot if recv_slot is None else recv_slot],
+            send_sem=self.send.at[send],
+            recv_sem=self.recv.at[recv],
             device_id=device,
             device_id_type=MESH,
         )
 
-    def post(self, src, dst, slot, device):
-        made = self.copy(src, dst, slot, device)
-        made.start()
-        self.open.append(made)
-
-    def arrived(self, dst, slot, device):
-        self.copy(dst, dst, slot, device).wait_recv()
-
-    def close(self):
-        for made in self.open:
-            made.wait_send()
+    def arrived(self, bulk, recv, device):
+        self.copy(bulk, bulk, 0, recv, device).wait_recv()
+
+    def gone(self, bulk, send, device):
+        self.copy(bulk, bulk, send, 0, device).wait_send()
 
 
 class PlaneGather:
@@ -527,7 +548,7 @@
         self.at, self.mail, self.shard, self.whole = at, mail, shard, whole
         self.rows = shard.shape[1]
         self.halves = shard.shape[0] // 2
-        self.base = mail.slots(10)
+        self.send, self.recv = mail.send_slots(), mail.recv_slots(5)
 
     def half(self, i):
         return self.shard.at[pl.ds(i * self.halves, self.halves)]
@@ -538,52 +559,54 @@
             return self.whole.at[:, rows, :]
         return self.whole.at[pl.ds(half * self.halves, self.halves), rows, :]
 
+    def bulk(self, shards):
+        return self.whole.at[:, pl.ds(0, shards * self.rows), :]
+
+    def post(self, src, dst, recv, device):
+        self.mail.copy(src, dst, self.send, self.recv + recv, device).start()
+
+    def arrived(self, bulk, recv, device):
+        self.mail.arrived(bulk, self.recv + recv, device)
+
     def start(self):
-        at, mail, s = self.at, self.mail, self.base
-        mail.post(self.half(1), self.block(0, 1), s, at.xn)
-        mail.post(self.half(0), self.block(0, 0), s + 1, at.yn)
-        mail.post(self.half(0), self.block(0, 0), s + 8, at.xn)
-        mail.post(self.half(1), self.block(0, 1), s + 9, at.yn)
-        mail.post(self.shard, self.block(0), s + 2, at.pn)
-        self.own = mail.bring(self.shard, self.block(0))
+        at = self.at
+        self.post(self.half(1), self.block(0, 1), 0, at.xn)
+        self.post(self.half(0), self.block(0, 0), 1, at.yn)
+        self.post(self.half(0), self.block(0, 0), 2, at.xn)
+        self.post(self.half(1), self.block(0, 1), 2, at.yn)
+        self.post(self.shard, self.block(0), 4, at.pn)
+        self.own = self.mail.bring(self.shard, self.block(0))
 
     def relay_y(self):
-        at, mail, s = self.at, self.mail, self.base
-        mail.arrived(self.block(2, 0), s + 1, at.yn)
-        mail.post(self.block(2, 0), self.block(2, 0), s + 3, at.xn)
+        self.arrived(self.block(2, 0), 1, self.at.yn)
+        self.post(self.block(2, 0), self.block(2, 0), 3, self.at.xn)
 
     def relay_x(self):
-        at, mail, s = self.at, self.mail, self.base
-        mail.arrived(self.block(4, 1), s, at.xn)
-        mail.post(self.block(4, 1), self.block(4, 1), s + 4, at.yn)
+        self.arrived(self.block(4, 1), 0, self.at.xn)
+        self.post(self.block(4, 1), self.block(4, 1), 3, self.at.yn)
 
     def share(self):
-        at, mail, s = self.at, self.mail, self.base
-        mail.arrived(self.block(2, 1), s + 9, at.yn)
-        mail.post(self.block(2), self.block(2), s + 5, at.pn)
-        mail.arrived(self.block(4, 0), s + 8, at.xn)
-        mail.post(self.block(4), self.block(4), s + 6, at.pn)
+        self.arrived(self.bulk(1), 2, self.at.xn)
+        self.post(self.block(2), self.block(2), 4, self.at.pn)
+        self.post(self.block(4), self.block(4), 4, self.at.pn)
 
     def far(self):
-        at, mail, s = self.at, self.mail, self.base
-        mail.arrived(self.block(6, 0), s + 3, at.xn)
-        mail.arrived(self.block(6, 1), s + 4, at.yn)
-        mail.post(self.block(6), self.block(6), s + 7, at.pn)
+        self.arrived(self.block(6), 3, self.at.xn)
+        self.post(self.block(6), self.block(6), 4, self.at.pn)
 
     def finish(self):
-        at, mail, s = self.at, self.mail, self.base
-        mail.arrived(self.block(1), s + 2, at.pn)
-        mail.arrived(self.block(3), s + 5, at.pn)
-        mail.arrived(self.block(5), s + 6, at.pn)
-        mail.arrived(self.block(7), s + 7, at.pn)
+        self.arrived(self.bulk(4), 4, self.at.pn)
         self.own.wait()
+
+    def close(self):
+        self.mail.gone(self.bulk(7), self.send, self.at.pn)
 
 
 class LineGather:
     def __init__(self, at, mail, held, first=0, count=None):
         self.at, self.mail, self.held = at, mail, held
         self.rows = pl.ds(first, held.shape[1] - first if count is None else count)
-        self.up, self.down = mail.slots(at.planes), mail.slots(at.planes)
+        self.send, self.recv = mail.send_slots(2), mail.recv_slots(at.planes)
 
     def part(self, slot):
         return self.held.at[slot, self.rows]
@@ -595,11 +618,11 @@
 
         @pl.when((slot <= at.b) & (at.b < at.planes - 1))
         def _():
-            self.mail.copy(src, part, self.up + slot, at.along(1)).start()
+            self.mail.copy(src, part, self.send, self.recv + slot, at.along(1)).start()
 
         @pl.when((slot >= at.b) & (at.b > 0))
         def _():
-            self.mail.copy(src, part, self.down + slot, at.along(-1)).start()
+            self.mail.copy(src, part, self.send + 1, self.recv + slot, at.along(-1)).start()
 
     def start(self, src=None):
         self.pass_on(self.at.b, src)
@@ -610,168 +633,158 @@
         @pl.when(at.b >= distance)
         def _():
             slot = at.b - distance
-            self.mail.arrived(self.part(slot), self.up + slot, at.along(-1))
+            self.mail.arrived(self.part(slot), self.recv + slot, at.along(-1))
             self.pass_on(slot)
 
         @pl.when(at.b + distance < at.planes)
         def _():
             slot = at.b + distance
-            self.mail.arrived(self.part(slot), self.down + slot, at.along(1))
+            self.mail.arrived(self.part(slot), self.recv + slot, at.along(1))
             self.pass_on(slot)
 
     def close(self):
         at = self.at
-        for slot in range(at.planes):
-            part = self.part(slot)
-
-            @pl.when((slot <= at.b) & (at.b < at.planes - 1))
+        for b in range(at.planes):
+
+            @pl.when(at.b == b)
             def _():
-                self.mail.copy(part, part, self.up + slot, at.along(1)).wait_send()
-
-            @pl.when((slot >= at.b) & (at.b > 0))
-            def _():
-                self.mail.copy(part, part, self.down + slot, at.along(-1)).wait_send()
+                if b < at.planes - 1:
+                    bulk = self.held.at[pl.ds(0, b + 1), self.rows]
+                    self.mail.gone(bulk, self.send, at.along(1))
+                if b > 0:
+                    bulk = self.held.at[pl.ds(0, at.planes - b), self.rows]
+                    self.mail.gone(bulk, self.send + 1, at.along(-1))
 
 
 class StarGather:
     def __init__(self, at, mail, held):
         self.at, self.mail, self.held = at, mail, held
-        self.base = mail.slots(2 * at.planes)
-
-    def each(self, action):
+        self.send, self.recv = mail.send_slots(), mail.recv_slots()
+
+    def start(self):
         at = self.at
+        part = self.held.at[at.b]
         for step in range(1, at.planes):
 
             @pl.when(at.b + step < at.planes)
             def _():
-                action(step, self.base + step)
+                self.mail.copy(part, part, self.send, self.recv, at.along(step)).start()
 
             @pl.when(at.b >= step)
             def _():
-                action(-step, self.base + at.planes + step)
+                self.mail.copy(part, part, self.send, self.recv, at.along(-step)).start()
+
+    def bulk(self):
+        return self.held.at[pl.ds(0, self.at.planes - 1)]
+
+    def finish(self):
+        self.mail.arrived(self.bulk(), self.recv, self.at.pn)
+
+    def close(self):
+        self.mail.gone(self.bulk(), self.send, self.at.pn)
+
+
+class PlaneExchange:
+    def __init__(self, at, mail, pieces, landings, bulk):
+        self.at, self.mail, self.bulk = at, mail, bulk
+        self.pieces, self.landings = pieces, landings
+        self.send, self.recv = mail.send_slots(), mail.recv_slots()
 
     def start(self):
-        part = self.held.at[self.at.b]
-        self.each(
-            lambda step, slot: self.mail.copy(part, part, slot, self.at.along(step)).start()
-        )
-
-    def finish(self):
-        n = self.at.planes
-        for step in range(1, n):
-
-            @pl.when(self.at.b + step < n)
-            def _():
-                part = self.held.at[self.at.b + step]
-                self.mail.arrived(part, self.base + n + step, self.at.along(step))
-
-            @pl.when(self.at.b >= step)
-            def _():
-                part = self.held.at[self.at.b - step]
-                self.mail.arrived(part, self.base + step, self.at.along(-step))
-
-    def close(self):
-        part = self.held.at[self.at.b]
-        self.each(
-            lambda step, slot: self.mail.copy(part, part, slot, self.at.along(step)).wait_send()
-        )
-
-
-class PlaneExchange:
-    def __init__(self, at, mail, pieces, landings, parts=1):
-        self.at, self.mail, self.parts = at, mail, parts
-        self.pieces = (lambda rank: [pieces(rank)]) if parts == 1 else pieces
-        self.landings = (lambda rank: [landings(rank)]) if parts == 1 else landings
-        self.base = mail.slots(8 * parts)
-
-    def start(self):
-        at, n = self.at, self.parts
+        at = self.at
         for d in range(1, 8):
-            for i, (piece, landing) in enumerate(
-                zip(self.pieces(at.rank(d)), self.landings(at.t))
-            ):
-                self.mail.post(piece, landing, self.base + d * n + i, at.peer(d))
+            for piece, landing in zip(self.pieces(at.rank(d)), self.landings(at.t)):
+                self.mail.copy(piece, landing, self.send, self.recv, at.peer(d)).start()
         self.own = [
             self.mail.bring(piece, landing)
             for piece, landing in zip(self.pieces(at.t), self.landings(at.t))
         ]
 
     def finish(self):
-        at, n = self.at, self.parts
-        for d in range(1, 8):
-            for i, landing in enumerate(self.landings(at.rank(d))):
-                self.mail.arrived(landing, self.base + d * n + i, at.peer(d))
+        self.mail.arrived(self.bulk, self.recv, self.at.pn)
         for own in self.own:
             own.wait()
+
+    def close(self):
+        self.mail.gone(self.bulk, self.send, self.at.pn)
 
 
 class PairExchange:
     def __init__(self, at, mail, src, dst, landed):
         self.at, self.mail, self.src, self.dst, self.landed = at, mail, src, dst, landed
-        self.base = mail.slots(1)
+        self.send, self.recv = mail.send_slots(), mail.recv_slots()
 
     def start(self):
-        self.mail.post(self.src, self.dst, self.base, self.at.pn)
+        self.mail.copy(self.src, self.dst, self.send, self.recv, self.at.pn).start()
 
     def finish(self):
-        self.mail.arrived(self.landed, self.base, self.at.pn)
+        self.mail.arrived(self.landed, self.recv, self.at.pn)
+
+    def close(self):
+        self.mail.gone(self.src, self.send, self.at.pn)
 
 
 class PlaneReduce:
-    def __init__(self, at, mail, terms, pairs, sums, side):
-        self.at, self.mail, self.terms = at, mail, terms
+    def __init__(self, at, mail, terms, pairs, sums, side, bulk):
+        self.at, self.mail, self.terms, self.bulk = at, mail, terms, bulk
         self.pairs, self.sums, self.side = pairs, sums, side
-        self.base = mail.slots(8)
-        self.order = (6, 4, 2, 0)
+        self.send, self.recv = mail.send_slots(), mail.recv_slots(5)
         self.halves = terms.shape[0] // 2
+
+    def post(self, src, dst, recv, device):
+        self.mail.copy(src, dst, self.send, self.recv + recv, device).start()
 
     def start(self):
         at = self.at
-        for i, d in enumerate(self.order):
+        for d in (6, 4, 2, 0):
             chip = at.chip(d)
-            self.mail.post(
-                self.terms.at[:, chip, 1 - at.c], self.pairs.at[:, chip], self.base + i, at.pn
+            self.post(
+                self.terms.at[:, chip, 1 - at.c], self.pairs.at[:, chip], 0 if d == 6 else 1, at.pn
             )
 
     def half(self, ref, i):
         return ref.at[pl.ds(i * self.halves, self.halves)]
 
+    def add_pair(self, d):
+        chip = self.at.chip(d)
+        total = self.terms[:, chip, self.at.c].astype(jnp.float32) + self.pairs[:, chip].astype(
+            jnp.float32
+        )
+        self.sums[:, chip] = total.astype(self.sums.dtype)
+
     def fold(self):
-        at, mail, s = self.at, self.mail, self.base
-        for i, d in enumerate(self.order):
-            chip = at.chip(d)
-            mail.arrived(self.pairs.at[:, chip], s + i, at.pn)
-            total = self.terms[:, chip, at.c].astype(jnp.float32) + self.pairs[:, chip].astype(
-                jnp.float32
-            )
-            self.sums[:, chip] = total.astype(self.sums.dtype)
-            if d == 6:
-                far = self.sums.at[:, chip]
-                mail.post(self.half(far, 0), self.half(self.side.at[0], 0), s + 4, at.xn)
-                mail.post(self.half(far, 1), self.half(self.side.at[0], 1), s + 5, at.yn)
+        at = self.at
+        far = self.sums.at[:, at.chip(6)]
+        self.mail.arrived(self.bulk(1), self.recv, at.pn)
+        self.add_pair(6)
+        self.post(self.half(far, 0), self.half(self.side.at[0], 0), 2, at.xn)
+        self.post(self.half(far, 1), self.half(self.side.at[0], 1), 3, at.yn)
+        self.mail.arrived(self.bulk(3), self.recv + 1, at.pn)
+        for d in (4, 2, 0):
+            self.add_pair(d)
 
     def turn(self):
-        at, mail, s = self.at, self.mail, self.base
-        for i, d, other, slot, nbr in ((1, 4, at.yn, 5, at.xn), (0, 2, at.xn, 4, at.yn)):
-            chip = at.chip(d)
+        at = self.at
+        for i, d, other, recv, nbr in ((1, 4, at.yn, 3, at.xn), (0, 2, at.xn, 2, at.yn)):
             landed = self.half(self.side.at[0], i)
-            mail.arrived(landed, s + slot, other)
-            part = self.half(self.sums.at[:, chip], i)
+            self.mail.arrived(landed, self.recv + recv, other)
+            whole = self.sums.at[:, at.chip(d)]
+            part = self.half(whole, i)
             part[...] = (part[...].astype(jnp.float32) + landed[...].astype(jnp.float32)).astype(
                 self.sums.dtype
             )
-            whole = self.sums.at[:, chip]
-            mail.post(whole, self.side.at[2 - i], s + 6 + i, nbr)
+            self.post(whole, self.side.at[2 - i], 4, nbr)
 
     def finish(self):
-        at, mail, s = self.at, self.mail, self.base
-        mail.arrived(self.side.at[1], s + 7, at.xn)
-        mail.arrived(self.side.at[2], s + 6, at.yn)
+        self.mail.arrived(self.bulk(2), self.recv + 4, self.at.xn)
         return (
-            self.sums[:, at.chip(0)].astype(jnp.float32)
+            self.sums[:, self.at.chip(0)].astype(jnp.float32)
             + self.side[1].astype(jnp.float32)
             + self.side[2].astype(jnp.float32)
         )
+
+    def close(self):
+        self.mail.gone(self.bulk(7), self.send, self.at.pn)
 
 
 class LineReduce:
@@ -780,62 +793,79 @@
         self.above, self.below = above, below
         whole = pl.ds(0, terms.shape[2])
         self.up_cut, self.down_cut = up_cut or whole, down_cut or whole
-        self.up, self.down = mail.slots(at.planes), mail.slots(at.planes)
+        self.send, self.recv = mail.send_slots(2), mail.recv_slots(at.planes + 1)
+
+    def upward(self, src, slot):
+        return self.mail.copy(
+            src.at[slot, :, self.up_cut],
+            self.below.at[slot, :, self.up_cut],
+            self.send,
+            self.recv + slot,
+            self.at.along(1),
+        )
+
+    def downward(self, src, slot, last_step):
+        return self.mail.copy(
+            src.at[slot, :, self.down_cut],
+            self.above.at[slot, :, self.down_cut],
+            self.send + 1,
+            self.recv + (self.at.planes if last_step else slot),
+            self.at.along(-1),
+        )
 
     def edge(self, slot):
         at, last = self.at, self.at.planes - 1
-
-        @pl.when((at.b == 0) & (slot > 0))
+        if slot == 0:
+            return
+
+        @pl.when(at.b == 0)
         def _():
-            self.mail.copy(
-                self.terms.at[slot, :, self.up_cut],
-                self.below.at[slot, :, self.up_cut],
-                self.up + slot,
-                at.along(1),
-            ).start()
-
-        @pl.when((at.b == last) & (slot < last))
+            self.upward(self.terms, slot).start()
+
+        @pl.when(at.b == last)
         def _():
-            self.mail.copy(
-                self.terms.at[slot, :, self.down_cut],
-                self.above.at[slot, :, self.down_cut],
-                self.down + slot,
-                at.along(-1),
-            ).start()
+            self.downward(self.terms, last - slot, slot == 1).start()
 
     def hop(self, hop, rank):
-        last = self.at.planes - 1
-        if last - rank > hop:
-            self._forward(last - rank, self.below, self.up_cut, self.up, 1, self.at.b == hop)
-            self._forward(rank, self.above, self.down_cut, self.down, -1, self.at.b == last - hop)
-
-    def _forward(self, slot, held, cut, base, step, here):
-        at, mail = self.at, self.mail
-        part = held.at[slot, :, cut]
-
-        @pl.when(here)
+        at, mail, last = self.at, self.mail, self.at.planes - 1
+        slot = last - rank
+        if slot <= hop:
+            return
+
+        @pl.when(at.b == hop)
         def _():
-            mail.arrived(part, base + slot, at.along(-step))
-            total = self.terms[slot, :, cut].astype(jnp.float32) + held[slot, :, cut].astype(
-                jnp.float32
-            )
-            held[slot, :, cut] = total.astype(held.dtype)
-            mail.copy(part, part, base + slot, at.along(step)).start()
+            cut = self.up_cut
+            mail.arrived(self.below.at[slot, :, cut], self.recv + slot, at.along(-1))
+            self.add(self.below, slot, cut)
+            self.upward(self.below, slot).start()
+
+        @pl.when(at.b == last - hop)
+        def _():
+            cut = self.down_cut
+            mail.arrived(self.above.at[rank, :, cut], self.recv + rank, at.along(1))
+            self.add(self.above, rank, cut)
+            self.downward(self.above, rank, rank == last - hop - 1).start()
+
+    def add(self, held, slot, cut):
+        total = self.terms[slot, :, cut].astype(jnp.float32) + held[slot, :, cut].astype(
+            jnp.float32
+        )
+        held[slot, :, cut] = total.astype(held.dtype)
 
     def landed(self):
         at, mail = self.at, self.mail
 
         @pl.when(at.b > 0)
         def _():
-            mail.arrived(self.below.at[at.b, :, self.up_cut], self.up + at.b, at.along(-1))
+            mail.arrived(self.below.at[at.b, :, self.up_cut], self.recv + at.b, at.along(-1))
 
         @pl.when(at.b < at.planes - 1)
         def _():
-            mail.arrived(self.above.at[at.b, :, self.down_cut], self.down + at.b, at.along(1))
+            bulk = self.above.at[at.b, :, self.down_cut]
+            mail.arrived(bulk, self.recv + at.planes, at.along(1))
 
     def total(self, out):
-        at = self.at
-        b, last = at.b, at.planes - 1
+        b, last = self.at.b, self.at.planes - 1
 
         def put(*parts):
             value = self.terms[b].astype(jnp.float32)
@@ -856,17 +886,17 @@
             put(self.below, self.above)
 
     def close(self):
-        at = self.at
-        for slot in range(at.planes):
-            up, down = self.terms.at[slot, :, self.up_cut], self.terms.at[slot, :, self.down_cut]
-
-            @pl.when(at.b < slot)
+        at, last = self.at, self.at.planes - 1
+        for b in range(at.planes):
+
+            @pl.when(at.b == b)
             def _():
-                self.mail.copy(up, up, self.up + slot, at.along(1)).wait_send()
-
-            @pl.when(at.b > slot)
-            def _():
-                self.mail.copy(down, down, self.down + slot, at.along(-1)).wait_send()
+                if b < last:
+                    bulk = self.terms.at[pl.ds(0, last - b), :, self.up_cut]
+                    self.mail.gone(bulk, self.send, at.along(1))
+                if b > 0:
+                    bulk = self.terms.at[pl.ds(0, b), :, self.down_cut]
+                    self.mail.gone(bulk, self.send + 1, at.along(-1))
 
 
 TILE = 256
@@ -1212,7 +1242,7 @@
             own[seq] = raw[:, seq, :]
 
     def own_rows(self, ref, rank):
-        rows = self.out.shape[1]
+        rows = self.out.shape[0]
         return ref[:, pl.ds(pl.multiple_of(rank * rows, rows), rows), :].astype(jnp.float32)
 
     def small_terms(self, rank):
@@ -1240,21 +1270,23 @@
         inverse = lax.rsqrt(jnp.mean(shifted * shifted, axis=2, keepdims=True) + EPSILON)
         normed = shifted * inverse
         bias = (self.wide(0) + self.wide(5))[None]
-        self.out[...] = (x + out_sum + bias).astype(jnp.bfloat16)
-        self.in_grad[...] = self.own_rows(self.ca, rank) + inverse * (
+        value = (x + out_sum + bias).astype(jnp.bfloat16)
+        grad = self.own_rows(self.ca, rank) + inverse * (
             in_sum
             - jnp.mean(in_sum, axis=2, keepdims=True)
             - normed * jnp.mean(in_sum * normed, axis=2, keepdims=True)
         )
-
-
-LAYER_SLOTS = 5 * 8 + 4 + 12 * 8 + 10 * 8 + 2
-NEAR_SLOTS = 24
+        for seq in range(x.shape[0]):
+            self.out[:, seq, :] = value[seq]
+            self.in_grad[:, seq, :] = grad[seq]
+
+
+SEND_SLOTS, RECV_SLOTS, NEAR_SLOTS = 37, 80, 22
 
 
 def layer_kernel(names, planes, *refs):
     refs = dict(zip(names, refs))
-    send, recv, near = (refs.pop(name) for name in names[-3:])
+    send, recv, near, second, third = (refs.pop(name) for name in names[-5:])
     refs.update(
         tables=tuple(refs["table"].at[i] for i in range(3)),
         probs=tuple(refs[name] for name in names if name.startswith("probs")),
@@ -1267,12 +1299,16 @@
     b, c = at.b, at.c
     rows = do.wq_s.shape[1]
     pair = planes // 2
+    others = pl.ds(0, 7)
+
+    def shards(n):
+        return do.xa.at[:, pl.ds(0, n * do.x_own.shape[1]), :]
 
     def strip(whole):
-        return lambda rank: whole.at[b, pl.ds(pl.multiple_of(rank * rows, rows), rows), :]
+        return lambda rank: [whole.at[b, pl.ds(pl.multiple_of(rank * rows, rows), rows), :]]
 
     def band(whole):
-        return lambda rank: whole.at[pl.ds(pl.multiple_of(rank * rows, rows), rows), :]
+        return lambda rank: [whole.at[pl.ds(pl.multiple_of(rank * rows, rows), rows), :]]
 
     def up_pieces(rank):
         return [
@@ -1294,18 +1330,20 @@
     half = do.wd.shape[1] // 2
     line_da = LineGather(at, mail, do.wd, 0, half)
     line_db = LineGather(at, mail, do.wd, half, half)
-    ex_v = PlaneExchange(at, mail, lambda rank: do.vec_s, lambda rank: do.vec_in.at[rank])
-    ex_q = PlaneExchange(at, mail, lambda rank: do.wq_s.at[rank], strip(do.wq))
-    ex_u = PlaneExchange(at, mail, up_pieces, up_landings, planes)
+    ex_v = PlaneExchange(at, mail, lambda rank: [do.vec_s], lambda rank: [do.vec_in.at[rank]], do.vec_in.at[others])
+    ex_q = PlaneExchange(
+        at, mail, lambda rank: [do.wq_s.at[rank]], strip(do.wq), do.wq_s.at[others]
+    )
+    ex_u = PlaneExchange(at, mail, up_pieces, up_landings, do.wu.at[0, pl.ds(0, 7 * rows)])
     mine = do.wo2.at[:, c]
     swap_w = PairExchange(
         at, mail, do.wo.at[pl.ds(pair * (1 - c), pair)], mine, do.wo2.at[:, 1 - c]
     )
     sum_o = LineReduce(at, mail, do.go4, do.above_o, do.below_o)
     sum_q = LineReduce(at, mail, do.gq, do.above_q, do.below_q)
-    first, second = (pl.ds(i * do.hidden // 2, do.hidden // 2) for i in range(2))
-    sum_un = LineReduce(at, mail, do.gu, do.above_u, do.below_u, first, second)
-    sum_uf = LineReduce(at, mail, do.gu, do.above_u, do.below_u, second, first)
+    low, high = (pl.ds(i * do.hidden // 2, do.hidden // 2) for i in range(2))
+    sum_un = LineReduce(at, mail, do.gu, do.above_u, do.below_u, low, high)
+    sum_uf = LineReduce(at, mail, do.gu, do.above_u, do.below_u, high, low)
     near_side = b // pair
     far_side = 1 - near_side
     sum_d = LineReduce(at, mail, do.gd, do.above_d, do.below_d)
@@ -1316,163 +1354,176 @@
         do.go4.at[pl.ds(pair * c, pair)],
         do.go4.at[pl.ds(pair * (1 - c), pair)],
     )
-    back_q = PlaneExchange(at, mail, band(do.fq), lambda rank: do.dq.at[rank])
-    back_u = PlaneExchange(at, mail, band(do.fu), lambda rank: do.du.at[rank])
-    fold_v = PlaneExchange(at, mail, lambda rank: do.sm.at[rank], lambda rank: do.sm_in.at[rank])
+    back_q = PlaneExchange(
+        at, mail, band(do.fq), lambda rank: [do.dq.at[rank]], do.fq.at[pl.ds(0, 7 * rows)]
+    )
+    back_u = PlaneExchange(
+        at, mail, band(do.fu), lambda rank: [do.du.at[rank]], do.fu.at[pl.ds(0, 7 * rows)]
+    )
+    fold_v = PlaneExchange(
+        at, mail, lambda rank: [do.sm.at[rank]], lambda rank: [do.sm_in.at[rank]], do.sm.at[others]
+    )
     line_s = StarGather(at, mail, do.vz)
-    share_v = PlaneExchange(at, mail, lambda rank: do.vt, lambda rank: do.dv.at[rank])
-    plane_o = PlaneReduce(at, mail, do.po, do.pairs_o, do.sums_o, do.side_o)
-    plane_g = PlaneReduce(at, mail, do.pg, do.pairs_g, do.sums_g, do.side_g)
+    share_v = PlaneExchange(
+        at, mail, lambda rank: [do.vt], lambda rank: [do.dv.at[rank]], do.dv.at[others]
+    )
+    plane_o = PlaneReduce(at, mail, do.po, do.pairs_o, do.sums_o, do.side_o, shards)
+    plane_g = PlaneReduce(at, mail, do.pg, do.pairs_g, do.sums_g, do.side_g, shards)
 
     slots = [s + b // pair * (planes - 1 - 2 * s) for s in (3, 0, 2, 1)]
 
     at.barrier()
+    at.reach(second, third)
     line_da.start(do.wd_s)
     own_d = mail.bring(do.wd_s, do.wd.at[b])
+    ex_u.start()
     raw_x = mail.bring(do.x_in, do.x_raw)
-    ex_u.start()
+    own_raw = mail.bring(do.wq_in, do.wq_raw)
     line_db.start(do.wd_s)
+    raw_c = mail.bring(do.cot_in, do.cot_raw)
+    do.own_vectors(at.t)
+    ex_v.start()
+    raw_x.wait()
+    do.split(do.x_raw, do.x_own)
     line_o.start(do.wo_s)
     own_o = mail.bring(do.wo_s, do.wo.at[b])
-    raw_x.wait()
-    do.split(do.x_raw, do.x_own)
-    own_raw = mail.bring(do.wq_in, do.wq_raw)
     gather_x.start()
-    own_o.wait()
     ex_u.finish()
     line_ua.start()
-    raw_c = mail.bring(do.cot_in, do.cot_raw)
-    own_table = mail.bring(do.table_in, do.table)
-    do.own_vectors(at.t)
-    ex_v.start()
     gather_x.relay_x()
     line_ub.start()
     own_raw.wait()
     do.sort_weight()
     ex_q.start()
-    own_table.wait()
     gather_x.relay_y()
     line_ua.take(1)
     raw_c.wait()
     do.split(do.cot_raw, do.cot_own)
+    own_table = mail.bring(do.table_in, do.table)
     ex_v.finish()
     do.plane_vectors(b)
     line_v.start()
+    gather_c.start()
+    line_ub.take(1)
     gather_x.share()
-    line_ub.take(1)
     gather_x.far()
-    gather_c.start()
     line_ua.take(2)
-    own_d.wait()
     gather_x.finish()
     do.statistics()
+    gather_c.relay_x()
+    line_ub.take(2)
     line_v.finish()
-    do.activations()
-    line_ub.take(2)
-    gather_c.relay_x()
-    do.expand_near(near_side)
-    gather_c.relay_y()
     ex_q.finish()
     line_q.start()
+    gather_c.relay_y()
+    do.activations()
     line_o.take(1)
     gather_c.share()
+    do.expand_near(near_side)
     line_ub.take(3)
     line_ua.take(3)
     gather_c.far()
     do.expand(at.t, far_side)
     gather_c.finish()
     do.down_weight_grad(slots[0])
-    sum_d.edge(slots[0])
+    sum_d.edge(3)
+    own_o.wait()
+    line_o.take(2)
     line_q.take(1)
     do.down_weight_grad(slots[1])
-    sum_d.edge(slots[1])
-    do.down_weight_grad(slots[2])
-    sum_d.edge(slots[2])
-    do.down_weight_grad(slots[3])
-    sum_d.edge(slots[3])
-    line_o.take(2)
+    sum_d.edge(0)
+    own_d.wait()
     line_o.take(3)
     swap_w.start()
     mine[...] = do.wo[pl.ds(pair * c, pair)]
+    do.down_weight_grad(slots[2])
+    sum_d.edge(2)
+    swap_w.finish()
     do.project_near(near_side)
-    swap_w.finish()
     do.attend_out_grad()
     line_q.take(2)
+    own_table.wait()
+    line_da.take(1)
     line_db.take(1)
-    line_da.take(1)
     do.hidden_grad(near_side)
     do.up_weight_grad(slots[0], near_side)
-    sum_un.edge(slots[0])
+    sum_un.edge(3)
+    do.down_weight_grad(slots[3])
+    sum_d.edge(1)
+    do.up_weight_grad(slots[1], near_side)
+    sum_un.edge(0)
+    sum_d.hop(1, 0)
     line_q.take(3)
     do.project(at.t, far_side)
+    do.up_weight_grad(slots[2], near_side)
+    sum_un.edge(2)
     do.attend(0)
+    do.attend_grad(0)
+    line_da.take(2)
+    line_db.take(2)
     do.attend(1)
-    do.dense_weight_grad()
-    swap_g.start()
-    do.go4[pl.ds(pair * c, pair)] = do.go[:, c]
-    line_da.take(2)
-    do.up_weight_grad(slots[1], near_side)
-    sum_un.edge(slots[1])
-    do.up_weight_grad(slots[2], near_side)
-    sum_un.edge(slots[2])
-    do.attend_grad(0)
+    do.up_weight_grad(slots[3], near_side)
+    sum_un.edge(1)
+    line_da.take(3)
+    sum_un.hop(1, 0)
     do.attend_grad(1)
     do.qkv_weight_grad(slots[0])
-    sum_q.edge(slots[0])
-    do.up_weight_grad(slots[3], near_side)
-    sum_un.edge(slots[3])
-    line_da.take(3)
-    line_db.take(2)
+    sum_q.edge(3)
+    do.qkv_weight_grad(slots[1])
+    sum_q.edge(0)
     line_db.take(3)
-    sum_d.hop(1, 0)
     do.out_terms(0)
     do.out_terms(1)
+    sum_d.hop(1, 1)
     do.out_terms(2)
     do.out_terms(3)
     plane_o.start()
     do.hidden_grad(far_side)
     do.up_weight_grad(slots[0], far_side)
-    sum_uf.edge(slots[0])
+    sum_uf.edge(3)
+    sum_d.hop(2, 0)
     do.up_weight_grad(slots[1], far_side)
-    sum_uf.edge(slots[1])
+    sum_uf.edge(0)
     do.up_weight_grad(slots[2], far_side)
-    sum_uf.edge(slots[2])
-    do.up_weight_grad(slots[3], far_side)
-    sum_uf.edge(slots[3])
-    sum_d.hop(1, 1)
+    sum_uf.edge(2)
     plane_o.fold()
-    do.qkv_weight_grad(slots[1])
-    sum_q.edge(slots[1])
+    do.in_terms(0)
+    do.in_terms(1)
+    plane_o.turn()
     do.qkv_weight_grad(slots[2])
-    sum_q.edge(slots[2])
-    do.qkv_weight_grad(slots[3])
-    sum_q.edge(slots[3])
-    do.in_terms(0)
-    sum_q.hop(1, 0)
-    plane_o.turn()
-    do.in_terms(1)
+    sum_q.edge(2)
+    sum_un.hop(1, 1)
     do.in_terms(2)
     do.in_terms(3)
     plane_g.start()
-    sum_un.hop(1, 0)
-    sum_d.hop(2, 0)
+    do.up_weight_grad(slots[3], far_side)
+    sum_uf.edge(1)
+    sum_uf.hop(1, 0)
+    do.qkv_weight_grad(slots[3])
+    sum_q.edge(1)
+    sum_q.hop(1, 0)
     plane_g.fold()
-    sum_uf.hop(1, 0)
-    sum_un.hop(2, 0)
-    sum_uf.hop(1, 1)
     do.small_terms(at.t)
     fold_v.start()
-    sum_un.hop(1, 1)
     sum_uf.hop(2, 0)
+    sum_uf.hop(1, 1)
+    sum_un.hop(2, 0)
     plane_g.turn()
+    do.dense_weight_grad()
+    swap_g.start()
+    do.go4[pl.ds(pair * c, pair)] = do.go[:, c]
+    sum_q.hop(2, 0)
     fold_v.finish()
     do.small_plane(b)
     line_s.start()
+    swap_g.finish()
+    sum_o.edge(3)
+    sum_o.edge(2)
+    sum_o.edge(1)
+    sum_d.landed()
+    sum_d.total(do.dd)
+    out_d = mail.bring(do.dd, do.dd_to)
     sum_q.hop(1, 1)
-    swap_g.finish()
-    for slot in slots:
-        sum_o.edge(slot)
-    sum_q.hop(2, 0)
     sum_un.landed()
     sum_uf.landed()
     sum_un.total(do.fu)
@@ -1488,33 +1539,47 @@
     sum_q.total(do.fq)
     back_q.start()
     sum_o.hop(1, 1)
-    sum_d.landed()
-    sum_d.total(do.dd)
-    out_d = mail.bring(do.dd, do.dd_to)
+    back_u.finish()
     sum_o.hop(2, 0)
-    back_u.finish()
-    share_v.finish()
     sum_o.landed()
     sum_o.total(do.dd_o)
     out_o = mail.bring(do.dd_o, do.dd_o_to)
+    share_v.finish()
     back_q.finish()
     for copied in (out_o, out_d, out_x, out_g):
         copied.wait()
-    mail.close()
-    for line in (line_v, line_o, line_q, line_ua, line_ub, line_da, line_db, line_s, sum_o, sum_q, sum_un, sum_uf, sum_d):
+    for line in (gather_x, gather_c, line_v, line_o, line_q, line_ua, line_ub, line_da, line_db, line_s, ex_v, ex_q, ex_u, back_q, back_u, fold_v, share_v, swap_w, swap_g, plane_o, plane_g, sum_o, sum_q, sum_un, sum_uf, sum_d):
         line.close()
 
 
 def finish_kernel(names, planes, *refs):
-    do = Layer(dict(zip(names, refs)))
+    refs = dict(zip(names, refs))
+    near = refs.pop(names[-1])
+    do = Layer(refs)
     at = Place(planes)
     ranks, rows = do.dq.shape[:2]
-    lane = lax.broadcasted_iota(jnp.int32, (rows, LANES), 1)
-    low = lane < HD
+    moves = []
+
+    def move(src, dst):
+        moves.append(pltpu.make_async_copy(src, dst, near.at[len(moves)]))
+        moves[-1].start()
+
+    move(do.in_grad, do.in_grad_out)
+    move(do.dd, do.down_out)
+    move(do.out, do.out_out)
+    move(do.dd_o, do.dense_out)
+    for rank in range(ranks):
+        for b in range(planes):
+            first = (b * ranks + rank) * LANES
+            do.up_v[:, first : first + LANES] = do.du[
+                rank, :, b * LANES : (b + 1) * LANES
+            ].astype(jnp.float32)
+    move(do.up_v, do.up_out)
+    low = lax.broadcasted_iota(jnp.int32, (rows, LANES), 1) < HD
     for part in range(3):
         for core in range(2):
             for pair in range(ranks // 4):
-                near, far = (
+                first, second = (
                     do.dq[2 * (2 * pair + i) + core, :, part * LANES : (part + 1) * LANES].astype(
                         jnp.float32
                     )
@@ -1522,23 +1587,13 @@
                 )
                 for j in range(2):
                     both = (
-                        jnp.where(low, near, pltpu.roll(far, HD, 1))
+                        jnp.where(low, first, pltpu.roll(second, HD, 1))
                         if j == 0
-                        else jnp.where(low, pltpu.roll(near, HD, 1), far)
+                        else jnp.where(low, pltpu.roll(first, HD, 1), second)
                     )
-                    first = (part * 4 + core * 2 + j) * ranks // 2 * HD + pair * LANES
-                    do.qkv_out[:, first : first + LANES] = both
-    for rank in range(ranks):
-        for b in range(planes):
-            first = (b * ranks + rank) * LANES
-            do.up_out[:, first : first + LANES] = do.du[
-                rank, :, b * LANES : (b + 1) * LANES
-            ].astype(jnp.float32)
-    do.down_out[...] = do.dd[...]
-    do.dense_out[...] = do.dd_o[...]
-    for seq in range(do.out.shape[0]):
-        do.in_grad_out[:, seq, :] = do.in_grad[seq]
-        do.out_out[:, seq, :] = do.out[seq]
+                    start = (part * 4 + core * 2 + j) * ranks // 2 * HD + pair * LANES
+                    do.qkv_v[:, start : start + LANES] = both
+    move(do.qkv_v, do.qkv_out)
     piece = lax.rem(at.t, 4)
     row = (at.b * ranks + at.t) // 4
     values = do.dv[pl.ds(row, 1), 0:8, :].reshape(8, LANES)
@@ -1566,6 +1621,8 @@
             total = total + jnp.where(spot == k, cut, jnp.zeros_like(cut))
         pieces.append(total)
     do.qkv_bias[...] = jnp.concatenate(pieces, axis=1).reshape(3 * rows)
+    for made in moves:
+        made.wait()
 
 
 VMEM = pl.BlockSpec(memory_space=pltpu.VMEM)
@@ -1632,14 +1689,15 @@
     owner = lax.axis_index(BATCH) * ranks + rank
 
     anywhere = pl.BlockSpec(memory_space=pl.ANY)
+    in_hbm = pl.BlockSpec(memory_space=pltpu.HBM)
     inputs = dict(
-        x_in=(residual_in, anywhere),
-        cot_in=(cotangent, anywhere),
-        wq_in=(qkv_weight, anywhere),
-        wu_s=(up_weight, anywhere),
-        wd_s=(down_weight, anywhere),
-        wo_s=(dense_weight, anywhere),
-        table_in=(jnp.asarray(rotary_rows(length)), anywhere),
+        x_in=(residual_in, in_hbm),
+        cot_in=(cotangent, in_hbm),
+        wq_in=(qkv_weight, in_hbm),
+        wu_s=(up_weight, in_hbm),
+        wd_s=(down_weight, in_hbm),
+        wo_s=(dense_weight, in_hbm),
+        table_in=(jnp.asarray(rotary_rows(length)), in_hbm),
         b_qkv=(qkv_bias, VMEM),
         b_up=(up_bias, VMEM),
     )
@@ -1647,8 +1705,8 @@
         inputs["vector%d" % i] = (v, VMEM)
     shard = (seqs, tok_rows, width)
     outputs = dict(
-        out_to=(shard, half_type),
-        in_grad_to=(shard, single),
+        out_to=(residual_in.shape, half_type),
+        in_grad_to=(residual_in.shape, single),
         dq=((ranks, rows, 3 * LANES), half_type),
         du=((ranks, rows, hidden), half_type),
         dd_to=((depth, width), single),
@@ -1676,8 +1734,8 @@
         wq_raw=(qkv_weight.shape, half_type),
         wq_s=((ranks, rows, 3 * LANES), half_type),
         table=((3, length, LANES), single),
-        out=(shard, half_type),
-        in_grad=(shard, single),
+        out=(residual_in.shape, half_type),
+        in_grad=(residual_in.shape, single),
         dd=((depth, width), single),
         dd_o=((rows, width), single),
         vec_s=((16, LANES), single),
@@ -1727,18 +1785,23 @@
     )
     for block in range(length // TILE):
         scratch["probs%d" % block] = ((seqs * LANES // HD, TILE, (block + 1) * TILE), single)
-    names = tuple(inputs) + tuple(outputs) + tuple(scratch) + ("send", "recv", "near")
+    names = tuple(inputs) + tuple(outputs) + tuple(scratch) + ("send", "recv", "near", "second", "third")
     out, in_grad, dq, du, dd, dd_o, dv = pl.pallas_call(
         functools.partial(layer_kernel, names, planes),
         out_shape=[jax.ShapeDtypeStruct(*what) for what in outputs.values()],
         in_specs=[where for _, where in inputs.values()],
         out_specs=[anywhere] * len(outputs),
         scratch_shapes=[pltpu.VMEM(*what) for what in scratch.values()]
-        + [pltpu.SemaphoreType.DMA((n,)) for n in (LAYER_SLOTS, LAYER_SLOTS, NEAR_SLOTS)],
+        + [pltpu.SemaphoreType.DMA((n,)) for n in (SEND_SLOTS, RECV_SLOTS, NEAR_SLOTS)]
+        + [pltpu.SemaphoreType.REGULAR] * 2,
         compiler_params=pltpu.CompilerParams(
-            collective_id=0, has_side_effects=True, vmem_limit_bytes=60 * 2**20
+            collective_id=0, has_side_effects=True, vmem_limit_bytes=52 * 2**20
         ),
-    )(*(value for value, _ in inputs.values()))
+    )(
+        *(
+            pltpu.with_memory_space_constraint(value, pltpu.HBM) for value, _ in inputs.values()
+        )
+    )
 
     results = dict(
         out_out=(residual_in.shape, half_type),
@@ -1756,14 +1819,19 @@
         down_out=(down_weight.shape, single),
         down_bias=(down_bias.shape, single),
     )
+    given = tuple(n.removesuffix("_to") for n in outputs)
+    staged = dict(up_v=results["up_out"], qkv_v=results["qkv_out"])
     return tuple(
         pl.pallas_call(
             functools.partial(
-                finish_kernel, tuple(n.removesuffix("_to") for n in outputs) + tuple(results), planes
+                finish_kernel, given + tuple(results) + tuple(staged) + ("near",), planes
             ),
             out_shape=[jax.ShapeDtypeStruct(*what) for what in results.values()],
-            in_specs=[VMEM] * len(outputs),
-            out_specs=[VMEM] * len(results),
+            in_specs=[VMEM] * len(given),
+            out_specs=[anywhere if len(what[0]) > 1 else VMEM for what in results.values()],
+            scratch_shapes=[pltpu.VMEM(*what) for what in staged.values()]
+            + [pltpu.SemaphoreType.DMA((8,))],
+            compiler_params=pltpu.CompilerParams(vmem_limit_bytes=8 * 2**20),
         )(out, in_grad, dq, du, dd, dd_o, dv)
     )
 

time: 103 us -> 98.3 us (0.954)
  Pallas kernels: 103 us -> 97.4 us
    pallas_call x1, Pallas kernels: 99.4 us -> 95.2 us  [fast_body(): pl.pallas_call(functools.partial(layer_kernel, names, planes), out_shape=...]
    pallas_call x1, Pallas kernels: 3.18 us -> 2.11 us  [fast_body(): pl.pallas_call(functools.partial(finish_kernel, given + tuple(results) +...]
where the time goes in v5:
time: 98.3 us; the launch traced here: 98.2 us
  Pallas kernels  97.4 us (99%)
    pallas_call x1, Pallas kernels, fast_body(): pl.pallas_call(functools.partial(layer_kernel, names, planes), out_shape=...  95.2 us
    pallas_call x1, Pallas kernels, fast_body(): pl.pallas_call(functools.partial(finish_kernel, given + tuple(results) +...  2.11 us

profile of v5, /device:TPU:0, one launch (start us, length us, event | category | flops | bytes accessed | tf_op | source)
XLA Modules:
  0.0 98.2 jit_solution(8103183622804473512)
XLA Ops:
  0.7 95.2 %shard_map.254 = (bf16[64,2,1024]{2,1,0:T(2,128)(2,1)S(1)}, f32[64,2,1024]{2,1,0:T(2,128)S(1)}, bf16[8,32,384]{2,1,0:T(8,128)(2,1)S(1)}, bf16[8,32,512]{2,1,0:T(...) custom-call(bf16[64,2,1024]{2,1,0:T(2,128)(2,1)} %refs_0_.1, ...), custom_call_target="tpu_custom_call" | custom-call | tf_op jit(solution)/shard_map/pallas_call | solution.py:1789
  95.9 2.1 %shard_map.255 = (bf16[64,2,1024]{2,1,0:T(2,128)(2,1)}, f32[64,2,1024]{2,1,0:T(2,128)}, f32[32,3072]{1,0:T(8,128)}, f32[96]{0:T(128)}, f32[32,1024]{1,0:T(8,128)...) custom-call(bf16[64,2,1024]{2,1,0:T(2,128)(2,1)S(1)} %get-tuple-elem, ...), custom_call_target="tpu_custom_call" | custom-call | tf_op jit(solution)/shard_map/pallas_call | solution.py:1825

commit v6 on v5

--- a/solution.py
+++ b/solution.py
@@ -603,44 +603,72 @@
 
 
 class LineGather:
-    def __init__(self, at, mail, held, first=0, count=None):
+    def __init__(self, at, mail, held, up_cut=None, down_cut=None):
         self.at, self.mail, self.held = at, mail, held
-        self.rows = pl.ds(first, held.shape[1] - first if count is None else count)
+        whole = tuple(pl.ds(0, n) for n in held.shape[1:])
+        self.up_cut, self.down_cut = up_cut or whole, down_cut or whole
         self.send, self.recv = mail.send_slots(2), mail.recv_slots(at.planes)
 
-    def part(self, slot):
-        return self.held.at[slot, self.rows]
-
-    def pass_on(self, slot, src=None):
+    def upward(self, slot, src):
+        part = self.held.at[(slot,) + self.up_cut]
+        src = part if src is None else src.at[self.up_cut]
+        return self.mail.copy(src, part, self.send, self.recv + slot, self.at.along(1))
+
+    def downward(self, slot, src):
+        part = self.held.at[(slot,) + self.down_cut]
+        src = part if src is None else src.at[self.down_cut]
+        return self.mail.copy(src, part, self.send + 1, self.recv + slot, self.at.along(-1))
+
+    def start(self, src=None):
         at = self.at
-        part = self.part(slot)
-        src = part if src is None else src.at[self.rows]
-
-        @pl.when((slot <= at.b) & (at.b < at.planes - 1))
+
+        @pl.when(at.b < at.planes - 1)
         def _():
-            self.mail.copy(src, part, self.send, self.recv + slot, at.along(1)).start()
-
-        @pl.when((slot >= at.b) & (at.b > 0))
+            self.upward(at.b, src).start()
+
+        @pl.when(at.b > 0)
         def _():
-            self.mail.copy(src, part, self.send + 1, self.recv + slot, at.along(-1)).start()
-
-    def start(self, src=None):
-        self.pass_on(self.at.b, src)
+            self.downward(at.b, src).start()
+
+    def from_below(self, distance, here):
+        at = self.at
+        slot = at.b - distance
+
+        @pl.when((slot >= 0) & here)
+        def _():
+            part = self.held.at[(slot,) + self.up_cut]
+            self.mail.arrived(part, self.recv + slot, at.along(-1))
+
+            @pl.when(at.b < at.planes - 1)
+            def _():
+                self.upward(slot, None).start()
+
+    def from_above(self, distance, here):
+        at = self.at
+        slot = at.b + distance
+
+        @pl.when((slot < at.planes) & here)
+        def _():
+            part = self.held.at[(slot,) + self.down_cut]
+            self.mail.arrived(part, self.recv + slot, at.along(1))
+
+            @pl.when(at.b > 0)
+            def _():
+                self.downward(slot, None).start()
 
     def take(self, distance):
-        at = self.at
-
-        @pl.when(at.b >= distance)
-        def _():
-            slot = at.b - distance
-            self.mail.arrived(self.part(slot), self.recv + slot, at.along(-1))
-            self.pass_on(slot)
-
-        @pl.when(at.b + distance < at.planes)
-        def _():
-            slot = at.b + distance
-            self.mail.arrived(self.part(slot), self.recv + slot, at.along(1))
-            self.pass_on(slot)
+        self.from_below(distance, self.at.b >= 0)
+        self.from_above(distance, self.at.b >= 0)
+
+    def inner(self, distance):
+        middle = self.at.planes // 2
+        self.from_below(distance, self.at.b >= middle)
+        self.from_above(distance, self.at.b < middle)
+
+    def outer(self, distance):
+        middle = self.at.planes // 2
+        self.from_below(distance, self.at.b < middle)
+        self.from_above(distance, self.at.b >= middle)
 
     def close(self):
         at = self.at
@@ -649,10 +677,10 @@
             @pl.when(at.b == b)
             def _():
                 if b < at.planes - 1:
-                    bulk = self.held.at[pl.ds(0, b + 1), self.rows]
+                    bulk = self.held.at[(pl.ds(0, b + 1),) + self.up_cut]
                     self.mail.gone(bulk, self.send, at.along(1))
                 if b > 0:
-                    bulk = self.held.at[pl.ds(0, at.planes - b), self.rows]
+                    bulk = self.held.at[(pl.ds(0, at.planes - b),) + self.down_cut]
                     self.mail.gone(bulk, self.send + 1, at.along(-1))
 
 
@@ -1044,11 +1072,6 @@
                 )
             )
         return jnp.concatenate(pieces, axis=1)
-
-    def up_bias(self, rank):
-        return jnp.concatenate(
-            [self.va[b, pl.ds(24 + rank, 1), :] for b in range(self.va.shape[0])], axis=1
-        )
 
     def near(self, ref, side):
         both = ref[pl.ds(side * 2, 2)]
@@ -1164,25 +1187,19 @@
             dot_tn(self.attn[...], self.cot_flat()).astype(jnp.bfloat16).reshape(self.go.shape)
         )
 
-    def expand_near(self, side):
+    def expand(self, rank, side):
+        cut = self.half_columns(side, self.hidden)
+        slots = self.va.shape[0] // 2
+        bias = jnp.concatenate(
+            [self.va[side * slots + i, pl.ds(24 + rank, 1), :] for i in range(slots)], axis=1
+        )
+
         def step(i):
-            cut = self.half_columns(side, self.width)
-            self.slope[self.rows(i), :] = dot_nn(
-                self.act_two[self.rows(i), cut], self.near(self.wu, side)
-            )
-
-        self.loop(self.tiles, step)
-
-    def expand(self, rank, side):
-        bias = self.up_bias(rank)
-
-        def step(i):
-            cut = self.half_columns(side, self.width)
-            pre = dot_nn(self.act_two[self.rows(i), cut], self.near(self.wu, side))
-            pre = pre + self.slope[self.rows(i), :] + bias
+            weight = self.wu[:, :, cut].reshape(self.width, self.hidden // 2)
+            pre = dot_nn(self.act_two[self.rows(i), :], weight) + bias
             cdf = 0.5 * (1.0 + lax.erf(pre * INV_ROOT_TWO))
-            self.gelu[self.rows(i), :] = (pre * cdf).astype(jnp.bfloat16)
-            self.slope[self.rows(i), :] = cdf + pre * jnp.exp(-0.5 * pre * pre) * INV_ROOT_TWO_PI
+            self.gelu[self.rows(i), cut] = (pre * cdf).astype(jnp.bfloat16)
+            self.slope[self.rows(i), cut] = cdf + pre * jnp.exp(-0.5 * pre * pre) * INV_ROOT_TWO_PI
 
         self.loop(self.tiles, step)
 
@@ -1324,12 +1341,14 @@
     gather_c = PlaneGather(at, mail, do.cot_own, do.ca)
     line_v, line_o = StarGather(at, mail, do.va), LineGather(at, mail, do.wo)
     line_q = LineGather(at, mail, do.wq)
-    half = do.wu.shape[1] // 2
-    line_ua = LineGather(at, mail, do.wu, 0, half)
-    line_ub = LineGather(at, mail, do.wu, half, half)
+    low, high = (pl.ds(i * do.hidden // 2, do.hidden // 2) for i in range(2))
+    all_rows = pl.ds(0, do.wu.shape[1])
+    line_ua = LineGather(at, mail, do.wu, (all_rows, low), (all_rows, high))
+    line_ub = LineGather(at, mail, do.wu, (all_rows, high), (all_rows, low))
     half = do.wd.shape[1] // 2
-    line_da = LineGather(at, mail, do.wd, 0, half)
-    line_db = LineGather(at, mail, do.wd, half, half)
+    cuts = [(pl.ds(i * half, half), pl.ds(0, do.wd.shape[2])) for i in range(2)]
+    line_da = LineGather(at, mail, do.wd, cuts[0], cuts[0])
+    line_db = LineGather(at, mail, do.wd, cuts[1], cuts[1])
     ex_v = PlaneExchange(at, mail, lambda rank: [do.vec_s], lambda rank: [do.vec_in.at[rank]], do.vec_in.at[others])
     ex_q = PlaneExchange(
         at, mail, lambda rank: [do.wq_s.at[rank]], strip(do.wq), do.wq_s.at[others]
@@ -1341,7 +1360,6 @@
     )
     sum_o = LineReduce(at, mail, do.go4, do.above_o, do.below_o)
     sum_q = LineReduce(at, mail, do.gq, do.above_q, do.below_q)
-    low, high = (pl.ds(i * do.hidden // 2, do.hidden // 2) for i in range(2))
     sum_un = LineReduce(at, mail, do.gu, do.above_u, do.below_u, low, high)
     sum_uf = LineReduce(at, mail, do.gu, do.above_u, do.below_u, high, low)
     near_side = b // pair
@@ -1371,159 +1389,167 @@
     plane_g = PlaneReduce(at, mail, do.pg, do.pairs_g, do.sums_g, do.side_g, shards)
 
     slots = [s + b // pair * (planes - 1 - 2 * s) for s in (3, 0, 2, 1)]
+    turned = [s + b // pair * (planes - 1 - 2 * s) for s in (3, 2, 1, 0)]
 
     at.barrier()
-    at.reach(second, third)
     line_da.start(do.wd_s)
     own_d = mail.bring(do.wd_s, do.wd.at[b])
+    raw_x = mail.bring(do.x_in, do.x_raw)
     ex_u.start()
-    raw_x = mail.bring(do.x_in, do.x_raw)
-    own_raw = mail.bring(do.wq_in, do.wq_raw)
     line_db.start(do.wd_s)
-    raw_c = mail.bring(do.cot_in, do.cot_raw)
+    at.reach(second, third)
     do.own_vectors(at.t)
     ex_v.start()
+    line_o.start(do.wo_s)
+    own_o = mail.bring(do.wo_s, do.wo.at[b])
     raw_x.wait()
     do.split(do.x_raw, do.x_own)
-    line_o.start(do.wo_s)
-    own_o = mail.bring(do.wo_s, do.wo.at[b])
     gather_x.start()
     ex_u.finish()
     line_ua.start()
     gather_x.relay_x()
+    gather_x.relay_y()
+    own_raw = mail.bring(do.wq_in, do.wq_raw)
+    ex_v.finish()
+    do.plane_vectors(b)
+    line_v.start()
+    raw_c = mail.bring(do.cot_in, do.cot_raw)
     line_ub.start()
+    own_o.wait()
     own_raw.wait()
     do.sort_weight()
     ex_q.start()
-    gather_x.relay_y()
-    line_ua.take(1)
+    line_ua.inner(1)
     raw_c.wait()
     do.split(do.cot_raw, do.cot_own)
+    gather_x.share()
+    line_ua.outer(1)
+    line_v.finish()
+    gather_x.far()
+    gather_c.start()
     own_table = mail.bring(do.table_in, do.table)
-    ex_v.finish()
-    do.plane_vectors(b)
-    line_v.start()
-    gather_c.start()
-    line_ub.take(1)
-    gather_x.share()
-    gather_x.far()
-    line_ua.take(2)
+    line_ub.outer(1)
+    line_ub.inner(1)
     gather_x.finish()
     do.statistics()
+    do.activations()
+    line_ua.inner(2)
+    line_o.take(1)
+    gather_c.relay_y()
+    own_d.wait()
+    line_ub.inner(2)
     gather_c.relay_x()
-    line_ub.take(2)
-    line_v.finish()
     ex_q.finish()
     line_q.start()
-    gather_c.relay_y()
-    do.activations()
-    line_o.take(1)
     gather_c.share()
-    do.expand_near(near_side)
-    line_ub.take(3)
-    line_ua.take(3)
+    line_ua.inner(3)
+    do.expand(at.t, far_side)
     gather_c.far()
-    do.expand(at.t, far_side)
+    own_table.wait()
+    line_o.take(2)
     gather_c.finish()
-    do.down_weight_grad(slots[0])
+    do.down_weight_grad(turned[0])
     sum_d.edge(3)
-    own_o.wait()
-    line_o.take(2)
+    do.down_weight_grad(turned[1])
+    sum_d.edge(2)
+    line_ub.inner(3)
     line_q.take(1)
-    do.down_weight_grad(slots[1])
+    do.expand(at.t, near_side)
+    do.down_weight_grad(turned[2])
+    sum_d.edge(1)
+    do.down_weight_grad(turned[3])
     sum_d.edge(0)
-    own_d.wait()
     line_o.take(3)
     swap_w.start()
     mine[...] = do.wo[pl.ds(pair * c, pair)]
-    do.down_weight_grad(slots[2])
-    sum_d.edge(2)
+    do.project_near(near_side)
     swap_w.finish()
-    do.project_near(near_side)
     do.attend_out_grad()
     line_q.take(2)
-    own_table.wait()
     line_da.take(1)
     line_db.take(1)
     do.hidden_grad(near_side)
     do.up_weight_grad(slots[0], near_side)
     sum_un.edge(3)
-    do.down_weight_grad(slots[3])
-    sum_d.edge(1)
     do.up_weight_grad(slots[1], near_side)
     sum_un.edge(0)
-    sum_d.hop(1, 0)
+    do.up_weight_grad(slots[2], near_side)
+    sum_un.edge(2)
+    do.up_weight_grad(slots[3], near_side)
+    sum_un.edge(1)
     line_q.take(3)
     do.project(at.t, far_side)
-    do.up_weight_grad(slots[2], near_side)
-    sum_un.edge(2)
     do.attend(0)
+    do.attend(1)
+    do.dense_weight_grad()
+    swap_g.start()
+    do.go4[pl.ds(pair * c, pair)] = do.go[:, c]
     do.attend_grad(0)
+    sum_d.hop(1, 0)
+    do.attend_grad(1)
     line_da.take(2)
-    line_db.take(2)
-    do.attend(1)
-    do.up_weight_grad(slots[3], near_side)
-    sum_un.edge(1)
-    line_da.take(3)
-    sum_un.hop(1, 0)
-    do.attend_grad(1)
     do.qkv_weight_grad(slots[0])
     sum_q.edge(3)
     do.qkv_weight_grad(slots[1])
     sum_q.edge(0)
+    do.qkv_weight_grad(slots[2])
+    sum_q.edge(2)
+    do.qkv_weight_grad(slots[3])
+    sum_q.edge(1)
+    line_db.take(2)
+    line_da.take(3)
     line_db.take(3)
     do.out_terms(0)
     do.out_terms(1)
-    sum_d.hop(1, 1)
+    sum_un.hop(1, 0)
     do.out_terms(2)
     do.out_terms(3)
     plane_o.start()
     do.hidden_grad(far_side)
     do.up_weight_grad(slots[0], far_side)
     sum_uf.edge(3)
-    sum_d.hop(2, 0)
+    sum_d.hop(1, 1)
     do.up_weight_grad(slots[1], far_side)
     sum_uf.edge(0)
+    plane_o.fold()
+    do.in_terms(0)
+    sum_d.hop(2, 0)
     do.up_weight_grad(slots[2], far_side)
     sum_uf.edge(2)
-    plane_o.fold()
-    do.in_terms(0)
+    plane_o.turn()
+    sum_q.hop(1, 0)
     do.in_terms(1)
-    plane_o.turn()
-    do.qkv_weight_grad(slots[2])
-    sum_q.edge(2)
-    sum_un.hop(1, 1)
     do.in_terms(2)
     do.in_terms(3)
     plane_g.start()
     do.up_weight_grad(slots[3], far_side)
     sum_uf.edge(1)
-    sum_uf.hop(1, 0)
-    do.qkv_weight_grad(slots[3])
-    sum_q.edge(1)
-    sum_q.hop(1, 0)
-    plane_g.fold()
+    sum_q.hop(1, 1)
+    sum_q.hop(2, 0)
     do.small_terms(at.t)
     fold_v.start()
-    sum_uf.hop(2, 0)
-    sum_uf.hop(1, 1)
     sum_un.hop(2, 0)
+    sum_un.hop(1, 1)
+    plane_g.fold()
+    sum_uf.hop(1, 0)
+    sum_q.landed()
+    sum_q.total(do.fq)
+    back_q.start()
     plane_g.turn()
-    do.dense_weight_grad()
-    swap_g.start()
-    do.go4[pl.ds(pair * c, pair)] = do.go[:, c]
-    sum_q.hop(2, 0)
     fold_v.finish()
     do.small_plane(b)
     line_s.start()
+    sum_uf.hop(1, 1)
+    sum_d.landed()
+    sum_d.total(do.dd)
+    out_d = mail.bring(do.dd, do.dd_to)
     swap_g.finish()
     sum_o.edge(3)
     sum_o.edge(2)
     sum_o.edge(1)
-    sum_d.landed()
-    sum_d.total(do.dd)
-    out_d = mail.bring(do.dd, do.dd_to)
-    sum_q.hop(1, 1)
+    sum_uf.hop(2, 0)
+    back_q.finish()
+    sum_o.hop(1, 0)
     sum_un.landed()
     sum_uf.landed()
     sum_un.total(do.fu)
@@ -1531,21 +1557,16 @@
     do.result(at.t, plane_o.finish(), plane_g.finish())
     out_x = mail.bring(do.out, do.out_to)
     out_g = mail.bring(do.in_grad, do.in_grad_to)
+    sum_o.hop(1, 1)
+    sum_o.hop(2, 0)
     line_s.finish()
-    sum_o.hop(1, 0)
     do.vt[...] = jnp.sum(do.vz[...], axis=0)
     share_v.start()
-    sum_q.landed()
-    sum_q.total(do.fq)
-    back_q.start()
-    sum_o.hop(1, 1)
-    back_u.finish()
-    sum_o.hop(2, 0)
     sum_o.landed()
     sum_o.total(do.dd_o)
     out_o = mail.bring(do.dd_o, do.dd_o_to)
+    back_u.finish()
     share_v.finish()
-    back_q.finish()
     for copied in (out_o, out_d, out_x, out_g):
         copied.wait()
     for line in (gather_x, gather_c, line_v, line_o, line_q, line_ua, line_ub, line_da, line_db, line_s, ex_v, ex_q, ex_u, back_q, back_u, fold_v, share_v, swap_w, swap_g, plane_o, plane_g, sum_o, sum_q, sum_un, sum_uf, sum_d):

time: 98.3 us -> 95.4 us (0.970)
  Pallas kernels: 97.4 us -> 94.4 us
    pallas_call x1, Pallas kernels: 95.2 us -> 92.2 us  [fast_body(): pl.pallas_call(functools.partial(layer_kernel, names, planes), out_shape=...]
where the time goes in v6:
time: 95.4 us; the launch traced here: 95.2 us
  Pallas kernels  94.4 us (99%)
    pallas_call x1, Pallas kernels, fast_body(): pl.pallas_call(functools.partial(layer_kernel, names, planes), out_shape=...  92.2 us
    pallas_call x1, Pallas kernels, fast_body(): pl.pallas_call(functools.partial(finish_kernel, given + tuple(results) +...  2.11 us

profile of v6, /device:TPU:0, one launch (start us, length us, event | category | flops | bytes accessed | tf_op | source)
XLA Modules:
  0.0 95.2 jit_solution(5449979110470469156)
XLA Ops:
  0.7 92.2 %shard_map.254 = (bf16[64,2,1024]{2,1,0:T(2,128)(2,1)S(1)}, f32[64,2,1024]{2,1,0:T(2,128)S(1)}, bf16[8,32,384]{2,1,0:T(8,128)(2,1)S(1)}, bf16[8,32,512]{2,1,0:T(...) custom-call(bf16[64,2,1024]{2,1,0:T(2,128)(2,1)} %refs_0_.1, ...), custom_call_target="tpu_custom_call" | custom-call | tf_op jit(solution)/shard_map/pallas_call | solution.py:1810
  92.9 2.1 %shard_map.255 = (bf16[64,2,1024]{2,1,0:T(2,128)(2,1)}, f32[64,2,1024]{2,1,0:T(2,128)}, f32[32,3072]{1,0:T(8,128)}, f32[96]{0:T(128)}, f32[32,1024]{1,0:T(8,128)...) custom-call(bf16[64,2,1024]{2,1,0:T(2,128)(2,1)S(1)} %get-tuple-elem, ...), custom_call_target="tpu_custom_call" | custom-call | tf_op jit(solution)/shard_map/pallas_call | solution.py:1846

commit v7 on v6

--- a/solution.py
+++ b/solution.py
@@ -756,19 +756,18 @@
     def __init__(self, at, mail, terms, pairs, sums, side, bulk):
         self.at, self.mail, self.terms, self.bulk = at, mail, terms, bulk
         self.pairs, self.sums, self.side = pairs, sums, side
-        self.send, self.recv = mail.send_slots(), mail.recv_slots(5)
+        self.send, self.recv = mail.send_slots(), mail.recv_slots(6)
         self.halves = terms.shape[0] // 2
 
     def post(self, src, dst, recv, device):
         self.mail.copy(src, dst, self.send, self.recv + recv, device).start()
 
-    def start(self):
+    def start(self, *chips):
         at = self.at
-        for d in (6, 4, 2, 0):
+        for d in chips:
             chip = at.chip(d)
-            self.post(
-                self.terms.at[:, chip, 1 - at.c], self.pairs.at[:, chip], 0 if d == 6 else 1, at.pn
-            )
+            recv = {6: 0, 4: 1}.get(d, 5)
+            self.post(self.terms.at[:, chip, 1 - at.c], self.pairs.at[:, chip], recv, at.pn)
 
     def half(self, ref, i):
         return ref.at[pl.ds(i * self.halves, self.halves)]
@@ -780,28 +779,38 @@
         )
         self.sums[:, chip] = total.astype(self.sums.dtype)
 
-    def fold(self):
+    def fold_far(self):
         at = self.at
         far = self.sums.at[:, at.chip(6)]
         self.mail.arrived(self.bulk(1), self.recv, at.pn)
         self.add_pair(6)
         self.post(self.half(far, 0), self.half(self.side.at[0], 0), 2, at.xn)
         self.post(self.half(far, 1), self.half(self.side.at[0], 1), 3, at.yn)
-        self.mail.arrived(self.bulk(3), self.recv + 1, at.pn)
-        for d in (4, 2, 0):
-            self.add_pair(d)
-
-    def turn(self):
-        at = self.at
-        for i, d, other, recv, nbr in ((1, 4, at.yn, 3, at.xn), (0, 2, at.xn, 2, at.yn)):
-            landed = self.half(self.side.at[0], i)
-            self.mail.arrived(landed, self.recv + recv, other)
-            whole = self.sums.at[:, at.chip(d)]
-            part = self.half(whole, i)
-            part[...] = (part[...].astype(jnp.float32) + landed[...].astype(jnp.float32)).astype(
-                self.sums.dtype
-            )
-            self.post(whole, self.side.at[2 - i], 4, nbr)
+
+    def fold_x(self):
+        self.mail.arrived(self.bulk(1), self.recv + 1, self.at.pn)
+        self.add_pair(4)
+
+    def fold_near(self):
+        self.mail.arrived(self.bulk(2), self.recv + 5, self.at.pn)
+        self.add_pair(2)
+        self.add_pair(0)
+
+    def turn_x(self):
+        self.turn(1, 4, self.at.yn, 3, self.at.xn)
+
+    def turn_y(self):
+        self.turn(0, 2, self.at.xn, 2, self.at.yn)
+
+    def turn(self, i, d, other, recv, nbr):
+        landed = self.half(self.side.at[0], i)
+        self.mail.arrived(landed, self.recv + recv, other)
+        whole = self.sums.at[:, self.at.chip(d)]
+        part = self.half(whole, i)
+        part[...] = (part[...].astype(jnp.float32) + landed[...].astype(jnp.float32)).astype(
+            self.sums.dtype
+        )
+        self.post(whole, self.side.at[2 - i], 4, nbr)
 
     def finish(self):
         self.mail.arrived(self.bulk(2), self.recv + 4, self.at.xn)
@@ -1240,19 +1249,38 @@
             dot_nn(self.attn[self.rows(i), :], dense) + dot_nn(self.gelu[self.rows(i), :], down),
         )
 
-    def in_terms(self, i):
-        gain_one, gain_two = self.wide(1), self.wide(3)
-        normed = self.normed(i)
+    def in_terms_one(self, i, first):
+        gain = self.wide(1)
         weight = self.wq[...].reshape(self.width, 3 * LANES)
-        one = dot_nt(self.qkv_grad[self.rows(i), :], weight)
+        value = dot_nt(self.qkv_grad[self.rows(i), :], weight)
+        self.park(i, value * gain)
+        self.add_sums(0, value, self.normed(i), first)
+
+    def in_terms_two(self, i, first):
+        gain = self.wide(3)
         weight = self.wu[...].reshape(self.width, self.hidden)
-        two = dot_nt(self.pre_grad[self.rows(i), :], weight)
-        self.put_terms(self.pg, i, one * gain_one + two * gain_two)
-        for j, value in enumerate((one * normed, one, two * normed, two)):
-            if i == 0:
-                self.sums[j : j + 1, :] = total_rows(value)
+        value = dot_nt(self.pre_grad[self.rows(i), :], weight)
+        self.put_terms(self.pg, i, self.parked(i) + value * gain)
+        self.add_sums(2, value, self.normed(i), first)
+
+    def park(self, i, value):
+        quarter = self.width // 4
+        self.probs[1][i] = value[:, : 2 * quarter]
+        self.probs[0][i] = value[:, 2 * quarter : 3 * quarter]
+        self.qkv[self.rows(i), :quarter] = value[:, 3 * quarter :]
+
+    def parked(self, i):
+        quarter = self.width // 4
+        return jnp.concatenate(
+            [self.probs[1][i], self.probs[0][i], self.qkv[self.rows(i), :quarter]], axis=1
+        )
+
+    def add_sums(self, row, value, normed, first):
+        for j, sums in ((row, total_rows(value * normed)), (row + 1, total_rows(value))):
+            if first:
+                self.sums[j : j + 1, :] = sums
             else:
-                self.sums[j : j + 1, :] += total_rows(value)
+                self.sums[j : j + 1, :] += sums
 
     def split(self, raw, own):
         for seq in range(own.shape[0]):
@@ -1298,7 +1326,7 @@
             self.in_grad[:, seq, :] = grad[seq]
 
 
-SEND_SLOTS, RECV_SLOTS, NEAR_SLOTS = 37, 80, 22
+SEND_SLOTS, RECV_SLOTS, NEAR_SLOTS = 37, 82, 30
 
 
 def layer_kernel(names, planes, *refs):
@@ -1310,6 +1338,8 @@
         vectors=tuple(refs[name] for name in names if name.startswith("vector")),
         hidden=refs["gelu"].shape[1],
     )
+    given = [refs["in_qkv"], refs["in_up"]]
+    given += [refs[name] for name in names if name.startswith("in_vector")]
     do = Layer(refs)
     at = Place(planes)
     mail = Mail(send, recv, near)
@@ -1389,85 +1419,89 @@
     plane_g = PlaneReduce(at, mail, do.pg, do.pairs_g, do.sums_g, do.side_g, shards)
 
     slots = [s + b // pair * (planes - 1 - 2 * s) for s in (3, 0, 2, 1)]
+    tiles = [seq * 2 + half for half in (1 - at.u, at.u) for seq in range(2)]
     turned = [s + b // pair * (planes - 1 - 2 * s) for s in (3, 2, 1, 0)]
 
     at.barrier()
+    own_v = [mail.bring(src, dst) for src, dst in zip(given, [do.b_qkv, do.b_up, *do.vectors])]
     line_da.start(do.wd_s)
     own_d = mail.bring(do.wd_s, do.wd.at[b])
     raw_x = mail.bring(do.x_in, do.x_raw)
+    at.reach(second, third)
     ex_u.start()
     line_db.start(do.wd_s)
-    at.reach(second, third)
+    raw_x.wait()
+    do.split(do.x_raw, do.x_own)
+    own_raw = mail.bring(do.wq_in, do.wq_raw)
+    line_o.start(do.wo_s)
+    own_o = mail.bring(do.wo_s, do.wo.at[b])
+    gather_x.start()
+    raw_c = mail.bring(do.cot_in, do.cot_raw)
+    own_table = mail.bring(do.table_in, do.table)
+    ex_u.finish()
+    line_ua.start()
+    for made in own_v:
+        made.wait()
     do.own_vectors(at.t)
     ex_v.start()
-    line_o.start(do.wo_s)
-    own_o = mail.bring(do.wo_s, do.wo.at[b])
-    raw_x.wait()
-    do.split(do.x_raw, do.x_own)
-    gather_x.start()
-    ex_u.finish()
-    line_ua.start()
+    line_o.take(1)
     gather_x.relay_x()
     gather_x.relay_y()
-    own_raw = mail.bring(do.wq_in, do.wq_raw)
+    own_raw.wait()
+    do.sort_weight()
+    ex_q.start()
+    line_ua.outer(1)
+    line_ua.inner(1)
+    gather_x.share()
+    raw_c.wait()
+    do.split(do.cot_raw, do.cot_own)
     ex_v.finish()
     do.plane_vectors(b)
     line_v.start()
-    raw_c = mail.bring(do.cot_in, do.cot_raw)
     line_ub.start()
-    own_o.wait()
-    own_raw.wait()
-    do.sort_weight()
-    ex_q.start()
-    line_ua.inner(1)
-    raw_c.wait()
-    do.split(do.cot_raw, do.cot_own)
-    gather_x.share()
-    line_ua.outer(1)
-    line_v.finish()
     gather_x.far()
     gather_c.start()
-    own_table = mail.bring(do.table_in, do.table)
-    line_ub.outer(1)
-    line_ub.inner(1)
+    line_o.take(2)
+    own_table.wait()
+    line_ua.inner(2)
     gather_x.finish()
     do.statistics()
+    line_v.finish()
     do.activations()
-    line_ua.inner(2)
-    line_o.take(1)
+    line_ub.outer(1)
+    gather_c.relay_x()
+    line_o.take(3)
     gather_c.relay_y()
-    own_d.wait()
-    line_ub.inner(2)
-    gather_c.relay_x()
+    line_ub.inner(1)
     ex_q.finish()
     line_q.start()
+    own_o.wait()
+    swap_w.start()
+    mine[...] = do.wo[pl.ds(pair * c, pair)]
+    line_ua.inner(3)
     gather_c.share()
-    line_ua.inner(3)
     do.expand(at.t, far_side)
     gather_c.far()
-    own_table.wait()
-    line_o.take(2)
+    line_ub.inner(2)
+    own_d.wait()
+    swap_w.finish()
     gather_c.finish()
     do.down_weight_grad(turned[0])
     sum_d.edge(3)
+    line_q.take(1)
     do.down_weight_grad(turned[1])
     sum_d.edge(2)
     line_ub.inner(3)
-    line_q.take(1)
     do.expand(at.t, near_side)
     do.down_weight_grad(turned[2])
     sum_d.edge(1)
     do.down_weight_grad(turned[3])
     sum_d.edge(0)
-    line_o.take(3)
-    swap_w.start()
-    mine[...] = do.wo[pl.ds(pair * c, pair)]
     do.project_near(near_side)
-    swap_w.finish()
     do.attend_out_grad()
     line_q.take(2)
+    line_db.take(1)
     line_da.take(1)
-    line_db.take(1)
     do.hidden_grad(near_side)
     do.up_weight_grad(slots[0], near_side)
     sum_un.edge(3)
@@ -1484,87 +1518,99 @@
     do.dense_weight_grad()
     swap_g.start()
     do.go4[pl.ds(pair * c, pair)] = do.go[:, c]
+    sum_d.hop(1, 0)
     do.attend_grad(0)
-    sum_d.hop(1, 0)
     do.attend_grad(1)
-    line_da.take(2)
     do.qkv_weight_grad(slots[0])
     sum_q.edge(3)
+    line_da.take(2)
+    line_da.take(3)
+    line_db.take(2)
+    do.in_terms_one(tiles[0], True)
+    do.in_terms_one(tiles[1], False)
+    line_db.take(3)
+    do.hidden_grad(far_side)
+    do.up_weight_grad(slots[0], far_side)
+    sum_uf.edge(3)
+    sum_d.hop(1, 1)
+    do.out_terms(tiles[0])
+    do.out_terms(tiles[1])
+    plane_o.start(6, 4)
+    do.in_terms_two(tiles[0], True)
+    do.in_terms_two(tiles[1], False)
+    plane_g.start(6, 4)
+    plane_o.fold_far()
+    do.up_weight_grad(slots[1], far_side)
+    sum_uf.edge(0)
+    do.up_weight_grad(slots[2], far_side)
+    sum_uf.edge(2)
+    do.up_weight_grad(slots[3], far_side)
+    sum_uf.edge(1)
+    do.out_terms(tiles[2])
+    do.out_terms(tiles[3])
+    plane_o.start(2, 0)
+    sum_un.hop(1, 0)
+    plane_g.fold_far()
     do.qkv_weight_grad(slots[1])
     sum_q.edge(0)
     do.qkv_weight_grad(slots[2])
     sum_q.edge(2)
+    swap_g.finish()
+    sum_o.edge(3)
     do.qkv_weight_grad(slots[3])
     sum_q.edge(1)
-    line_db.take(2)
-    line_da.take(3)
-    line_db.take(3)
-    do.out_terms(0)
-    do.out_terms(1)
-    sum_un.hop(1, 0)
-    do.out_terms(2)
-    do.out_terms(3)
-    plane_o.start()
-    do.hidden_grad(far_side)
-    do.up_weight_grad(slots[0], far_side)
-    sum_uf.edge(3)
-    sum_d.hop(1, 1)
-    do.up_weight_grad(slots[1], far_side)
-    sum_uf.edge(0)
-    plane_o.fold()
-    do.in_terms(0)
-    sum_d.hop(2, 0)
-    do.up_weight_grad(slots[2], far_side)
-    sum_uf.edge(2)
-    plane_o.turn()
+    sum_un.hop(1, 1)
+    plane_o.fold_x()
+    plane_o.turn_x()
+    plane_o.fold_near()
+    plane_o.turn_y()
+    do.in_terms_one(tiles[2], False)
     sum_q.hop(1, 0)
-    do.in_terms(1)
-    do.in_terms(2)
-    do.in_terms(3)
-    plane_g.start()
-    do.up_weight_grad(slots[3], far_side)
-    sum_uf.edge(1)
-    sum_q.hop(1, 1)
-    sum_q.hop(2, 0)
+    do.in_terms_two(tiles[2], False)
+    do.in_terms_one(tiles[3], False)
+    do.in_terms_two(tiles[3], False)
+    plane_g.start(2, 0)
+    plane_g.fold_x()
+    sum_uf.hop(1, 0)
+    sum_un.hop(2, 0)
     do.small_terms(at.t)
     fold_v.start()
-    sum_un.hop(2, 0)
-    sum_un.hop(1, 1)
-    plane_g.fold()
-    sum_uf.hop(1, 0)
-    sum_q.landed()
-    sum_q.total(do.fq)
-    back_q.start()
-    plane_g.turn()
+    sum_uf.hop(1, 1)
+    plane_g.turn_x()
+    plane_g.fold_near()
+    plane_g.turn_y()
+    sum_q.hop(2, 0)
+    sum_uf.hop(2, 0)
     fold_v.finish()
     do.small_plane(b)
     line_s.start()
-    sum_uf.hop(1, 1)
-    sum_d.landed()
-    sum_d.total(do.dd)
-    out_d = mail.bring(do.dd, do.dd_to)
-    swap_g.finish()
-    sum_o.edge(3)
+    sum_d.hop(2, 0)
     sum_o.edge(2)
-    sum_o.edge(1)
-    sum_uf.hop(2, 0)
-    back_q.finish()
-    sum_o.hop(1, 0)
+    sum_q.hop(1, 1)
     sum_un.landed()
     sum_uf.landed()
     sum_un.total(do.fu)
     back_u.start()
+    sum_o.edge(1)
+    sum_o.hop(1, 0)
     do.result(at.t, plane_o.finish(), plane_g.finish())
     out_x = mail.bring(do.out, do.out_to)
     out_g = mail.bring(do.in_grad, do.in_grad_to)
-    sum_o.hop(1, 1)
+    sum_q.landed()
+    sum_q.total(do.fq)
+    back_q.start()
     sum_o.hop(2, 0)
     line_s.finish()
+    sum_o.hop(1, 1)
     do.vt[...] = jnp.sum(do.vz[...], axis=0)
     share_v.start()
+    sum_d.landed()
+    sum_d.total(do.dd)
+    out_d = mail.bring(do.dd, do.dd_to)
     sum_o.landed()
     sum_o.total(do.dd_o)
     out_o = mail.bring(do.dd_o, do.dd_o_to)
+    back_q.finish()
     back_u.finish()
     share_v.finish()
     for copied in (out_o, out_d, out_x, out_g):
@@ -1669,10 +1715,10 @@
     fits = (
         (shape[ULY], shape[BLK]) == (2, 4)
         and planes == 4
-        and seqs % 2 == 0
+        and seqs == 2
         and 2 * qkv_weight.shape[0] == HD
-        and width == ranks * LANES
-        and ranks * tok_rows % TILE == 0
+        and width == ranks * LANES == 4 * TILE
+        and ranks * tok_rows == 2 * TILE
         and TILE % (2 * tok_rows) == 0
         and down_weight.shape[0] == LANES
     )
@@ -1719,11 +1765,11 @@
         wd_s=(down_weight, in_hbm),
         wo_s=(dense_weight, in_hbm),
         table_in=(jnp.asarray(rotary_rows(length)), in_hbm),
-        b_qkv=(qkv_bias, VMEM),
-        b_up=(up_bias, VMEM),
+        in_qkv=(qkv_bias, in_hbm),
+        in_up=(up_bias, in_hbm),
     )
     for i, v in enumerate((dense_bias, norm1_gain, norm1_bias, norm2_gain, norm2_bias, down_bias)):
-        inputs["vector%d" % i] = (v, VMEM)
+        inputs["in_vector%d" % i] = (v, in_hbm)
     shard = (seqs, tok_rows, width)
     outputs = dict(
         out_to=(residual_in.shape, half_type),
@@ -1747,6 +1793,8 @@
         wd=(d_shape, half_type),
         wo=(o_shape, half_type),
         wo2=((pair, 2, rows, width), half_type),
+        b_qkv=(qkv_bias.shape, half_type),
+        b_up=(up_bias.shape, half_type),
         x_raw=(residual_in.shape, half_type),
         cot_raw=(residual_in.shape, half_type),
         x_own=(shard, half_type),
@@ -1804,6 +1852,8 @@
         vz=((planes, 16, LANES), single),
         vt=((16, LANES), single),
     )
+    for i in range(6):
+        scratch["vector%d" % i] = (norm1_gain.shape, half_type)
     for block in range(length // TILE):
         scratch["probs%d" % block] = ((seqs * LANES // HD, TILE, (block + 1) * TILE), single)
     names = tuple(inputs) + tuple(outputs) + tuple(scratch) + ("send", "recv", "near", "second", "third")

time: 95.4 us -> 94.3 us (0.988)
  Pallas kernels: 94.4 us -> 93.3 us
    pallas_call x1, Pallas kernels: 92.2 us -> 91.1 us  [fast_body(): pl.pallas_call(functools.partial(layer_kernel, names, planes), out_shape=...]
where the time goes in v7:
time: 94.3 us; the launch traced here: 94.1 us
  Pallas kernels  93.3 us (99%)
    pallas_call x1, Pallas kernels, fast_body(): pl.pallas_call(functools.partial(layer_kernel, names, planes), out_shape=...  91.1 us
    pallas_call x1, Pallas kernels, fast_body(): pl.pallas_call(functools.partial(finish_kernel, given + tuple(results) +...  2.11 us

profile of v7, /device:TPU:0, one launch (start us, length us, event | category | flops | bytes accessed | tf_op | source)
XLA Modules:
  0.0 94.1 jit_solution(10705321368052961460)
XLA Ops:
  0.7 91.1 %shard_map.254 = (bf16[64,2,1024]{2,1,0:T(2,128)(2,1)S(1)}, f32[64,2,1024]{2,1,0:T(2,128)S(1)}, bf16[8,32,384]{2,1,0:T(8,128)(2,1)S(1)}, bf16[8,32,512]{2,1,0:T(...) custom-call(bf16[64,2,1024]{2,1,0:T(2,128)(2,1)} %refs_0_.1, ...), custom_call_target="tpu_custom_call" | custom-call | tf_op jit(solution)/shard_map/pallas_call | solution.py:1860
  91.8 2.1 %shard_map.255 = (bf16[64,2,1024]{2,1,0:T(2,128)(2,1)}, f32[64,2,1024]{2,1,0:T(2,128)}, f32[32,3072]{1,0:T(8,128)}, f32[96]{0:T(128)}, f32[32,1024]{1,0:T(8,128)...) custom-call(bf16[64,2,1024]{2,1,0:T(2,128)(2,1)S(1)} %get-tuple-elem, ...), custom_call_target="tpu_custom_call" | custom-call | tf_op jit(solution)/shard_map/pallas_call | solution.py:1896

commit v8 on v7

--- a/solution.py
+++ b/solution.py
@@ -1423,85 +1423,85 @@
     turned = [s + b // pair * (planes - 1 - 2 * s) for s in (3, 2, 1, 0)]
 
     at.barrier()
-    own_v = [mail.bring(src, dst) for src, dst in zip(given, [do.b_qkv, do.b_up, *do.vectors])]
     line_da.start(do.wd_s)
     own_d = mail.bring(do.wd_s, do.wd.at[b])
     raw_x = mail.bring(do.x_in, do.x_raw)
-    at.reach(second, third)
     ex_u.start()
-    line_db.start(do.wd_s)
+    line_o.start(do.wo_s)
+    own_o = mail.bring(do.wo_s, do.wo.at[b])
     raw_x.wait()
     do.split(do.x_raw, do.x_own)
-    own_raw = mail.bring(do.wq_in, do.wq_raw)
-    line_o.start(do.wo_s)
-    own_o = mail.bring(do.wo_s, do.wo.at[b])
     gather_x.start()
+    line_db.start(do.wd_s)
     raw_c = mail.bring(do.cot_in, do.cot_raw)
-    own_table = mail.bring(do.table_in, do.table)
+    line_o.take(1)
     ex_u.finish()
     line_ua.start()
+    gather_x.relay_x()
+    own_v = [mail.bring(src, dst) for src, dst in zip(given, [do.b_qkv, do.b_up, *do.vectors])]
+    own_raw = mail.bring(do.wq_in, do.wq_raw)
+    gather_x.relay_y()
+    line_ub.start()
     for made in own_v:
         made.wait()
     do.own_vectors(at.t)
     ex_v.start()
-    line_o.take(1)
-    gather_x.relay_x()
-    gather_x.relay_y()
+    gather_x.share()
+    own_d.wait()
+    raw_c.wait()
+    do.split(do.cot_raw, do.cot_own)
+    line_ua.outer(1)
     own_raw.wait()
     do.sort_weight()
     ex_q.start()
-    line_ua.outer(1)
+    at.reach(second, third)
+    gather_x.far()
     line_ua.inner(1)
-    gather_x.share()
-    raw_c.wait()
-    do.split(do.cot_raw, do.cot_own)
+    line_o.take(2)
+    gather_c.start()
+    gather_x.finish()
     ex_v.finish()
     do.plane_vectors(b)
     line_v.start()
-    line_ub.start()
-    gather_x.far()
-    gather_c.start()
-    line_o.take(2)
-    own_table.wait()
     line_ua.inner(2)
-    gather_x.finish()
-    do.statistics()
-    line_v.finish()
-    do.activations()
     line_ub.outer(1)
     gather_c.relay_x()
-    line_o.take(3)
     gather_c.relay_y()
+    do.statistics()
     line_ub.inner(1)
     ex_q.finish()
     line_q.start()
+    line_o.take(3)
+    own_table = mail.bring(do.table_in, do.table)
+    line_v.finish()
+    do.activations()
+    line_ua.inner(3)
     own_o.wait()
-    swap_w.start()
-    mine[...] = do.wo[pl.ds(pair * c, pair)]
-    line_ua.inner(3)
     gather_c.share()
     do.expand(at.t, far_side)
     gather_c.far()
-    line_ub.inner(2)
-    own_d.wait()
-    swap_w.finish()
     gather_c.finish()
     do.down_weight_grad(turned[0])
     sum_d.edge(3)
+    line_ub.inner(2)
+    swap_w.start()
+    mine[...] = do.wo[pl.ds(pair * c, pair)]
     line_q.take(1)
+    own_table.wait()
     do.down_weight_grad(turned[1])
     sum_d.edge(2)
+    swap_w.finish()
+    do.attend_out_grad()
+    do.project_near(near_side)
     line_ub.inner(3)
     do.expand(at.t, near_side)
+    line_q.take(2)
+    line_da.take(1)
     do.down_weight_grad(turned[2])
     sum_d.edge(1)
+    line_db.take(1)
     do.down_weight_grad(turned[3])
     sum_d.edge(0)
-    do.project_near(near_side)
-    do.attend_out_grad()
-    line_q.take(2)
-    line_db.take(1)
-    line_da.take(1)
     do.hidden_grad(near_side)
     do.up_weight_grad(slots[0], near_side)
     sum_un.edge(3)
@@ -1509,108 +1509,108 @@
     sum_un.edge(0)
     do.up_weight_grad(slots[2], near_side)
     sum_un.edge(2)
+    line_q.take(3)
+    do.project(at.t, far_side)
+    sum_d.hop(1, 0)
     do.up_weight_grad(slots[3], near_side)
     sum_un.edge(1)
-    line_q.take(3)
-    do.project(at.t, far_side)
     do.attend(0)
+    line_da.take(2)
     do.attend(1)
+    do.attend_grad(0)
+    line_db.take(2)
     do.dense_weight_grad()
     swap_g.start()
     do.go4[pl.ds(pair * c, pair)] = do.go[:, c]
-    sum_d.hop(1, 0)
-    do.attend_grad(0)
     do.attend_grad(1)
+    line_da.take(3)
+    sum_d.hop(1, 1)
+    do.in_terms_one(tiles[0], True)
     do.qkv_weight_grad(slots[0])
     sum_q.edge(3)
-    line_da.take(2)
-    line_da.take(3)
-    line_db.take(2)
-    do.in_terms_one(tiles[0], True)
     do.in_terms_one(tiles[1], False)
+    sum_un.hop(1, 0)
+    swap_g.finish()
+    sum_o.edge(3)
     line_db.take(3)
+    do.qkv_weight_grad(slots[1])
+    sum_q.edge(0)
+    do.out_terms(tiles[0])
+    do.out_terms(tiles[1])
+    plane_o.start(6, 4)
     do.hidden_grad(far_side)
     do.up_weight_grad(slots[0], far_side)
     sum_uf.edge(3)
-    sum_d.hop(1, 1)
-    do.out_terms(tiles[0])
-    do.out_terms(tiles[1])
-    plane_o.start(6, 4)
+    plane_o.fold_far()
     do.in_terms_two(tiles[0], True)
+    sum_un.hop(1, 1)
     do.in_terms_two(tiles[1], False)
     plane_g.start(6, 4)
-    plane_o.fold_far()
+    plane_o.fold_x()
+    do.out_terms(tiles[2])
+    do.qkv_weight_grad(slots[2])
+    sum_q.edge(2)
+    plane_g.fold_far()
+    do.out_terms(tiles[3])
+    plane_o.start(2, 0)
     do.up_weight_grad(slots[1], far_side)
     sum_uf.edge(0)
     do.up_weight_grad(slots[2], far_side)
     sum_uf.edge(2)
+    plane_o.turn_x()
+    sum_d.hop(2, 0)
+    do.qkv_weight_grad(slots[3])
+    sum_q.edge(1)
     do.up_weight_grad(slots[3], far_side)
     sum_uf.edge(1)
-    do.out_terms(tiles[2])
-    do.out_terms(tiles[3])
-    plane_o.start(2, 0)
-    sum_un.hop(1, 0)
-    plane_g.fold_far()
-    do.qkv_weight_grad(slots[1])
-    sum_q.edge(0)
-    do.qkv_weight_grad(slots[2])
-    sum_q.edge(2)
-    swap_g.finish()
-    sum_o.edge(3)
-    do.qkv_weight_grad(slots[3])
-    sum_q.edge(1)
-    sum_un.hop(1, 1)
-    plane_o.fold_x()
-    plane_o.turn_x()
+    sum_q.hop(1, 0)
+    plane_g.fold_x()
     plane_o.fold_near()
     plane_o.turn_y()
     do.in_terms_one(tiles[2], False)
-    sum_q.hop(1, 0)
+    do.in_terms_one(tiles[3], False)
     do.in_terms_two(tiles[2], False)
-    do.in_terms_one(tiles[3], False)
+    sum_uf.hop(1, 0)
     do.in_terms_two(tiles[3], False)
     plane_g.start(2, 0)
-    plane_g.fold_x()
-    sum_uf.hop(1, 0)
     sum_un.hop(2, 0)
+    sum_o.hop(1, 0)
     do.small_terms(at.t)
     fold_v.start()
+    sum_q.hop(2, 0)
+    plane_g.turn_x()
+    sum_q.hop(1, 1)
+    plane_g.fold_near()
+    sum_uf.hop(2, 0)
+    plane_g.turn_y()
     sum_uf.hop(1, 1)
-    plane_g.turn_x()
-    plane_g.fold_near()
-    plane_g.turn_y()
-    sum_q.hop(2, 0)
-    sum_uf.hop(2, 0)
     fold_v.finish()
     do.small_plane(b)
     line_s.start()
-    sum_d.hop(2, 0)
+    sum_q.landed()
+    sum_q.total(do.fq)
+    back_q.start()
+    sum_o.hop(2, 0)
+    sum_d.landed()
+    sum_d.total(do.dd)
+    out_d = mail.bring(do.dd, do.dd_to)
     sum_o.edge(2)
-    sum_q.hop(1, 1)
     sum_un.landed()
     sum_uf.landed()
     sum_un.total(do.fu)
     back_u.start()
-    sum_o.edge(1)
-    sum_o.hop(1, 0)
     do.result(at.t, plane_o.finish(), plane_g.finish())
     out_x = mail.bring(do.out, do.out_to)
     out_g = mail.bring(do.in_grad, do.in_grad_to)
-    sum_q.landed()
-    sum_q.total(do.fq)
-    back_q.start()
-    sum_o.hop(2, 0)
+    sum_o.edge(1)
+    sum_o.hop(1, 1)
+    back_q.finish()
     line_s.finish()
-    sum_o.hop(1, 1)
     do.vt[...] = jnp.sum(do.vz[...], axis=0)
     share_v.start()
-    sum_d.landed()
-    sum_d.total(do.dd)
-    out_d = mail.bring(do.dd, do.dd_to)
     sum_o.landed()
     sum_o.total(do.dd_o)
     out_o = mail.bring(do.dd_o, do.dd_o_to)
-    back_q.finish()
     back_u.finish()
     share_v.finish()
     for copied in (out_o, out_d, out_x, out_g):

time: 94.3 us -> 92.8 us (0.984)
  Pallas kernels: 93.3 us -> 91.5 us
    pallas_call x1, Pallas kernels: 91.1 us -> 89.4 us  [fast_body(): pl.pallas_call(functools.partial(layer_kernel, names, planes), out_shape=...]
where the time goes in v8:
time: 92.8 us; the launch traced here: 92.4 us
  Pallas kernels  91.5 us (99%)
    pallas_call x1, Pallas kernels, fast_body(): pl.pallas_call(functools.partial(layer_kernel, names, planes), out_shape=...  89.4 us
    pallas_call x1, Pallas kernels, fast_body(): pl.pallas_call(functools.partial(finish_kernel, given + tuple(results) +...  2.11 us

profile of v8, /device:TPU:0, one launch (start us, length us, event | category | flops | bytes accessed | tf_op | source)
XLA Modules:
  0.0 92.4 jit_solution(15583711960917402002)
XLA Ops:
  0.7 89.4 %shard_map.254 = (bf16[64,2,1024]{2,1,0:T(2,128)(2,1)S(1)}, f32[64,2,1024]{2,1,0:T(2,128)S(1)}, bf16[8,32,384]{2,1,0:T(8,128)(2,1)S(1)}, bf16[8,32,512]{2,1,0:T(...) custom-call(bf16[64,2,1024]{2,1,0:T(2,128)(2,1)} %refs_0_.1, ...), custom_call_target="tpu_custom_call" | custom-call | tf_op jit(solution)/shard_map/pallas_call | solution.py:1860
  90.1 2.1 %shard_map.255 = (bf16[64,2,1024]{2,1,0:T(2,128)(2,1)}, f32[64,2,1024]{2,1,0:T(2,128)}, f32[32,3072]{1,0:T(8,128)}, f32[96]{0:T(128)}, f32[32,1024]{1,0:T(8,128)...) custom-call(bf16[64,2,1024]{2,1,0:T(2,128)(2,1)S(1)} %get-tuple-elem, ...), custom_call_target="tpu_custom_call" | custom-call | tf_op jit(solution)/shard_map/pallas_call | solution.py:1896
